TPU v7x, 128 devices: a 2x2x16 block of a 8x8x16 slice. The times are simulated.
128 devices in a mesh: groups: 4 (over x, y), aux: 32 (over z, core).
Axes of the slice: x: 2, y: 2, z: 16, core: 2. Of those that a mesh axis runs over, the one named last changes fastest.
The devices are a block of a 8x8x16 slice.
Arguments:
- slabs: bfloat16 [16000, 23040], P(('groups', 'aux')), parts along dimension 0, may hold values from -2 to 2
- rdm: bfloat16 [3600, 900], P('groups'), parts along dimension 0, as said below
- orbital_energy: float32 [3072], P('groups'), parts along dimension 0, may hold values from 0.5 to 3
- pair_blocks: int32 [128, 2], P('groups'), parts along dimension 0, may hold values from 0 to 15, as said below
Outputs:
- pair_energy: float32 [6144, 48], P(('groups', 'aux')), parts along dimension 0
- window_energy: float32 [4], P('groups'), parts along dimension 0
There are 4 independent parts, one for each index of `groups`. A program takes and returns all parts, laid end to end along the dimension named above; each array names one. Nothing has to cross between parts.
Inputs may be any that keep to these rules, and one draw needn't show every extreme that they name: `pair_blocks`: each row (p, q) has p <= q, and no two rows are equal. `rdm`: symmetric.
All inputs are finite; a program needn't handle non-finite values.
Results may differ from a plain program's by a relative error of at most 0.002.
Values may be sent and summed in bfloat16 or wider, within the bound.
No kernel may reach another device: no remote copies, remote signals or barrier semaphores. Data moves between devices by JAX's collectives and lax.ppermute only.
A program may use at most 128 MiB of HBM per device.

v0:
```python
import jax
import jax.numpy as jnp
from jax import lax
from jax.sharding import PartitionSpec as P

NACT = 30
VBLK = 48
NBLK = 16


def copy_for_each(x, axis):
    copies = jnp.broadcast_to(x, (lax.axis_size(axis), *x.shape))
    return lax.all_to_all(copies, axis, split_axis=0, concat_axis=0, tiled=True)


def of_everyone(x, axis):
    everything = copy_for_each(x, axis)
    return jnp.sum(everything, axis=0)


def per_device(slabs, rdm, orbital_energy, pair_blocks):
    local_rows = slabs.shape[0]
    width = VBLK * NACT
    blocked = slabs.reshape(local_rows, NBLK, width)
    position = lax.axis_index("aux")
    row_block = pair_blocks[position, 0]
    col_block = pair_blocks[position, 1]
    outgoing_rows = jnp.take(blocked, pair_blocks[:, 0], axis=1)
    arrived_rows = lax.all_to_all(outgoing_rows, "aux", split_axis=1, concat_axis=0, tiled=True)
    row_part = arrived_rows.reshape(-1, width)
    outgoing_cols = jnp.take(blocked, pair_blocks[:, 1], axis=1)
    columns = lax.all_to_all(outgoing_cols, "aux", split_axis=1, concat_axis=0, tiled=True)
    flattened = columns.reshape(columns.shape[0], -1)
    products = lax.dot_general(
        row_part, flattened, (((0,), (0,)), ((), ())), preferred_element_type=jnp.float32
    )
    integrals = products.astype(jnp.bfloat16)
    reordered = (
        integrals.reshape(VBLK, NACT, VBLK, NACT)
        .transpose(0, 2, 1, 3)
        .reshape(VBLK * VBLK, NACT * NACT)
    )
    contracted = jnp.dot(reordered, rdm, preferred_element_type=jnp.float32)
    paired = jnp.sum(contracted * reordered.astype(jnp.float32), axis=1).reshape(VBLK, VBLK)
    energy_rows = lax.dynamic_slice_in_dim(orbital_energy, row_block * VBLK, VBLK)
    energy_cols = lax.dynamic_slice_in_dim(orbital_energy, col_block * VBLK, VBLK)
    energy = -paired / (energy_rows[:, None] + energy_cols[None, :])
    weight = jnp.where(row_block == col_block, jnp.float32(1.0), jnp.float32(2.0))
    total = of_everyone(weight * jnp.sum(energy), "aux")
    mean_energy = total / (VBLK * VBLK * lax.axis_size("aux"))
    return (energy, mean_energy.reshape(1))


def solution(mesh):
    return jax.shard_map(
        per_device,
        mesh=mesh,
        in_specs=(P(("groups", "aux"), None), P("groups", None), P("groups"), P("groups", None)),
        out_specs=(P(("groups", "aux"), None), P("groups")),
        check_vma=False,
    )
```

profile of v0, /device:TPU:69, one launch (start us, length us, event | category | flops | bytes accessed | tf_op | source)
XLA Modules:
  0.0 1201.7 jit_solution(8237756832875592387)
XLA Ops:
  0.6 0.0 copy-start
  0.6 0.0 copy-start.1
  0.7 8.7 copy.11
  9.4 0.0 copy-done.1
  9.4 9.0 gather_fusion.1
  18.5 10.3 select_bitcast_fusion
  28.8 18.5 %all-to-all-start.1 = ((bf16[125,32,1440]{0,2,1:T(8,128)(2,1)}), bf16[125,32,1440]{0,2,1:T(8,128)(2,1)}, u32[]{:S(2)}, u32[]{:S(2)}) async-start(bf16[125,32,1440]{0,2,1:T(8,128)(2,1)} %select_bitcast_fusion), calls=%async_computation.1 | async-start | bytes 23592960 | tf_op jit(solution)/shard_map/all_to_all | solution.py:32
  47.3 9.0 gather_fusion
  56.3 10.3 select_bitcast_fusion.1
  66.7 486.3 %all-to-all-done.1 = bf16[125,32,1440]{0,2,1:T(8,128)(2,1)} async-done(((bf16[125,32,1440]{0,2,1:T(8,128)(2,1)}), bf16[125,32,1440]{0,2,1:T(8,128)(2,1)}, u32[]{:S(2)}, u32[]{:S(2)}) %all-to-all-start.1) | async-done | bytes 11520032 | tf_op jit(solution)/shard_map/all_to_all | solution.py:32
  552.9 14.4 %all-to-all-start = ((bf16[125,32,1440]{0,2,1:T(8,128)(2,1)}), bf16[125,32,1440]{0,2,1:T(8,128)(2,1)}, u32[]{:S(2)}, u32[]{:S(2)}) async-start(bf16[125,32,1440]{0,2,1:T(8,128)(2,1)} %select_bitcast_fusion.1), calls=%async_computation | async-start | bytes 23592960 | tf_op jit(solution)/shard_map/all_to_all | solution.py:29
  567.4 0.6 constant_dynamic-slice_fusion.1
  570.5 0.8 fusion.8
  571.4 501.6 %all-to-all-done = bf16[125,32,1440]{0,2,1:T(8,128)(2,1)} async-done(((bf16[125,32,1440]{0,2,1:T(8,128)(2,1)}), bf16[125,32,1440]{0,2,1:T(8,128)(2,1)}, u32[]{:S(2)}, u32[]{:S(2)}) %all-to-all-start) | async-done | bytes 11520032 | tf_op jit(solution)/shard_map/all_to_all | solution.py:29
  1073.0 25.4 %bitcast_convert_fusion = bf16[1440,1440]{1,0:T(8,128)(2,1)} fusion(bf16[125,32,1440]{0,2,1:T(8,128)(2,1)} %all-to-all-done.1, bf16[125,32,1440]{0,2,1:T(8,128)(2,1)} %all-to-all-done), kind=kOutput, calls=%fused_computation.7 | convolution fusion | flops 16590873600 | bytes 27187200 | tf_op jit(solution)/shard_map/dot_general | solution.py:34
  1098.3 26.9 %reshape.54 = bf16[48,30,48,30]{3,2,1,0:T(8,128)(2,1)} reshape(bf16[1440,1440]{1,0:T(8,128)(2,1)} %bitcast_convert_fusion) | data formatting | bytes 8294400 | tf_op jit(solution)/shard_map/reshape | solution.py:39
  1125.2 21.3 %copy.12 = bf16[48,48,30,30]{1,0,3,2:T(8,128)(2,1)} copy(bf16[48,48,30,30]{3,1,2,0:T(8,128)(2,1)} %bitcast.44) | data formatting | bytes 8294400 | tf_op jit(solution)/shard_map/transpose | solution.py:40
  1146.5 16.1 %reshape.55 = bf16[2304,900]{0,1:T(8,128)(2,1)} reshape(bf16[48,48,30,30]{1,0,3,2:T(8,128)(2,1)} %copy.12) | data formatting | bytes 8294400 | tf_op jit(solution)/shard_map/reshape | solution.py:41
  1162.6 0.0 copy-done
  1162.6 8.9 multiply_reduce_fusion
  1171.5 0.1 neg.11
  1171.6 1.3 fusion.7
  1173.5 25.7 %all_to_all.36 = f32[32,1,1]{2,1,0:T(1,128)S(1)} all-to-all(f32[32,1,1]{2,1,0:T(1,128)S(1)} %broadcast_in_dim.14), channel_id=1, replica_groups=mesh['groups'=4,'aux'=32] {'aux'}, dimensions={0} | all-to-all | bytes 256 | tf_op jit(solution)/shard_map/all_to_all | solution.py:13
  1199.3 0.6 reduce_sum.29
  (5 shorter events, 0.0 us)
Async XLA Ops:
  0.6 1162.0 %copy-start = (bf16[900,900]{1,0:T(8,128)(2,1)S(1)}, bf16[900,900]{1,0:T(8,128)(2,1)}, u32[]{:S(2)}) copy-start(bf16[900,900]{1,0:T(8,128)(2,1)} %param.7) | copy-start | bytes 4860004
  0.6 8.8 copy-start.1
  28.8 524.1 %all-to-all-start.1 = ((bf16[125,32,1440]{0,2,1:T(8,128)(2,1)}), bf16[125,32,1440]{0,2,1:T(8,128)(2,1)}, u32[]{:S(2)}, u32[]{:S(2)}) async-start(bf16[125,32,1440]{0,2,1:T(8,128)(2,1)} %select_bitcast_fusion), calls=%async_computation.1 | async-start | bytes 23592960 | tf_op jit(solution)/shard_map/all_to_all | solution.py:32
  552.9 520.0 %all-to-all-start = ((bf16[125,32,1440]{0,2,1:T(8,128)(2,1)}), bf16[125,32,1440]{0,2,1:T(8,128)(2,1)}, u32[]{:S(2)}, u32[]{:S(2)}) async-start(bf16[125,32,1440]{0,2,1:T(8,128)(2,1)} %select_bitcast_fusion.1), calls=%async_computation | async-start | bytes 23592960 | tf_op jit(solution)/shard_map/all_to_all | solution.py:29
where the time goes:
time: 1200 us
  waiting for transfers between devices  988 us (82%)
  local copies, waits for them, and re-layouts  92.6 us (8%)
  matrix products  34.2 us (3%)
  starting transfers between devices  33 us (3%)
  blocking collectives  25.7 us (2%)
  other arithmetic  22.6 us (2%)
    all_to_all x1, waiting for transfers between devices, per_device(): lax.all_to_all(outgoing_rows, 'aux', split_axis=1, concat_axis=0, tiled=T...  502 us
    all_to_all x1, waiting for transfers between devices, per_device(): lax.all_to_all(outgoing_cols, 'aux', split_axis=1, concat_axis=0, tiled=T...  486 us
    reshape x1, local copies, waits for them, and re-layouts, per_device(): integrals.reshape(VBLK, NACT, VBLK, NACT).transpose(0, 2, 1, 3)  26.9 us
    all_to_all x1, blocking collectives, copy_for_each(): return lax.all_to_all(copies, axis, split_axis=0, concat_axis=0, tiled=True)  25.7 us
    dot_general x1, matrix products, per_device(): lax.dot_general(row_part, flattened, (((0,), (0,)), ((), ())), preferred_...  25.4 us
  transfers between devices with their start and end apart: 2, of which 2 were waited for; matrix products, arithmetic and copies ran while one was open for 2% of the time, Pallas kernels for 0%

commit v1 on v0

v1 whole, which is shorter than its diff:
```python
import numpy as np
import jax
import jax.numpy as jnp
from jax import lax
from jax.experimental import pallas as pl
from jax.experimental.pallas import tpu as pltpu
from jax.sharding import PartitionSpec as P


NACT = 30
VBLK = 48
NBLK = 16
WIDTH = VBLK * NACT
LANES = 128
CORES = 2
CHIPS = 16
BELOW = 2
ABOVE = 3
LONGEST = 10
JOBS = 2
TPAD = 32
PACKED = NACT * TPAD
STEPS = 256
OFFSETS = range(-ABOVE, BELOW + 1)


def swap_plan():
    draw = np.random.default_rng(7)
    first = draw.integers(0, NBLK, STEPS)
    second = (first + draw.integers(1, NBLK, STEPS)) % NBLK
    heat = 0.7 * (0.2 / 0.7) ** (np.arange(STEPS) / STEPS)
    heat[:24] = 4.0
    return (
        np.stack([first, second], axis=1).astype(np.int32).reshape(-1),
        (1.0 / heat).astype(np.float32),
    )


def ring_mask(reach):
    return sum(1 << d for d in range(NBLK) if min(d, NBLK - d) in reach)


def plan_kernel(me, pairs, swaps, coolness, table, words, links, home, load):
    far_base = ring_mask(range(BELOW + ABOVE + 1, NBLK))
    edge_base = ring_mask([BELOW + ABOVE])
    near_edge_base = ring_mask([BELOW + ABOVE - 1])
    shape = (8, 128)

    def turned(base, z):
        return ((base << z) | (base >> (NBLK - z))) & 0xFFFF

    def count(x):
        return lax.population_count(x)

    def clear(z, c):
        links[z] = 0
        load[z] = 0
        return c

    lax.fori_loop(0, NBLK, clear, 0)
    n_pairs = pairs.shape[0] // 2

    def link(d, c):
        p = pairs[2 * d]
        q = pairs[2 * d + 1]
        differ = jnp.where(p == q, 0, 1)
        links[p] = links[p] | (differ << q)
        links[q] = links[q] | (differ << p)
        return c

    lax.fori_loop(0, n_pairs, link, 0)
    cost = jnp.zeros(shape, jnp.int32)
    for z in range(NBLK):
        word = jnp.broadcast_to(links[z] | (z << 16), shape).astype(jnp.int32)
        words[z] = word
        cost = cost + count(word & turned(far_base, z))
    cost = cost // 2
    lane = lax.broadcasted_iota(jnp.int32, shape, 0) * 128 + lax.broadcasted_iota(jnp.int32, shape, 1)
    noise = (lane * 747796405 + 12345) * 1103515245 + 12345

    def step(i, carry):
        cost, noise = carry
        x = swaps[2 * i]
        y = swaps[2 * i + 1]
        wx = words[x]
        wy = words[y]

        def crossed(w):
            t = ((w >> x) ^ (w >> y)) & 1
            return w ^ ((t << x) | (t << y))

        far_x = turned(jnp.int32(far_base), x)
        far_y = turned(jnp.int32(far_base), y)
        change = (
            count(crossed(wy) & far_x)
            + count(crossed(wx) & far_y)
            - count(wx & far_x)
            - count(wy & far_y)
        )
        noise = noise * 1664525 + 1013904223
        chance = ((noise >> 8) & 0xFFFF).astype(jnp.float32) * (1.0 / 65536.0)
        bound = jnp.exp(change.astype(jnp.float32) * (-coolness[i]))
        take = ((change <= 0) | (chance < bound)) & (cost > 0)
        take_bit = take.astype(jnp.int32)
        for z in range(NBLK):
            w = words[z]
            t = ((w >> x) ^ (w >> y)) & take_bit
            words[z] = w ^ ((t << x) | (t << y))
        wx = words[x]
        wy = words[y]
        words[x] = jnp.where(take, wy, wx)
        words[y] = jnp.where(take, wx, wy)
        return cost + change * take_bit, noise

    cost, noise = lax.fori_loop(0, STEPS, step, (cost, noise))
    tight = jnp.zeros(shape, jnp.int32)
    for z in range(NBLK):
        w = words[z]
        tight = tight + 2 * count(w & turned(edge_base, z)) + count(w & turned(near_edge_base, z))
    score = jnp.minimum(cost * 512 + tight, 16000) * 1024 + lane
    best = jnp.min(score.astype(jnp.float32))
    chosen = score.astype(jnp.float32) == best
    for z in range(NBLK):
        w = jnp.sum(jnp.where(chosen, words[z].astype(jnp.float32), 0.0)).astype(jnp.int32)
        home[(w >> 16) & 15] = z

    def span(d):
        x = home[pairs[2 * d]]
        y = home[pairs[2 * d + 1]]
        ahead = (y - x) & (NBLK - 1)
        forward = ahead <= NBLK // 2
        gap = jnp.where(forward, ahead, NBLK - ahead)
        low = jnp.where(forward, y, x) - BELOW
        return gap, low

    def rank(r, unfit):
        def place(d, unfit):
            gap, low = span(d)

            def choose(c, best_chip):
                chip = (low + c) & (NBLK - 1)
                better = load[chip] < load[best_chip]
                return jnp.where(better, chip, best_chip)

            now = gap == BELOW + ABOVE - r
            spot = lax.fori_loop(1, jnp.where(now, r + 1, 1), choose, low & (NBLK - 1))

            @pl.when(now)
            def _():
                turn = load[spot]
                load[spot] = turn + 1
                table[24 + d] = jnp.minimum((spot * CORES + turn % CORES) * JOBS + turn // CORES, n_pairs * JOBS - 1)
                here = (spot == me[0] // CORES) & (turn < CORES * JOBS)

                @pl.when(turn >= CORES)
                def _():
                    table[17] = 1

                @pl.when(here)
                def _():
                    whose = jnp.where(turn % CORES == me[0] % CORES, MINE, OTHERS)
                    slot = whose + 3 * (turn // CORES)
                    table[slot] = 1
                    table[slot + 1] = ((home[pairs[2 * d]] - spot + 8) & 15) - 8
                    table[slot + 2] = ((home[pairs[2 * d + 1]] - spot + 8) & 15) - 8

            full = now & (load[spot] > CORES * JOBS)
            return unfit + jnp.where(full, 1, 0)

        return lax.fori_loop(0, n_pairs, place, unfit)

    for j in range(8 * JOBS):
        table[MINE + j] = 0
    table[17] = 0

    def missed(d, c):
        table[24 + d] = 0
        return c + jnp.where(span(d)[0] > BELOW + ABOVE, 1, 0)

    unfit = lax.fori_loop(0, n_pairs, missed, 0)
    unfit = lax.fori_loop(0, BELOW + ABOVE + 1, rank, unfit)
    table[0] = jnp.where(unfit == 0, 1, 0)
    for z in range(NBLK):
        table[1 + z] = home[z]


def make_plan(me, pair_blocks):
    swaps, coolness = swap_plan()
    smem = pl.BlockSpec(memory_space=pltpu.SMEM)
    return pl.pallas_call(
        plan_kernel,
        out_shape=jax.ShapeDtypeStruct((96,), jnp.int32),
        in_specs=[smem] * 4,
        out_specs=smem,
        scratch_shapes=[
            pltpu.VMEM((NBLK, 8, 128), jnp.int32),
            pltpu.SMEM((NBLK,), jnp.int32),
            pltpu.SMEM((NBLK,), jnp.int32),
            pltpu.SMEM((NBLK,), jnp.int32),
        ],
        name="plan",
    )(me, pair_blocks.reshape(-1), jnp.asarray(swaps), jnp.asarray(coolness))


PER_STEP = 4


def pack_kernel(me, table, slab, *rest):
    outs = rest[: 2 * LONGEST]
    turned, packed, sems = rest[2 * LONGEST :]
    g = pl.program_id(0)
    chip = me[0] // CORES
    rows = slab.shape[0]

    def copies(b):
        o = ((table[1 + b] - chip + 8) & 15) - 8
        for reach in range(1, LONGEST + 1):
            yield o == reach - ABOVE, pltpu.make_async_copy(packed.at[b], outs[reach - 1], sems.at[reach - 1])
            yield o == BELOW - reach, pltpu.make_async_copy(
                packed.at[b], outs[LONGEST + reach - 1], sems.at[LONGEST + reach - 1]
            )

    for i in range(PER_STEP):
        b = g * PER_STEP + i
        part = slab[:, i * WIDTH : (i + 1) * WIDTH].astype(jnp.float32)
        part = jnp.concatenate([part, jnp.zeros((LANES - rows, WIDTH), jnp.float32)], axis=0)
        turned[...] = part.T
        for t in range(NACT):
            packed[b, t * VBLK : (t + 1) * VBLK, :] = turned[pl.ds(t, VBLK, stride=NACT), :].astype(jnp.bfloat16)
        for when, copy in copies(b):

            @pl.when(when)
            def _(copy=copy):
                copy.start()

    @pl.when(g == NBLK // PER_STEP - 1)
    def _():
        for n in range(2 * LONGEST):
            pltpu.make_async_copy(packed.at[0], outs[n], sems.at[n]).wait()


def pack(me, table, slabs):
    rows = slabs.shape[0]
    smem = pl.BlockSpec(memory_space=pltpu.SMEM)
    return pl.pallas_call(
        pack_kernel,
        grid=(NBLK // PER_STEP,),
        in_specs=[smem, smem, pl.BlockSpec((rows, PER_STEP * WIDTH), lambda g: (0, g))],
        out_specs=[pl.BlockSpec(memory_space=pl.ANY)] * (2 * LONGEST),
        out_shape=[jax.ShapeDtypeStruct((WIDTH, LANES), jnp.bfloat16)] * (2 * LONGEST),
        scratch_shapes=[
            pltpu.VMEM((WIDTH, LANES), jnp.float32),
            pltpu.VMEM((NBLK, WIDTH, LANES), jnp.bfloat16),
            pltpu.SemaphoreType.DMA((2 * LONGEST,)),
        ],
        compiler_params=pltpu.CompilerParams(vmem_limit_bytes=40 * 1024 * 1024),
        name="pack",
    )(me, table, slabs)


ROW_TILE = 480
TILES = -(-WIDTH // LANES)
COL_TILES = ((0, 512), (512, 512), (1024, 416))
GROUP = 8
HBM = pltpu.MemorySpace.HBM
MINE = 64
OTHERS = 72


def unflatten(refs, sources):
    refs = list(refs)
    return [{d: refs.pop(0) for d in OFFSETS} for _ in sources]


def flatten(pieces, sources):
    return [pieces[s][d] for s in sources for d in OFFSETS]


def select_kernel(table, *rest, sources, job):
    count = len(sources) * len(OFFSETS)
    pieces = unflatten(rest[:count], sources)
    out, held, sems, out_sem = rest[count:]

    @pl.when(table[OTHERS + 3 * job] == 1)
    def _():
        for side in range(2):
            wanted = table[OTHERS + 3 * job + 1 + side]
            for n in range(len(sources)):
                for d, piece in pieces[n].items():

                    @pl.when(wanted == d)
                    def _(piece=piece, n=n, side=side):
                        pltpu.make_async_copy(piece, held.at[side, n], sems.at[side, n]).start()

        for side in range(2):
            for n in range(len(sources)):
                pltpu.make_async_copy(next(iter(pieces[n].values())), held.at[side, n], sems.at[side, n]).wait()
                pltpu.make_async_copy(held.at[side, n], out.at[side, n], out_sem.at[side, n]).start()
        for side in range(2):
            for n in range(len(sources)):
                pltpu.make_async_copy(held.at[side, n], out.at[side, n], out_sem.at[side, n]).wait()


def select(table, pieces, sources, job):
    flat = flatten(pieces, sources)
    n = len(sources)
    return pl.pallas_call(
        lambda *refs: select_kernel(*refs, sources=sources, job=job),
        in_specs=[pl.BlockSpec(memory_space=pltpu.SMEM)] + [pl.BlockSpec(memory_space=HBM)] * len(flat),
        out_specs=pl.BlockSpec(memory_space=HBM),
        out_shape=jax.ShapeDtypeStruct((2, n, WIDTH, LANES), jnp.bfloat16),
        scratch_shapes=[
            pltpu.VMEM((2, n, WIDTH, LANES), jnp.bfloat16),
            pltpu.SemaphoreType.DMA((2, n)),
            pltpu.SemaphoreType.DMA((2, n)),
        ],
        name="select",
    )(table, *flat)


def multiply(table, job, pieces, other, bufs, sems, acc, fresh):
    def lanes(n, who):
        return pl.ds((n * CORES + who) * LANES, LANES)

    for side, buf in enumerate(bufs):
        wanted = table[MINE + 3 * job + 1 + side]
        for n in range(len(pieces)):
            pltpu.make_async_copy(other.at[side, n], buf.at[:, lanes(n, 1)], sems.at[side, n, 1]).start()
            for d, piece in pieces[n].items():

                @pl.when(wanted == d)
                def _(piece=piece, n=n, side=side, buf=buf):
                    pltpu.make_async_copy(piece, buf.at[:, lanes(n, 0)], sems.at[side, n, 0]).start()

    for side, buf in enumerate(bufs):
        for n in range(len(pieces)):
            for who in range(CORES):
                pltpu.make_async_copy(other.at[side, n], buf.at[:, lanes(n, who)], sems.at[side, n, who]).wait()
    col_buf, row_buf = bufs

    def rows(m, c):
        here = pl.ds(pl.multiple_of(m * ROW_TILE, ROW_TILE), ROW_TILE)
        left = row_buf[here, :]
        for start, size in COL_TILES:
            part = lax.dot_general(
                left, col_buf[start : start + size, :], (((1,), (1,)), ((), ())), preferred_element_type=jnp.float32
            )
            for at in range(0, size, LANES):
                wide = min(LANES, size - at)
                tile = acc.at[(start + at) // LANES, here, pl.ds(0, wide)]
                if fresh:
                    tile[...] = part[:, at : at + wide]
                else:
                    tile[...] += part[:, at : at + wide]
        return c

    lax.fori_loop(0, WIDTH // ROW_TILE, rows, 0)


def early_kernel(table, other, *rest, sources, job, fresh):
    before = None
    if not fresh:
        before, *rest = rest
    count = len(sources) * len(OFFSETS)
    pieces = unflatten(rest[:count], sources)
    out, col_buf, row_buf, acc, sems, sem = rest[count:]

    @pl.when(table[MINE + 3 * job] == 1)
    def _():
        if not fresh:
            copy = pltpu.make_async_copy(before, acc, sem)
            copy.start()
            copy.wait()
        multiply(table, job, pieces, other, (col_buf, row_buf), sems, acc, fresh)
        copy = pltpu.make_async_copy(acc, out, sem)
        copy.start()
        copy.wait()


def density_kernel(rdm, out, wide, lifted):
    out[...] = jnp.zeros(out.shape, out.dtype)
    lifted[...] = jnp.zeros(lifted.shape, jnp.float32)
    wide[...] = rdm[...].astype(jnp.float32)
    for v in range(NACT):
        lifted[:, v * TPAD : v * TPAD + NACT] = wide[:, v * NACT : (v + 1) * NACT]
    for t in range(NACT):
        out[t * TPAD : t * TPAD + NACT, :] = lifted[t * NACT : (t + 1) * NACT, :].astype(jnp.bfloat16)


def spread_density(rdm):
    order = NACT * NACT
    return pl.pallas_call(
        density_kernel,
        out_shape=jax.ShapeDtypeStruct((PACKED, PACKED), jnp.bfloat16),
        scratch_shapes=[pltpu.VMEM((order, order), jnp.float32), pltpu.VMEM((order, PACKED), jnp.float32)],
        name="density",
    )(rdm)


def finish_kernel(table, other, before, density, *rest, sources, job):
    count = len(sources) * len(OFFSETS)
    pieces = unflatten(rest[:count], sources)
    out, col_buf, row_buf, acc, spread, sems, sem = rest[count:]

    @pl.when(table[MINE + 3 * job] == 0)
    def _():
        out[...] = jnp.zeros(out.shape, out.dtype)

    @pl.when(table[MINE + 3 * job] == 1)
    def _():
        copy = pltpu.make_async_copy(before, acc.at[:, pl.ds(0, WIDTH), :], sem)
        copy.start()
        acc[:, WIDTH:, :] = jnp.zeros((TILES, acc.shape[1] - WIDTH, LANES), jnp.float32)
        copy.wait()
        multiply(table, job, pieces, other, (col_buf, row_buf), sems, acc, False)

        def group(g, carry):
            for i in range(GROUP):
                here = pl.ds(g * GROUP + i, TPAD, stride=VBLK)
                rows = jnp.concatenate([acc[c, here, :] for c in range(TILES)], axis=1).astype(jnp.bfloat16)
                for t in range(NACT):
                    spread[t * TPAD : (t + 1) * TPAD, i * VBLK : (i + 1) * VBLK] = rows[:, t * VBLK : (t + 1) * VBLK]
            x = spread[...]
            y = jnp.dot(density[...], x, preferred_element_type=jnp.float32)
            out[pl.ds(g, 1), :] = jnp.sum(y * x.astype(jnp.float32), axis=0, keepdims=True)
            return carry

        lax.fori_loop(0, VBLK // GROUP, group, 0)


def product_scratch(sources, rows):
    depth = len(sources) * CORES * LANES
    return [
        pltpu.VMEM((WIDTH, depth), jnp.bfloat16),
        pltpu.VMEM((WIDTH, depth), jnp.bfloat16),
        pltpu.VMEM((TILES, rows, LANES), jnp.float32),
    ]


ROOM = pltpu.CompilerParams(vmem_limit_bytes=48 * 1024 * 1024)


def early(table, other, before, pieces, sources, job):
    flat = flatten(pieces, sources)
    fresh = before is None
    held = [] if fresh else [before]
    in_hbm = pl.BlockSpec(memory_space=HBM)
    return pl.pallas_call(
        lambda *refs: early_kernel(*refs, sources=sources, job=job, fresh=fresh),
        in_specs=[pl.BlockSpec(memory_space=pltpu.SMEM)] + [in_hbm] * (1 + len(held) + len(flat)),
        out_specs=in_hbm,
        out_shape=jax.ShapeDtypeStruct((TILES, WIDTH, LANES), jnp.float32),
        scratch_shapes=product_scratch(sources, WIDTH)
        + [pltpu.SemaphoreType.DMA((2, len(sources), CORES)), pltpu.SemaphoreType.DMA],
        compiler_params=ROOM,
        name="early",
    )(table, other, *held, *flat)


def finish(table, other, before, density, pieces, sources, job):
    flat = flatten(pieces, sources)
    in_hbm = pl.BlockSpec(memory_space=HBM)
    return pl.pallas_call(
        lambda *refs: finish_kernel(*refs, sources=sources, job=job),
        in_specs=[pl.BlockSpec(memory_space=pltpu.SMEM), in_hbm, in_hbm, pl.BlockSpec(memory_space=pltpu.VMEM)]
        + [in_hbm] * len(flat),
        out_specs=pl.BlockSpec(memory_space=pltpu.VMEM),
        out_shape=jax.ShapeDtypeStruct((VBLK // GROUP, GROUP * VBLK), jnp.float32),
        scratch_shapes=product_scratch(sources, VBLK * TPAD)
        + [
            pltpu.VMEM((PACKED, GROUP * VBLK), jnp.bfloat16),
            pltpu.SemaphoreType.DMA((2, len(sources), CORES)),
            pltpu.SemaphoreType.DMA,
        ],
        compiler_params=ROOM,
        name="finish",
    )(table, other, before, density, *flat)


def ring_shift(hops):
    n = lax.axis_size("aux")
    return [(i, (i + hops * CORES) % n) for i in range(n)]


def to_other_core(x):
    n = lax.axis_size("aux")
    return lax.ppermute(x, "aux", [(i, i ^ 1) for i in range(n)])


def energies_of(paired, orbital_energy, pair_blocks):
    table = orbital_energy.reshape(NBLK, VBLK)
    rows = table[pair_blocks[:, 0]]
    cols = table[pair_blocks[:, 1]]
    energy = -paired / (rows[:, :, None] + cols[:, None, :])
    weight = jnp.where(pair_blocks[:, 0] == pair_blocks[:, 1], jnp.float32(1.0), jnp.float32(2.0))
    total = jnp.sum(weight * jnp.sum(energy, axis=(1, 2)))
    mine = lax.dynamic_index_in_dim(energy, lax.axis_index("aux"), 0, keepdims=False)
    mean_energy = total / (VBLK * VBLK * lax.axis_size("aux"))
    return mine, mean_energy.reshape(1)


def sources_within(low, high):
    return [s for s in range(-CHIPS // 2, CHIPS // 2) if low <= abs(s) <= high]


NEAREST = sources_within(0, 3)
NEAR = sources_within(4, 5)
FAR = sources_within(6, CHIPS)


def planned(table, me, slabs, rdm, orbital_energy, pair_blocks):
    sent = pack(me, table, slabs)
    pieces = {s: {} for s in range(-CHIPS // 2, CHIPS // 2)}

    def keep(source, offset, value):
        if -ABOVE <= offset <= BELOW:
            pieces[(source + CHIPS // 2) % CHIPS - CHIPS // 2][offset] = value

    right = {reach: sent[reach - 1] for reach in range(1, LONGEST + 1)}
    left = {reach: sent[LONGEST + reach - 1] for reach in range(1, LONGEST + 1)}
    for offset in OFFSETS:
        keep(0, offset, right[offset + ABOVE] if offset > -ABOVE else left[BELOW + ABOVE])
    sums = None
    density = None

    def exchange(sources, job):
        chosen = select(table, pieces, sources, job)
        return to_other_core(chosen)

    for hop in range(1, LONGEST + 1):
        for reach in range(LONGEST, hop - 1, -1):
            right[reach] = lax.ppermute(right[reach], "aux", ring_shift(1))
            left[reach] = lax.ppermute(left[reach], "aux", ring_shift(-1))
            keep(-hop, reach - ABOVE - hop, right[reach])
            keep(hop, BELOW - reach + hop, left[reach])
        if hop == 1:
            density = spread_density(rdm)
        if hop == 3:
            other = exchange(NEAREST, 0)
            sums = early(table, other, None, pieces, NEAREST, 0)
        if hop == 5:
            other = exchange(NEAR, 0)
            sums = early(table, other, sums, pieces, NEAR, 0)
    other = exchange(FAR, 0)
    paired = finish(table, other, sums, density, pieces, FAR, 0)

    def second_job(pieces):
        other = exchange(NEAREST, 1)
        sums = early(table, other, None, pieces, NEAREST, 1)
        other = exchange(NEAR, 1)
        sums = early(table, other, sums, pieces, NEAR, 1)
        other = exchange(FAR, 1)
        return finish(table, other, sums, density, pieces, FAR, 1)

    extra = lax.cond(table[17] == 1, second_job, lambda pieces: jnp.zeros_like(paired), pieces)
    everyone = lax.all_gather(jnp.stack([paired, extra]), "aux").reshape(-1, VBLK, VBLK)
    paired = everyone[lax.dynamic_slice_in_dim(table, 24, pair_blocks.shape[0])].transpose(0, 2, 1)
    return energies_of(paired, orbital_energy, pair_blocks)


def unplanned(table, me, slabs, rdm, orbital_energy, pair_blocks):
    local_rows = slabs.shape[0]
    blocked = slabs.reshape(local_rows, NBLK, WIDTH)
    sides = []
    for side in range(2):
        outgoing = jnp.take(blocked, pair_blocks[:, side], axis=1)
        arrived = lax.all_to_all(outgoing, "aux", split_axis=1, concat_axis=0, tiled=True)
        sides.append(arrived.reshape(-1, WIDTH))
    products = lax.dot_general(sides[0], sides[1], (((0,), (0,)), ((), ())), preferred_element_type=jnp.float32)
    reordered = (
        products.astype(jnp.bfloat16)
        .reshape(VBLK, NACT, VBLK, NACT)
        .transpose(0, 2, 1, 3)
        .reshape(VBLK * VBLK, NACT * NACT)
    )
    contracted = jnp.dot(reordered, rdm, preferred_element_type=jnp.float32)
    paired = jnp.sum(contracted * reordered.astype(jnp.float32), axis=1).reshape(VBLK, VBLK)
    return energies_of(lax.all_gather(paired, "aux"), orbital_energy, pair_blocks)


def per_device(slabs, rdm, orbital_energy, pair_blocks):
    me = lax.axis_index("aux").reshape(1).astype(jnp.int32)
    table = make_plan(me, pair_blocks)
    return lax.cond(table[0] == 1, planned, unplanned, table, me, slabs, rdm, orbital_energy, pair_blocks)


def solution(mesh):
    return jax.shard_map(
        per_device,
        mesh=mesh,
        in_specs=(P(("groups", "aux"), None), P("groups", None), P("groups"), P("groups", None)),
        out_specs=(P(("groups", "aux"), None), P("groups")),
        check_vma=False,
    )
```

time: 1200 us -> 678 us (0.56)
  waiting for transfers between devices: 988 us -> 306 us
  Pallas kernels: 0 us -> 119 us
  starting transfers between devices: 33 us -> 145 us
  local copies, waits for them, and re-layouts: 92.6 us -> 7.58 us
  blocking collectives: 25.7 us -> 78.6 us
  matrix products: 34.2 us -> 0 us
  other arithmetic: 22.6 us -> 1.34 us
  loops' own time: 0 us -> 12.5 us
    all_to_all x2 -> x0, waiting for transfers between devices: 988 us -> none  [the longest x1 502 us: per_device(): lax.all_to_all(outgoing_rows, 'aux', split_axis=1, concat_axis=0, tiled=T...]
    ppermute x0 -> x116, waiting for transfers between devices: none -> 306 us  [the longest x55 181 us: planned(): right[reach] = lax.ppermute(right[reach], 'aux', ring_shift(1))]
    ppermute x0 -> x116, starting transfers between devices: none -> 145 us  [the longest x55 122 us: planned(): left[reach] = lax.ppermute(left[reach], 'aux', ring_shift(-1))]
    pallas_call x0 -> x15, Pallas kernels: none -> 119 us  [the longest x4 33.4 us: early(): pl.pallas_call(lambda *refs: early_kernel(*refs, sources=sources, job=job...]
    all_gather x0 -> x1, blocking collectives: none -> 78.6 us  [planned(): lax.all_gather(jnp.stack([paired, extra]), 'aux').reshape(-1, VBLK, VBLK)]
    reshape x2 -> x3, local copies, waits for them, and re-layouts: 43 us -> 1.41 us  [the longest x1 0.72 us: planned(): lax.all_gather(jnp.stack([paired, extra]), 'aux').reshape(-1, VBLK, VBLK)]
    dot_general x2 -> x0, matrix products: 34.2 us -> none  [the longest x1 25.4 us: per_device(): lax.dot_general(row_part, flattened, (((0,), (0,)), ((), ())), preferred_...]
    all_to_all x2 -> x0, starting transfers between devices: 33 us -> none  [the longest x1 18.5 us: per_device(): lax.all_to_all(outgoing_cols, 'aux', split_axis=1, concat_axis=0, tiled=T...]
  transfers between devices with their start and end apart: 2 -> 116, of which waited for: 2 -> 72; matrix products, arithmetic and copies ran while one was open for 2% -> 0% of each run, Pallas kernels for 0% -> 8%
where the time goes in v1:
time: 678 us; the launch traced here: 672 us
  waiting for transfers between devices  306 us (45%)
  starting transfers between devices  145 us (21%)
  Pallas kernels  119 us (18%)
  blocking collectives  78.6 us (12%)
  loops' own time  12.5 us (2%)
  local copies, waits for them, and re-layouts  7.58 us (1%)
    ppermute x55, waiting for transfers between devices, planned(): right[reach] = lax.ppermute(right[reach], 'aux', ring_shift(1))  181 us
    ppermute x55, starting transfers between devices, planned(): left[reach] = lax.ppermute(left[reach], 'aux', ring_shift(-1))  122 us
    ppermute x55, waiting for transfers between devices, planned(): left[reach] = lax.ppermute(left[reach], 'aux', ring_shift(-1))  110 us
    all_gather x1, blocking collectives, planned(): lax.all_gather(jnp.stack([paired, extra]), 'aux').reshape(-1, VBLK, VBLK)  78.6 us
    pallas_call x4, Pallas kernels, early(): pl.pallas_call(lambda *refs: early_kernel(*refs, sources=sources, job=job...  33.4 us
    pallas_call x2, Pallas kernels, finish(): pl.pallas_call(lambda *refs: finish_kernel(*refs, sources=sources, job=jo...  26.4 us
    pallas_call x1, Pallas kernels, make_plan(): pl.pallas_call(plan_kernel, out_shape=jax.ShapeDtypeStruct((96,), jnp.int...  26.1 us
    ppermute x6, waiting for transfers between devices, to_other_core(): return lax.ppermute(x, 'aux', [(i, i ^ 1) for i in range(n)])  14.4 us
  transfers between devices with their start and end apart: 116, of which 72 were waited for; matrix products, arithmetic and copies ran while one was open for 0% of the time, Pallas kernels for 8%

profile of v1, /device:TPU:69, one launch (start us, length us, event | category | flops | bytes accessed | tf_op | source)
XLA Modules:
  0.0 672.2 jit_solution(14402700648876396914)
XLA Ops:
  2.0 26.1 %plan.1 = s32[96]{0:T(128)S(1)} custom-call(s32[1]{0:T(128)} %bitcast.27.me, s32[64]{0:T(128)} %reshape.69.pairs, s32[512]{0:T(512)} %constant.70.clone.swaps, f32[256]{0:T(256)} %constant.71.clone.coolness), custom_call_target="tpu_custom_call" | custom-call | tf_op jit(solution)/shard_map/plan/pallas_call | solution.py:190
  28.2 642.3 %conditional.2 = (f32[48,48]{1,0:T(8,128)}, f32[1]{0:T(128)}) conditional(s32[]{:T(128)} %bitcast.28, (bf16[125,23040]{1,0:T(8,128)(2,1)}, s32[32,2]{0,1:T(2,128)}, bf16[900,900]{1,0:T(8,128)(2,1)}, f32[768]{0:T(1024)}) %tuple.24, (s32[1]{0:T(128)}, s32[96]{0:T(128)S(1)}, bf16[125,23040]{1,0:T(8,128)(2,1)}, bf16[900,900]{1,0:T(8,128)(2,1)}, ...), branch_computations={%region_0.5_spmd, %region_4.10_spmd} | conditional | flops 20341391360 | bytes 456990848 | solution.py:584
  37.1 11.4 %pack.1 = (bf16[1440,128]{1,0:T(8,128)(2,1)S(1)}, bf16[1440,128]{1,0:T(8,128)(2,1)S(1)}, bf16[1440,128]{1,0:T(8,128)(2,1)S(1)}, bf16[1440,128]{1,0:T(8,128)(2,1)...) custom-call(s32[1]{0:T(128)} %get-tuple-element.324.me, ...), custom_call_target="tpu_custom_call" | custom-call | tf_op jit(solution)/shard_map/cond/branch_1_fun/pack/pallas_call | solution.py:245
  53.2 8.8 %collective-permute-start.93 = (bf16[1440,128]{1,0:T(8,128)(2,1)S(1)}, bf16[1440,128]{1,0:T(8,128)(2,1)S(1)}, u32[]{:S(2)}, u32[]{:S(2)}) collective-permute-start(bf16[1440,128]{1,0:T(8,128)(2,1)S(1)} %get-tuple-element.338.refs_19_.refs_20_), channel_id=1, source_target_pairs={{0,30},{1,31},{2,0},{3,1},{4,2},{5,3},{6,4},{7,5},{8,6},{9,7},{10,... | collective-permute-start | bytes 1105928 | tf_op jit(solution)/shard_map/cond/branch_1_fun/ppermute | solution.py:533
  62.1 8.1 %collective-permute-done.84.refs_17_.refs_18_ = bf16[1440,128]{1,0:T(8,128)(2,1)S(1)} collective-permute-done((bf16[1440,128]{1,0:T(8,128)(2,1)S(1)}, bf16[1440,128]{1,0:T(8,128)(2,1)S(1)}, u32[]{:S(2)}, u32[]{:S(2)}) %collective-permute-start.84) | collective-permute-done | bytes 368672 | tf_op jit(solution)/shard_map/cond/branch_1_fun/ppermute | solution.py:532
  71.3 6.7 %collective-permute-done.89.refs_16_.refs_17_ = bf16[1440,128]{1,0:T(8,128)(2,1)S(1)} collective-permute-done((bf16[1440,128]{1,0:T(8,128)(2,1)S(1)}, bf16[1440,128]{1,0:T(8,128)(2,1)S(1)}, u32[]{:S(2)}, u32[]{:S(2)}) %collective-permute-start.89) | collective-permute-done | bytes 368672 | tf_op jit(solution)/shard_map/cond/branch_1_fun/ppermute | solution.py:532
  79.8 6.2 collective-permute-done.103.refs_15_.refs_16_
  86.0 7.9 %collective-permute-done.60.refs_18_.refs_19_ = bf16[1440,128]{1,0:T(8,128)(2,1)S(1)} collective-permute-done((bf16[1440,128]{1,0:T(8,128)(2,1)S(1)}, bf16[1440,128]{1,0:T(8,128)(2,1)S(1)}, u32[]{:S(2)}, u32[]{:S(2)}) %collective-permute-start.60) | collective-permute-done | bytes 368672 | tf_op jit(solution)/shard_map/cond/branch_1_fun/ppermute | solution.py:532
  102.9 6.7 %collective-permute-done.51 = bf16[1440,128]{1,0:T(8,128)(2,1)S(1)} collective-permute-done((bf16[1440,128]{1,0:T(8,128)(2,1)S(1)}, bf16[1440,128]{1,0:T(8,128)(2,1)S(1)}, u32[]{:S(2)}, u32[]{:S(2)}) %collective-permute-start.51) | collective-permute-done | bytes 368672 | tf_op jit(solution)/shard_map/cond/branch_1_fun/ppermute | solution.py:532
  112.4 5.2 collective-permute-done.108.refs_13_.refs_14_
  119.0 6.4 collective-permute-done.3
  126.9 6.4 collective-permute-done.11
  141.8 7.4 %collective-permute-done.85.refs_10_.refs_11_ = bf16[1440,128]{1,0:T(8,128)(2,1)S(1)} collective-permute-done((bf16[1440,128]{1,0:T(8,128)(2,1)S(1)}, bf16[1440,128]{1,0:T(8,128)(2,1)S(1)}, u32[]{:S(2)}, u32[]{:S(2)}) %collective-permute-start.85) | collective-permute-done | bytes 368672 | tf_op jit(solution)/shard_map/cond/branch_1_fun/ppermute | solution.py:532
  150.3 6.7 %collective-permute-done.90.refs_9_.refs_10_ = bf16[1440,128]{1,0:T(8,128)(2,1)S(1)} collective-permute-done((bf16[1440,128]{1,0:T(8,128)(2,1)S(1)}, bf16[1440,128]{1,0:T(8,128)(2,1)S(1)}, u32[]{:S(2)}, u32[]{:S(2)}) %collective-permute-start.90) | collective-permute-done | bytes 368672 | tf_op jit(solution)/shard_map/cond/branch_1_fun/ppermute | solution.py:532
  158.9 6.1 collective-permute-done.104.refs_8_.refs_9_
  165.0 7.9 %collective-permute-done.61.refs_11_.refs_12_ = bf16[1440,128]{1,0:T(8,128)(2,1)S(1)} collective-permute-done((bf16[1440,128]{1,0:T(8,128)(2,1)S(1)}, bf16[1440,128]{1,0:T(8,128)(2,1)S(1)}, u32[]{:S(2)}, u32[]{:S(2)}) %collective-permute-start.61) | collective-permute-done | bytes 368672 | tf_op jit(solution)/shard_map/cond/branch_1_fun/ppermute | solution.py:532
  180.8 7.9 %collective-permute-done.52.refs_12_.refs_13_ = bf16[1440,128]{1,0:T(8,128)(2,1)S(1)} collective-permute-done((bf16[1440,128]{1,0:T(8,128)(2,1)S(1)}, bf16[1440,128]{1,0:T(8,128)(2,1)S(1)}, u32[]{:S(2)}, u32[]{:S(2)}) %collective-permute-start.52) | collective-permute-done | bytes 368672 | tf_op jit(solution)/shard_map/cond/branch_1_fun/ppermute | solution.py:532
  191.5 5.7 collective-permute-done.44
  213.0 7.3 %collective-permute-done.86.refs_3_.refs_4_ = bf16[1440,128]{1,0:T(8,128)(2,1)S(1)} collective-permute-done((bf16[1440,128]{1,0:T(8,128)(2,1)S(1)}, bf16[1440,128]{1,0:T(8,128)(2,1)S(1)}, u32[]{:S(2)}, u32[]{:S(2)}) %collective-permute-start.86) | collective-permute-done | bytes 368672 | tf_op jit(solution)/shard_map/cond/branch_1_fun/ppermute | solution.py:532
  221.4 6.7 %collective-permute-done.91.refs_2_.refs_3_ = bf16[1440,128]{1,0:T(8,128)(2,1)S(1)} collective-permute-done((bf16[1440,128]{1,0:T(8,128)(2,1)S(1)}, bf16[1440,128]{1,0:T(8,128)(2,1)S(1)}, u32[]{:S(2)}, u32[]{:S(2)}) %collective-permute-start.91) | collective-permute-done | bytes 368672 | tf_op jit(solution)/shard_map/cond/branch_1_fun/ppermute | solution.py:532
  230.0 6.1 collective-permute-done.105.refs_1_.refs_2_
  236.1 7.9 %collective-permute-done.62.refs_4_.refs_5_ = bf16[1440,128]{1,0:T(8,128)(2,1)S(1)} collective-permute-done((bf16[1440,128]{1,0:T(8,128)(2,1)S(1)}, bf16[1440,128]{1,0:T(8,128)(2,1)S(1)}, u32[]{:S(2)}, u32[]{:S(2)}) %collective-permute-start.62) | collective-permute-done | bytes 368672 | tf_op jit(solution)/shard_map/cond/branch_1_fun/ppermute | solution.py:532
  247.4 4.5 collective-permute-done.53.refs_5_.refs_6_
  253.6 7.9 %collective-permute-done.45.refs_37_.refs_38_ = bf16[1440,128]{1,0:T(8,128)(2,1)S(1)} collective-permute-done((bf16[1440,128]{1,0:T(8,128)(2,1)S(1)}, bf16[1440,128]{1,0:T(8,128)(2,1)S(1)}, u32[]{:S(2)}, u32[]{:S(2)}) %collective-permute-start.45) | collective-permute-done | bytes 368672 | tf_op jit(solution)/shard_map/cond/branch_1_fun/ppermute | solution.py:533
  269.4 6.2 collective-permute-done.21
  285.2 6.2 collective-permute-done.54.refs_10_.refs_12_
  293.1 7.9 %collective-permute-done.46.refs_14_.refs_16_ = bf16[1440,128]{1,0:T(8,128)(2,1)S(1)} collective-permute-done((bf16[1440,128]{1,0:T(8,128)(2,1)S(1)}, bf16[1440,128]{1,0:T(8,128)(2,1)S(1)}, u32[]{:S(2)}, u32[]{:S(2)}) %collective-permute-start.46) | collective-permute-done | bytes 368672 | tf_op jit(solution)/shard_map/cond/branch_1_fun/ppermute | solution.py:533
  308.9 6.2 collective-permute-done.22
  324.7 6.2 collective-permute-done.55.refs_3_.refs_5_
  332.6 7.9 %collective-permute-done.47.refs_21_.refs_23_ = bf16[1440,128]{1,0:T(8,128)(2,1)S(1)} collective-permute-done((bf16[1440,128]{1,0:T(8,128)(2,1)S(1)}, bf16[1440,128]{1,0:T(8,128)(2,1)S(1)}, u32[]{:S(2)}, u32[]{:S(2)}) %collective-permute-start.47) | collective-permute-done | bytes 368672 | tf_op jit(solution)/shard_map/cond/branch_1_fun/ppermute | solution.py:533
  340.5 7.9 %collective-permute-done.31.refs_19_.refs_21_ = bf16[1440,128]{1,0:T(8,128)(2,1)S(1)} collective-permute-done((bf16[1440,128]{1,0:T(8,128)(2,1)S(1)}, bf16[1440,128]{1,0:T(8,128)(2,1)S(1)}, u32[]{:S(2)}, u32[]{:S(2)}) %collective-permute-start.31) | collective-permute-done | bytes 368672 | tf_op jit(solution)/shard_map/cond/branch_1_fun/ppermute | solution.py:533
  351.8 4.5 collective-permute-done.39.refs_20_.refs_22_
  359.8 4.3 collective-permute-done.32.refs_20_.refs_23_
  395.8 7.9 %collective-permute-done.33.refs_27_.refs_30_ = bf16[1440,128]{1,0:T(8,128)(2,1)S(1)} collective-permute-done((bf16[1440,128]{1,0:T(8,128)(2,1)S(1)}, bf16[1440,128]{1,0:T(8,128)(2,1)S(1)}, u32[]{:S(2)}, u32[]{:S(2)}) %collective-permute-start.33) | collective-permute-done | bytes 368672 | tf_op jit(solution)/shard_map/cond/branch_1_fun/ppermute | solution.py:533
  407.9 4.3 select.11
  415.3 4.5 collective-permute-start.115
  427.5 7.9 %collective-permute-done.34.refs_4_.refs_7_ = bf16[1440,128]{1,0:T(8,128)(2,1)S(1)} collective-permute-done((bf16[1440,128]{1,0:T(8,128)(2,1)}, bf16[1440,128]{1,0:T(8,128)(2,1)S(1)}, u32[]{:S(2)}, u32[]{:S(2)}) %collective-permute-start.34) | collective-permute-done | bytes 368672 | tf_op jit(solution)/shard_map/cond/branch_1_fun/ppermute | solution.py:533
  438.8 4.5 collective-permute-done.42.refs_5_.refs_8_
  451.2 7.8 %collective-permute-done.58.refs_11_.refs_14_ = bf16[1440,128]{1,0:T(8,128)(2,1)S(1)} collective-permute-done((bf16[1440,128]{1,0:T(8,128)(2,1)S(1)}, bf16[1440,128]{1,0:T(8,128)(2,1)S(1)}, u32[]{:S(2)}, u32[]{:S(2)}) %collective-permute-start.58) | collective-permute-done | bytes 368672 | tf_op jit(solution)/shard_map/cond/branch_1_fun/ppermute | solution.py:533
  462.5 4.3 collective-permute-done.59.refs_12_.refs_15_
  488.4 7.9 %density.1.refs_3_ = bf16[960,960]{1,0:T(8,128)(2,1)} custom-call(bf16[900,900]{1,0:T(8,128)(2,1)} %get-tuple-element.346.rdm), custom_call_target="tpu_custom_call" | custom-call | tf_op jit(solution)/shard_map/cond/branch_1_fun/density/pallas_call | solution.py:392
  504.1 24.6 %conditional = (f32[1,6,384]{2,1,0:T(8,128)S(1)}) conditional(s32[]{:T(128)} %bitcast.19, () %tuple.18, (s32[96]{0:T(128)S(1)}, bf16[1440,128]{1,0:T(8,128)(2,1)}, bf16[1440,128]{1,0:T(8,128)(2,1)}, bf16[1440,128]{1,0:T(8,128)(2,1)}, bf16[1440,128]{1,0:T(8,128)(2,1)}, /*index=5*/bf16[1440,128]{1,0:T(8,128)(2,1)}, bf16[1440,128]{1,0:T(8,128)(2,1)}, ...), branch_computations={%region_5.6_spmd, %region_6.7_spmd} | conditional | bytes 92898336 | solution.py:555
  510.1 6.2 collective-permute-done.2.refs_1_
  517.5 8.2 %collective-permute-done.1.refs_1_ = bf16[2,4,1440,128]{3,2,1,0:T(8,128)(2,1)S(1)} collective-permute-done((bf16[2,4,1440,128]{3,2,1,0:T(8,128)(2,1)}, bf16[2,4,1440,128]{3,2,1,0:T(8,128)(2,1)S(1)}, u32[]{:S(2)}, u32[]{:S(2)}) %collective-permute-start.1) | collective-permute-done | bytes 2949152 | tf_op jit(solution)/shard_map/cond/branch_1_fun/cond/branch_1_fun/ppermute | solution.py:487
  530.8 17.1 %early.6.refs_2_ = f32[12,1440,128]{2,1,0:T(8,128)} custom-call(s32[96]{0:T(128)S(1)} %get-tuple-element.323.table.refs_0_, bf16[2,7,1440,128]{3,2,1,0:T(8,128)(2,1)} %collective-permute-done.115.refs_1_, bf16[1440,128]{1,0:T(8,128)(2,1)} %copy-done.32, bf16[1440,128]{1,0:T(8,128)(2,1)} %copy-done.30, bf16[1440,128]{1,0:T(8,128)(2,1)} %copy-done.29, ...), custom_call_target="tpu_custom_call" | custom-call | tf_op jit(solution)/shard_map/cond/branch_1_fun/early/pallas_call | solution.py:448
  548.2 14.5 %early.7.refs_2_ = f32[12,1440,128]{2,1,0:T(8,128)} custom-call(s32[96]{0:T(128)S(1)} %get-tuple-element.323.table.refs_0_, bf16[2,4,1440,128]{3,2,1,0:T(8,128)(2,1)S(1)} %collective-permute-done.102.refs_1_, f32[12,1440,128]{2,1,0:T(8,128)} %early.6.refs_2_, bf16[1440,128]{1,0:T(8,128)(2,1)} %collective-permute-done.88.refs_1_.refs_3_, ...), custom_call_target="tpu_custom_call" | custom-call | tf_op jit(solution)/shard_map/cond/branch_1_fun/early/pallas_call | solution.py:448
  562.7 24.6 %finish.3 = f32[6,384]{1,0:T(8,128)S(1)} custom-call(s32[96]{0:T(128)S(1)} %get-tuple-element.323.table.refs_0_, bf16[2,5,1440,128]{3,2,1,0:T(8,128)(2,1)} %collective-permute-done.83.refs_1_, f32[12,1440,128]{2,1,0:T(8,128)} %early.7.refs_2_, bf16[960,960]{1,0:T(8,128)(2,1)} %density.1.refs_3_, bf16[1440,128]{1,0:T(8,128)(2,1)} %copy-done.119, ...), custom_call_target="tpu_custom_call" | custom-call | tf_op jit(solution)/shard_map/cond/branch_1_fun/finish/pallas_call | solution.py:463
  587.4 78.6 %all-gather = f32[64,6,384]{2,1,0:T(8,128)S(1)} all-gather(f32[2,6,384]{2,1,0:T(8,128)S(1)} %pad_maximum_fusion), channel_id=2, replica_groups=mesh['groups'=4,'aux'=32] {'aux'}, dimensions={0}, use_global_device_ids=true | all-gather | bytes 608256 | tf_op jit(solution)/shard_map/cond/branch_1_fun/all_gather | solution.py:556
  (490 shorter events, 219.7 us)
Async XLA Ops:
  48.6 21.5 %collective-permute-start.84 = (bf16[1440,128]{1,0:T(8,128)(2,1)S(1)}, bf16[1440,128]{1,0:T(8,128)(2,1)S(1)}, u32[]{:S(2)}, u32[]{:S(2)}) collective-permute-start(bf16[1440,128]{1,0:T(8,128)(2,1)S(1)} %get-tuple-element.336.refs_24_.refs_25_), channel_id=1, source_target_pairs={{0,2},{1,3},{2,4},{3,5},{4,6},{5,7},{6,8},{7,9},{8,10},{9,11},{10,... | collective-permute-start | bytes 1105928 | tf_op jit(solution)/shard_map/cond/branch_1_fun/ppermute | solution.py:532
  51.4 26.7 %collective-permute-start.89 = (bf16[1440,128]{1,0:T(8,128)(2,1)S(1)}, bf16[1440,128]{1,0:T(8,128)(2,1)S(1)}, u32[]{:S(2)}, u32[]{:S(2)}) collective-permute-start(bf16[1440,128]{1,0:T(8,128)(2,1)S(1)} %get-tuple-element.337.refs_23_.refs_24_), channel_id=1, source_target_pairs={{0,2},{1,3},{2,4},{3,5},{4,6},{5,7},{6,8},{7,9},{8,10},{9,11},{10,... | collective-permute-start | bytes 1105928 | tf_op jit(solution)/shard_map/cond/branch_1_fun/ppermute | solution.py:532
  53.2 26.0 %collective-permute-start.93 = (bf16[1440,128]{1,0:T(8,128)(2,1)S(1)}, bf16[1440,128]{1,0:T(8,128)(2,1)S(1)}, u32[]{:S(2)}, u32[]{:S(2)}) collective-permute-start(bf16[1440,128]{1,0:T(8,128)(2,1)S(1)} %get-tuple-element.338.refs_19_.refs_20_), channel_id=1, source_target_pairs={{0,30},{1,31},{2,0},{3,1},{4,2},{5,3},{6,4},{7,5},{8,6},{9,7},{10,... | collective-permute-start | bytes 1105928 | tf_op jit(solution)/shard_map/cond/branch_1_fun/ppermute | solution.py:533
  62.1 23.9 %collective-permute-start.103 = (bf16[1440,128]{1,0:T(8,128)(2,1)S(1)}, bf16[1440,128]{1,0:T(8,128)(2,1)S(1)}, u32[]{:S(2)}, u32[]{:S(2)}) collective-permute-start(bf16[1440,128]{1,0:T(8,128)(2,1)S(1)} %get-tuple-element.340.refs_22_.refs_23_), channel_id=1, source_target_pairs={{0,2},{1,3},{2,4},{3,5},{4,6},{5,7},{6,8},{7,9},{8,10},{9,11},{10,... | collective-permute-start | bytes 1105928 | tf_op jit(solution)/shard_map/cond/branch_1_fun/ppermute | solution.py:532
  62.1 31.8 %collective-permute-start.60 = (bf16[1440,128]{1,0:T(8,128)(2,1)S(1)}, bf16[1440,128]{1,0:T(8,128)(2,1)S(1)}, u32[]{:S(2)}, u32[]{:S(2)}) collective-permute-start(bf16[1440,128]{1,0:T(8,128)(2,1)S(1)} %get-tuple-element.333), channel_id=1, source_target_pairs={{0,2},{1,3},{2,4},{3,5},{4,6},{5,7},{6,8},{7,9},{8,10},{9,11},{10,... | collective-permute-start | bytes 1105928 | tf_op jit(solution)/shard_map/cond/branch_1_fun/ppermute | solution.py:532
  70.2 23.7 %collective-permute-start.75 = (bf16[1440,128]{1,0:T(8,128)(2,1)S(1)}, bf16[1440,128]{1,0:T(8,128)(2,1)S(1)}, u32[]{:S(2)}, u32[]{:S(2)}) collective-permute-start(bf16[1440,128]{1,0:T(8,128)(2,1)S(1)} %get-tuple-element.335), channel_id=1, source_target_pairs={{0,30},{1,31},{2,0},{3,1},{4,2},{5,3},{6,4},{7,5},{8,6},{9,7},{10,... | collective-permute-start | bytes 1105928 | tf_op jit(solution)/shard_map/cond/branch_1_fun/ppermute | solution.py:533
  96.7 20.9 %collective-permute-start.108 = (bf16[1440,128]{1,0:T(8,128)(2,1)S(1)}, bf16[1440,128]{1,0:T(8,128)(2,1)S(1)}, u32[]{:S(2)}, u32[]{:S(2)}) collective-permute-start(bf16[1440,128]{1,0:T(8,128)(2,1)S(1)} %get-tuple-element.342.refs_20_.refs_21_), channel_id=1, source_target_pairs={{0,2},{1,3},{2,4},{3,5},{4,6},{5,7},{6,8},{7,9},{8,10},{9,11},{10,... | collective-permute-start | bytes 1105928 | tf_op jit(solution)/shard_map/cond/branch_1_fun/ppermute | solution.py:532
  112.4 21.0 %collective-permute-start.11 = (bf16[1440,128]{1,0:T(8,128)(2,1)S(1)}, bf16[1440,128]{1,0:T(8,128)(2,1)S(1)}, u32[]{:S(2)}, u32[]{:S(2)}) collective-permute-start(bf16[1440,128]{1,0:T(8,128)(2,1)S(1)} %get-tuple-element.327), channel_id=1, source_target_pairs={{0,2},{1,3},{2,4},{3,5},{4,6},{5,7},{6,8},{7,9},{8,10},{9,11},{10,... | collective-permute-start | bytes 1105928 | tf_op jit(solution)/shard_map/cond/branch_1_fun/ppermute | solution.py:532
  118.7 22.5 %collective-permute-start.19 = (bf16[1440,128]{1,0:T(8,128)(2,1)S(1)}, bf16[1440,128]{1,0:T(8,128)(2,1)S(1)}, u32[]{:S(2)}, u32[]{:S(2)}) collective-permute-start(bf16[1440,128]{1,0:T(8,128)(2,1)S(1)} %get-tuple-element.328), channel_id=1, source_target_pairs={{0,2},{1,3},{2,4},{3,5},{4,6},{5,7},{6,8},{7,9},{8,10},{9,11},{10,... | collective-permute-start | bytes 1105928 | tf_op jit(solution)/shard_map/cond/branch_1_fun/ppermute | solution.py:532
  126.6 22.5 %collective-permute-start.85 = (bf16[1440,128]{1,0:T(8,128)(2,1)S(1)}, bf16[1440,128]{1,0:T(8,128)(2,1)S(1)}, u32[]{:S(2)}, u32[]{:S(2)}) collective-permute-start(bf16[1440,128]{1,0:T(8,128)(2,1)S(1)} %collective-permute-done.84.refs_17_.refs_18_), channel_id=1, source_target_pairs={{0,2},{1,3},{2,4},{3,5},{4,6},{5,7},{6,8},{7,9},{8,10},{9,11},{10,... | collective-permute-start | bytes 1105928 | tf_op jit(solution)/shard_map/cond/branch_1_fun/ppermute | solution.py:532
  133.4 23.7 %collective-permute-start.90 = (bf16[1440,128]{1,0:T(8,128)(2,1)S(1)}, bf16[1440,128]{1,0:T(8,128)(2,1)S(1)}, u32[]{:S(2)}, u32[]{:S(2)}) collective-permute-start(bf16[1440,128]{1,0:T(8,128)(2,1)S(1)} %collective-permute-done.89.refs_16_.refs_17_), channel_id=1, source_target_pairs={{0,2},{1,3},{2,4},{3,5},{4,6},{5,7},{6,8},{7,9},{8,10},{9,11},{10,... | collective-permute-start | bytes 1105928 | tf_op jit(solution)/shard_map/cond/branch_1_fun/ppermute | solution.py:532
  133.9 24.4 %collective-permute-start.94 = (bf16[1440,128]{1,0:T(8,128)(2,1)S(1)}, bf16[1440,128]{1,0:T(8,128)(2,1)S(1)}, u32[]{:S(2)}, u32[]{:S(2)}) collective-permute-start(bf16[1440,128]{1,0:T(8,128)(2,1)S(1)} %collective-permute-done.93.refs_26_.refs_27_), channel_id=1, source_target_pairs={{0,30},{1,31},{2,0},{3,1},{4,2},{5,3},{6,4},{7,5},{8,6},{9,7},{10,... | collective-permute-start | bytes 1105928 | tf_op jit(solution)/shard_map/cond/branch_1_fun/ppermute | solution.py:533
  141.3 23.7 %collective-permute-start.104 = (bf16[1440,128]{1,0:T(8,128)(2,1)S(1)}, bf16[1440,128]{1,0:T(8,128)(2,1)S(1)}, u32[]{:S(2)}, u32[]{:S(2)}) collective-permute-start(bf16[1440,128]{1,0:T(8,128)(2,1)S(1)} %collective-permute-done.103.refs_15_.refs_16_), channel_id=1, source_target_pairs={{0,2},{1,3},{2,4},{3,5},{4,6},{5,7},{6,8},{7,9},{8,10},{9,11},{10,... | collective-permute-start | bytes 1105928 | tf_op jit(solution)/shard_map/cond/branch_1_fun/ppermute | solution.py:532
  141.8 31.1 %collective-permute-start.61 = (bf16[1440,128]{1,0:T(8,128)(2,1)S(1)}, bf16[1440,128]{1,0:T(8,128)(2,1)S(1)}, u32[]{:S(2)}, u32[]{:S(2)}) collective-permute-start(bf16[1440,128]{1,0:T(8,128)(2,1)S(1)} %collective-permute-done.60.refs_18_.refs_19_), channel_id=1, source_target_pairs={{0,2},{1,3},{2,4},{3,5},{4,6},{5,7},{6,8},{7,9},{8,10},{9,11},{10,... | collective-permute-start | bytes 1105928 | tf_op jit(solution)/shard_map/cond/branch_1_fun/ppermute | solution.py:532
  149.2 23.7 %collective-permute-start.76 = (bf16[1440,128]{1,0:T(8,128)(2,1)S(1)}, bf16[1440,128]{1,0:T(8,128)(2,1)S(1)}, u32[]{:S(2)}, u32[]{:S(2)}) collective-permute-start(bf16[1440,128]{1,0:T(8,128)(2,1)S(1)} %collective-permute-done.75.refs_25_.refs_26_), channel_id=1, source_target_pairs={{0,30},{1,31},{2,0},{3,1},{4,2},{5,3},{6,4},{7,5},{8,6},{9,7},{10,... | collective-permute-start | bytes 1105928 | tf_op jit(solution)/shard_map/cond/branch_1_fun/ppermute | solution.py:533
  175.8 21.3 %collective-permute-start.44 = (bf16[1440,128]{1,0:T(8,128)(2,1)S(1)}, bf16[1440,128]{1,0:T(8,128)(2,1)S(1)}, u32[]{:S(2)}, u32[]{:S(2)}) collective-permute-start(bf16[1440,128]{1,0:T(8,128)(2,1)S(1)} %collective-permute-done.43), channel_id=1, source_target_pairs={{0,30},{1,31},{2,0},{3,1},{4,2},{5,3},{6,4},{7,5},{8,6},{9,7},{10,... | collective-permute-start | bytes 1105928 | tf_op jit(solution)/shard_map/cond/branch_1_fun/ppermute | solution.py:533
  180.8 19.8 %collective-permute-start.4 = (bf16[1440,128]{1,0:T(8,128)(2,1)S(1)}, bf16[1440,128]{1,0:T(8,128)(2,1)S(1)}, u32[]{:S(2)}, u32[]{:S(2)}) collective-permute-start(bf16[1440,128]{1,0:T(8,128)(2,1)S(1)} %collective-permute-done.3), channel_id=1, source_target_pairs={{0,2},{1,3},{2,4},{3,5},{4,6},{5,7},{6,8},{7,9},{8,10},{9,11},{10,... | collective-permute-start | bytes 1105928 | tf_op jit(solution)/shard_map/cond/branch_1_fun/ppermute | solution.py:532
  191.4 21.0 %collective-permute-start.20 = (bf16[1440,128]{1,0:T(8,128)(2,1)S(1)}, bf16[1440,128]{1,0:T(8,128)(2,1)S(1)}, u32[]{:S(2)}, u32[]{:S(2)}) collective-permute-start(bf16[1440,128]{1,0:T(8,128)(2,1)S(1)} %collective-permute-done.19), channel_id=1, source_target_pairs={{0,2},{1,3},{2,4},{3,5},{4,6},{5,7},{6,8},{7,9},{8,10},{9,11},{10,... | collective-permute-start | bytes 1105928 | tf_op jit(solution)/shard_map/cond/branch_1_fun/ppermute | solution.py:532
  200.6 19.7 %collective-permute-start.86 = (bf16[1440,128]{1,0:T(8,128)(2,1)S(1)}, bf16[1440,128]{1,0:T(8,128)(2,1)S(1)}, u32[]{:S(2)}, u32[]{:S(2)}) collective-permute-start(bf16[1440,128]{1,0:T(8,128)(2,1)S(1)} %collective-permute-done.85.refs_10_.refs_11_), channel_id=1, source_target_pairs={{0,2},{1,3},{2,4},{3,5},{4,6},{5,7},{6,8},{7,9},{8,10},{9,11},{10,... | collective-permute-start | bytes 1105928 | tf_op jit(solution)/shard_map/cond/branch_1_fun/ppermute | solution.py:532
  204.5 23.7 %collective-permute-start.91 = (bf16[1440,128]{1,0:T(8,128)(2,1)S(1)}, bf16[1440,128]{1,0:T(8,128)(2,1)S(1)}, u32[]{:S(2)}, u32[]{:S(2)}) collective-permute-start(bf16[1440,128]{1,0:T(8,128)(2,1)S(1)} %collective-permute-done.90.refs_9_.refs_10_), channel_id=1, source_target_pairs={{0,2},{1,3},{2,4},{3,5},{4,6},{5,7},{6,8},{7,9},{8,10},{9,11},{10,... | collective-permute-start | bytes 1105928 | tf_op jit(solution)/shard_map/cond/branch_1_fun/ppermute | solution.py:532
  205.1 24.3 %collective-permute-start.95 = (bf16[1440,128]{1,0:T(8,128)(2,1)S(1)}, bf16[1440,128]{1,0:T(8,128)(2,1)S(1)}, u32[]{:S(2)}, u32[]{:S(2)}) collective-permute-start(bf16[1440,128]{1,0:T(8,128)(2,1)S(1)} %collective-permute-done.94.refs_33_.refs_34_), channel_id=1, source_target_pairs={{0,30},{1,31},{2,0},{3,1},{4,2},{5,3},{6,4},{7,5},{8,6},{9,7},{10,... | collective-permute-start | bytes 1105928 | tf_op jit(solution)/shard_map/cond/branch_1_fun/ppermute | solution.py:533
  212.4 23.7 %collective-permute-start.105 = (bf16[1440,128]{1,0:T(8,128)(2,1)S(1)}, bf16[1440,128]{1,0:T(8,128)(2,1)S(1)}, u32[]{:S(2)}, u32[]{:S(2)}) collective-permute-start(bf16[1440,128]{1,0:T(8,128)(2,1)S(1)} %collective-permute-done.104.refs_8_.refs_9_), channel_id=1, source_target_pairs={{0,2},{1,3},{2,4},{3,5},{4,6},{5,7},{6,8},{7,9},{8,10},{9,11},{10,... | collective-permute-start | bytes 1105928 | tf_op jit(solution)/shard_map/cond/branch_1_fun/ppermute | solution.py:532
  213.0 31.0 %collective-permute-start.62 = (bf16[1440,128]{1,0:T(8,128)(2,1)S(1)}, bf16[1440,128]{1,0:T(8,128)(2,1)S(1)}, u32[]{:S(2)}, u32[]{:S(2)}) collective-permute-start(bf16[1440,128]{1,0:T(8,128)(2,1)S(1)} %collective-permute-done.61.refs_11_.refs_12_), channel_id=1, source_target_pairs={{0,2},{1,3},{2,4},{3,5},{4,6},{5,7},{6,8},{7,9},{8,10},{9,11},{10,... | collective-permute-start | bytes 1105928 | tf_op jit(solution)/shard_map/cond/branch_1_fun/ppermute | solution.py:532
  220.3 24.9 %collective-permute-start.77 = (bf16[1440,128]{1,0:T(8,128)(2,1)S(1)}, bf16[1440,128]{1,0:T(8,128)(2,1)S(1)}, u32[]{:S(2)}, u32[]{:S(2)}) collective-permute-start(bf16[1440,128]{1,0:T(8,128)(2,1)S(1)} %collective-permute-done.76.refs_32_.refs_33_), channel_id=1, source_target_pairs={{0,30},{1,31},{2,0},{3,1},{4,2},{5,3},{6,4},{7,5},{8,6},{9,7},{10,... | collective-permute-start | bytes 1105928 | tf_op jit(solution)/shard_map/cond/branch_1_fun/ppermute | solution.py:533
  246.8 20.8 %collective-permute-start.13 = (bf16[1440,128]{1,0:T(8,128)(2,1)S(1)}, bf16[1440,128]{1,0:T(8,128)(2,1)S(1)}, u32[]{:S(2)}, u32[]{:S(2)}) collective-permute-start(bf16[1440,128]{1,0:T(8,128)(2,1)S(1)} %collective-permute-done.12), channel_id=1, source_target_pairs={{0,2},{1,3},{2,4},{3,5},{4,6},{5,7},{6,8},{7,9},{8,10},{9,11},{10,... | collective-permute-start | bytes 1105928 | tf_op jit(solution)/shard_map/cond/branch_1_fun/ppermute | solution.py:532
  253.6 22.0 %collective-permute-start.21 = (bf16[1440,128]{1,0:T(8,128)(2,1)S(1)}, bf16[1440,128]{1,0:T(8,128)(2,1)S(1)}, u32[]{:S(2)}, u32[]{:S(2)}) collective-permute-start(bf16[1440,128]{1,0:T(8,128)(2,1)S(1)} %collective-permute-done.20), channel_id=1, source_target_pairs={{0,2},{1,3},{2,4},{3,5},{4,6},{5,7},{6,8},{7,9},{8,10},{9,11},{10,... | collective-permute-start | bytes 1105928 | tf_op jit(solution)/shard_map/cond/branch_1_fun/ppermute | solution.py:532
  269.3 22.0 %collective-permute-start.54 = (bf16[1440,128]{1,0:T(8,128)(2,1)S(1)}, bf16[1440,128]{1,0:T(8,128)(2,1)S(1)}, u32[]{:S(2)}, u32[]{:S(2)}) collective-permute-start(bf16[1440,128]{1,0:T(8,128)(2,1)S(1)} %collective-permute-done.53.refs_5_.refs_6_), channel_id=1, source_target_pairs={{0,2},{1,3},{2,4},{3,5},{4,6},{5,7},{6,8},{7,9},{8,10},{9,11},{10,... | collective-permute-start | bytes 1105928 | tf_op jit(solution)/shard_map/cond/branch_1_fun/ppermute | solution.py:532
  277.2 23.7 %collective-permute-start.46 = (bf16[1440,128]{1,0:T(8,128)(2,1)S(1)}, bf16[1440,128]{1,0:T(8,128)(2,1)S(1)}, u32[]{:S(2)}, u32[]{:S(2)}) collective-permute-start(bf16[1440,128]{1,0:T(8,128)(2,1)S(1)} %collective-permute-done.45.refs_37_.refs_38_), channel_id=1, source_target_pairs={{0,30},{1,31},{2,0},{3,1},{4,2},{5,3},{6,4},{7,5},{8,6},{9,7},{10,... | collective-permute-start | bytes 1105928 | tf_op jit(solution)/shard_map/cond/branch_1_fun/ppermute | solution.py:533
  283.5 20.9 %collective-permute-start.6 = (bf16[1440,128]{1,0:T(8,128)(2,1)S(1)}, bf16[1440,128]{1,0:T(8,128)(2,1)S(1)}, u32[]{:S(2)}, u32[]{:S(2)}) collective-permute-start(bf16[1440,128]{1,0:T(8,128)(2,1)S(1)} %collective-permute-done.5.refs_6_.refs_7_), channel_id=1, source_target_pairs={{0,2},{1,3},{2,4},{3,5},{4,6},{5,7},{6,8},{7,9},{8,10},{9,11},{10,... | collective-permute-start | bytes 1105928 | tf_op jit(solution)/shard_map/cond/branch_1_fun/ppermute | solution.py:532
  285.2 22.0 %collective-permute-start.14 = (bf16[1440,128]{1,0:T(8,128)(2,1)S(1)}, bf16[1440,128]{1,0:T(8,128)(2,1)S(1)}, u32[]{:S(2)}, u32[]{:S(2)}) collective-permute-start(bf16[1440,128]{1,0:T(8,128)(2,1)S(1)} %collective-permute-done.13), channel_id=1, source_target_pairs={{0,2},{1,3},{2,4},{3,5},{4,6},{5,7},{6,8},{7,9},{8,10},{9,11},{10,... | collective-permute-start | bytes 1105928 | tf_op jit(solution)/shard_map/cond/branch_1_fun/ppermute | solution.py:532
  293.1 22.0 %collective-permute-start.22 = (bf16[1440,128]{1,0:T(8,128)(2,1)S(1)}, bf16[1440,128]{1,0:T(8,128)(2,1)S(1)}, u32[]{:S(2)}, u32[]{:S(2)}) collective-permute-start(bf16[1440,128]{1,0:T(8,128)(2,1)S(1)} %collective-permute-done.21), channel_id=1, source_target_pairs={{0,2},{1,3},{2,4},{3,5},{4,6},{5,7},{6,8},{7,9},{8,10},{9,11},{10,... | collective-permute-start | bytes 1105928 | tf_op jit(solution)/shard_map/cond/branch_1_fun/ppermute | solution.py:532
  308.9 22.0 %collective-permute-start.55 = (bf16[1440,128]{1,0:T(8,128)(2,1)S(1)}, bf16[1440,128]{1,0:T(8,128)(2,1)S(1)}, u32[]{:S(2)}, u32[]{:S(2)}) collective-permute-start(bf16[1440,128]{1,0:T(8,128)(2,1)S(1)} %collective-permute-done.54.refs_10_.refs_12_), channel_id=1, source_target_pairs={{0,2},{1,3},{2,4},{3,5},{4,6},{5,7},{6,8},{7,9},{8,10},{9,11},{10,... | collective-permute-start | bytes 1105928 | tf_op jit(solution)/shard_map/cond/branch_1_fun/ppermute | solution.py:532
  316.7 23.7 %collective-permute-start.47 = (bf16[1440,128]{1,0:T(8,128)(2,1)S(1)}, bf16[1440,128]{1,0:T(8,128)(2,1)S(1)}, u32[]{:S(2)}, u32[]{:S(2)}) collective-permute-start(bf16[1440,128]{1,0:T(8,128)(2,1)S(1)} %collective-permute-done.46.refs_14_.refs_16_), channel_id=1, source_target_pairs={{0,30},{1,31},{2,0},{3,1},{4,2},{5,3},{6,4},{7,5},{8,6},{9,7},{10,... | collective-permute-start | bytes 1105928 | tf_op jit(solution)/shard_map/cond/branch_1_fun/ppermute | solution.py:533
  323.0 25.4 %collective-permute-start.31 = (bf16[1440,128]{1,0:T(8,128)(2,1)S(1)}, bf16[1440,128]{1,0:T(8,128)(2,1)S(1)}, u32[]{:S(2)}, u32[]{:S(2)}) collective-permute-start(bf16[1440,128]{1,0:T(8,128)(2,1)S(1)} %collective-permute-done.30), channel_id=1, source_target_pairs={{0,30},{1,31},{2,0},{3,1},{4,2},{5,3},{6,4},{7,5},{8,6},{9,7},{10,... | collective-permute-start | bytes 1105928 | tf_op jit(solution)/shard_map/cond/branch_1_fun/ppermute | solution.py:533
  324.7 27.1 %collective-permute-start.23 = (bf16[1440,128]{1,0:T(8,128)(2,1)S(1)}, bf16[1440,128]{1,0:T(8,128)(2,1)S(1)}, u32[]{:S(2)}, u32[]{:S(2)}) collective-permute-start(bf16[1440,128]{1,0:T(8,128)(2,1)S(1)} %collective-permute-done.22), channel_id=1, source_target_pairs={{0,2},{1,3},{2,4},{3,5},{4,6},{5,7},{6,8},{7,9},{8,10},{9,11},{10,... | collective-permute-start | bytes 1105928 | tf_op jit(solution)/shard_map/cond/branch_1_fun/ppermute | solution.py:532
  330.9 25.4 %collective-permute-start.39 = (bf16[1440,128]{1,0:T(8,128)(2,1)S(1)}, bf16[1440,128]{1,0:T(8,128)(2,1)S(1)}, u32[]{:S(2)}, u32[]{:S(2)}) collective-permute-start(bf16[1440,128]{1,0:T(8,128)(2,1)S(1)} %collective-permute-done.38.refs_13_.refs_15_), channel_id=1, source_target_pairs={{0,30},{1,31},{2,0},{3,1},{4,2},{5,3},{6,4},{7,5},{8,6},{9,7},{10,... | collective-permute-start | bytes 1105928 | tf_op jit(solution)/shard_map/cond/branch_1_fun/ppermute | solution.py:533
  332.6 27.1 %collective-permute-start.15 = (bf16[1440,128]{1,0:T(8,128)(2,1)S(1)}, bf16[1440,128]{1,0:T(8,128)(2,1)S(1)}, u32[]{:S(2)}, u32[]{:S(2)}) collective-permute-start(bf16[1440,128]{1,0:T(8,128)(2,1)S(1)} %collective-permute-done.14.refs_12_.refs_14_), channel_id=1, source_target_pairs={{0,2},{1,3},{2,4},{3,5},{4,6},{5,7},{6,8},{7,9},{8,10},{9,11},{10,... | collective-permute-start | bytes 1105928 | tf_op jit(solution)/shard_map/cond/branch_1_fun/ppermute | solution.py:532
  340.5 19.2 %collective-permute-start.7 = (bf16[1440,128]{1,0:T(8,128)(2,1)S(1)}, bf16[1440,128]{1,0:T(8,128)(2,1)S(1)}, u32[]{:S(2)}, u32[]{:S(2)}) collective-permute-start(bf16[1440,128]{1,0:T(8,128)(2,1)S(1)} %collective-permute-done.6.refs_11_.refs_13_), channel_id=1, source_target_pairs={{0,2},{1,3},{2,4},{3,5},{4,6},{5,7},{6,8},{7,9},{8,10},{9,11},{10,... | collective-permute-start | bytes 1105928 | tf_op jit(solution)/shard_map/cond/branch_1_fun/ppermute | solution.py:532
  376.0 19.8 %collective-permute-start.80 = (bf16[1440,128]{1,0:T(8,128)(2,1)S(1)}, bf16[1440,128]{1,0:T(8,128)(2,1)S(1)}, u32[]{:S(2)}, u32[]{:S(2)}) collective-permute-start(bf16[1440,128]{1,0:T(8,128)(2,1)S(1)} %collective-permute-done.79.refs_23_.refs_25_), channel_id=1, source_target_pairs={{0,30},{1,31},{2,0},{3,1},{4,2},{5,3},{6,4},{7,5},{8,6},{9,7},{10,... | collective-permute-start | bytes 1105928 | tf_op jit(solution)/shard_map/cond/branch_1_fun/ppermute | solution.py:533
  379.9 23.7 %collective-permute-start.33 = (bf16[1440,128]{1,0:T(8,128)(2,1)S(1)}, bf16[1440,128]{1,0:T(8,128)(2,1)S(1)}, u32[]{:S(2)}, u32[]{:S(2)}) collective-permute-start(bf16[1440,128]{1,0:T(8,128)(2,1)S(1)} %collective-permute-done.32.refs_20_.refs_23_), channel_id=1, source_target_pairs={{0,30},{1,31},{2,0},{3,1},{4,2},{5,3},{6,4},{7,5},{8,6},{9,7},{10,... | collective-permute-start | bytes 1105928 | tf_op jit(solution)/shard_map/cond/branch_1_fun/ppermute | solution.py:533
  383.9 23.2 %collective-permute-start.25 = (bf16[1440,128]{1,0:T(8,128)(2,1)S(1)}, bf16[1440,128]{1,0:T(8,128)(2,1)S(1)}, u32[]{:S(2)}, u32[]{:S(2)}) collective-permute-start(bf16[1440,128]{1,0:T(8,128)(2,1)S(1)} %collective-permute-done.24.refs_17_.refs_20_), channel_id=1, source_target_pairs={{0,2},{1,3},{2,4},{3,5},{4,6},{5,7},{6,8},{7,9},{8,10},{9,11},{10,... | collective-permute-start | bytes 1105928 | tf_op jit(solution)/shard_map/cond/branch_1_fun/ppermute | solution.py:532
  387.8 24.4 %collective-permute-start.41 = (bf16[1440,128]{1,0:T(8,128)(2,1)}, bf16[1440,128]{1,0:T(8,128)(2,1)}, u32[]{:S(2)}, u32[]{:S(2)}) collective-permute-start(bf16[1440,128]{1,0:T(8,128)(2,1)} %collective-permute-done.40.refs_21_.refs_24_), channel_id=1, source_target_pairs={{0,30},{1,31},{2,0},{3,1},{4,2},{5,3},{6,4},{7,5},{8,6},{9,7},{10,... | collective-permute-start | bytes 1105928 | tf_op jit(solution)/shard_map/cond/branch_1_fun/ppermute | solution.py:533
  391.8 23.6 %collective-permute-start.17 = (bf16[1440,128]{1,0:T(8,128)(2,1)}, bf16[1440,128]{1,0:T(8,128)(2,1)}, u32[]{:S(2)}, u32[]{:S(2)}) collective-permute-start(bf16[1440,128]{1,0:T(8,128)(2,1)} %collective-permute-done.16.refs_16_.refs_19_), channel_id=1, source_target_pairs={{0,2},{1,3},{2,4},{3,5},{4,6},{5,7},{6,8},{7,9},{8,10},{9,11},{10,... | collective-permute-start | bytes 1105928 | tf_op jit(solution)/shard_map/cond/branch_1_fun/ppermute | solution.py:532
  395.8 24.1 %collective-permute-start.9 = (bf16[1440,128]{1,0:T(8,128)(2,1)}, bf16[1440,128]{1,0:T(8,128)(2,1)}, u32[]{:S(2)}, u32[]{:S(2)}) collective-permute-start(bf16[1440,128]{1,0:T(8,128)(2,1)} %collective-permute-done.8.refs_15_.refs_18_), channel_id=1, source_target_pairs={{0,2},{1,3},{2,4},{3,5},{4,6},{5,7},{6,8},{7,9},{8,10},{9,11},{10,... | collective-permute-start | bytes 1105928 | tf_op jit(solution)/shard_map/cond/branch_1_fun/ppermute | solution.py:532
  415.3 115.4 %collective-permute-start.115 = (bf16[2,7,1440,128]{3,2,1,0:T(8,128)(2,1)}, bf16[2,7,1440,128]{3,2,1,0:T(8,128)(2,1)}, u32[]{:S(2)}, u32[]{:S(2)}) collective-permute-start(bf16[2,7,1440,128]{3,2,1,0:T(8,128)(2,1)} %select.11), channel_id=1, source_target_pairs={{0,1},{1,0},{2,3},{3,2},{4,5},{5,4},{6,7},{7,6},{8,9},{9,8},{10,11... | collective-permute-start | bytes 15482888 | tf_op jit(solution)/shard_map/cond/branch_1_fun/ppermute | solution.py:487
  423.4 19.9 %collective-permute-start.42 = (bf16[1440,128]{1,0:T(8,128)(2,1)}, bf16[1440,128]{1,0:T(8,128)(2,1)S(1)}, u32[]{:S(2)}, u32[]{:S(2)}) collective-permute-start(bf16[1440,128]{1,0:T(8,128)(2,1)} %collective-permute-done.41.refs_28_.refs_31_), channel_id=1, source_target_pairs={{0,30},{1,31},{2,0},{3,1},{4,2},{5,3},{6,4},{7,5},{8,6},{9,7},{10,... | collective-permute-start | bytes 1105928 | tf_op jit(solution)/shard_map/cond/branch_1_fun/ppermute | solution.py:533
  479.2 83.4 %collective-permute-start.83 = (bf16[2,5,1440,128]{3,2,1,0:T(8,128)(2,1)}, bf16[2,5,1440,128]{3,2,1,0:T(8,128)(2,1)}, u32[]{:S(2)}, u32[]{:S(2)}) collective-permute-start(bf16[2,5,1440,128]{3,2,1,0:T(8,128)(2,1)} %select.9), channel_id=1, source_target_pairs={{0,1},{1,0},{2,3},{3,2},{4,5},{5,4},{6,7},{7,6},{8,9},{9,8},{10,11... | collective-permute-start | bytes 11059208 | tf_op jit(solution)/shard_map/cond/branch_1_fun/ppermute | solution.py:487
  528.7 19.2 %collective-permute-start.102 = (bf16[2,4,1440,128]{3,2,1,0:T(8,128)(2,1)}, bf16[2,4,1440,128]{3,2,1,0:T(8,128)(2,1)S(1)}, u32[]{:S(2)}, u32[]{:S(2)}) collective-permute-start(bf16[2,4,1440,128]{3,2,1,0:T(8,128)(2,1)} %select.10), channel_id=1, source_target_pairs={{0,1},{1,0},{2,3},{3,2},{4,5},{5,4},{6,7},{7,6},{8,9},{9,8},{10,11... | collective-permute-start | bytes 8847368 | tf_op jit(solution)/shard_map/cond/branch_1_fun/ppermute | solution.py:487
  (203 other events, 8506.5 us)

commit v2 on v1

--- a/solution.py
+++ b/solution.py
@@ -20,7 +20,7 @@
 JOBS = 2
 TPAD = 32
 PACKED = NACT * TPAD
-STEPS = 256
+STEPS = 152
 OFFSETS = range(-ABOVE, BELOW + 1)
 
 
@@ -28,7 +28,7 @@
     draw = np.random.default_rng(7)
     first = draw.integers(0, NBLK, STEPS)
     second = (first + draw.integers(1, NBLK, STEPS)) % NBLK
-    heat = 0.7 * (0.2 / 0.7) ** (np.arange(STEPS) / STEPS)
+    heat = 0.5 * (0.15 / 0.5) ** (np.arange(STEPS) / STEPS)
     heat[:24] = 4.0
     return (
         np.stack([first, second], axis=1).astype(np.int32).reshape(-1),
@@ -40,7 +40,7 @@
     return sum(1 << d for d in range(NBLK) if min(d, NBLK - d) in reach)
 
 
-def plan_kernel(me, pairs, swaps, coolness, table, words, links, home, load):
+def plan_kernel(me, pairs, swaps, coolness, table, words, links, home, load, spots, found, waiting, queue):
     far_base = ring_mask(range(BELOW + ABOVE + 1, NBLK))
     edge_base = ring_mask([BELOW + ABOVE])
     near_edge_base = ring_mask([BELOW + ABOVE - 1])
@@ -63,9 +63,8 @@
     def link(d, c):
         p = pairs[2 * d]
         q = pairs[2 * d + 1]
-        differ = jnp.where(p == q, 0, 1)
-        links[p] = links[p] | (differ << q)
-        links[q] = links[q] | (differ << p)
+        links[p] = links[p] | (1 << q)
+        links[q] = links[q] | (1 << p)
         return c
 
     lax.fori_loop(0, n_pairs, link, 0)
@@ -113,13 +112,31 @@
         return cost + change * take_bit, noise
 
     cost, noise = lax.fori_loop(0, STEPS, step, (cost, noise))
-    tight = jnp.zeros(shape, jnp.int32)
-    for z in range(NBLK):
-        w = words[z]
-        tight = tight + 2 * count(w & turned(edge_base, z)) + count(w & turned(near_edge_base, z))
-    score = jnp.minimum(cost * 512 + tight, 16000) * 1024 + lane
+    span_limit = BELOW + ABOVE
+    one = jnp.ones(shape, jnp.int32)
+
+    def lap(_, carry):
+        slack, late = list(carry[:-1]), carry[-1]
+        for chip in range(NBLK):
+            y = (chip + BELOW) % NBLK
+            for gap in range(span_limit + 1):
+                slack[span_limit - gap] = slack[span_limit - gap] + ((words[(y - gap) % NBLK] >> y) & one)
+            room = jnp.full(shape, CORES, jnp.int32)
+            for k in range(span_limit + 1):
+                served = jnp.minimum(slack[k], room)
+                slack[k] = slack[k] - served
+                room = room - served
+            late = late + slack[0]
+            slack = slack[1:] + [jnp.zeros(shape, jnp.int32)]
+        return (*slack, late)
+
+    nothing = jnp.zeros(shape, jnp.int32)
+    late = lax.fori_loop(0, 3, lap, (nothing,) * (span_limit + 2))[-1]
+    late = jnp.minimum(late, 1)
+    score = jnp.minimum(cost * 2 + late, 8000) * 1024 + lane
     best = jnp.min(score.astype(jnp.float32))
     chosen = score.astype(jnp.float32) == best
+    even = best < 1024.0
     for z in range(NBLK):
         w = jnp.sum(jnp.where(chosen, words[z].astype(jnp.float32), 0.0)).astype(jnp.int32)
         home[(w >> 16) & 15] = z
@@ -133,12 +150,12 @@
         low = jnp.where(forward, y, x) - BELOW
         return gap, low
 
-    def rank(r, unfit):
-        def place(d, unfit):
+    def rank(r, c):
+        def place(d, c):
             gap, low = span(d)
 
-            def choose(c, best_chip):
-                chip = (low + c) & (NBLK - 1)
+            def choose(step, best_chip):
+                chip = (low + step) & (NBLK - 1)
                 better = load[chip] < load[best_chip]
                 return jnp.where(better, chip, best_chip)
 
@@ -147,39 +164,109 @@
 
             @pl.when(now)
             def _():
-                turn = load[spot]
-                load[spot] = turn + 1
-                table[24 + d] = jnp.minimum((spot * CORES + turn % CORES) * JOBS + turn // CORES, n_pairs * JOBS - 1)
-                here = (spot == me[0] // CORES) & (turn < CORES * JOBS)
-
-                @pl.when(turn >= CORES)
-                def _():
-                    table[17] = 1
-
-                @pl.when(here)
-                def _():
-                    whose = jnp.where(turn % CORES == me[0] % CORES, MINE, OTHERS)
-                    slot = whose + 3 * (turn // CORES)
-                    table[slot] = 1
-                    table[slot + 1] = ((home[pairs[2 * d]] - spot + 8) & 15) - 8
-                    table[slot + 2] = ((home[pairs[2 * d + 1]] - spot + 8) & 15) - 8
-
-            full = now & (load[spot] > CORES * JOBS)
-            return unfit + jnp.where(full, 1, 0)
-
-        return lax.fori_loop(0, n_pairs, place, unfit)
+                load[spot] = load[spot] + 1
+                spots[d] = spot
+
+            return c
+
+        return lax.fori_loop(0, n_pairs, place, c)
+
+    @pl.when(jnp.logical_not(even))
+    def _():
+        lax.fori_loop(0, span_limit + 1, rank, 0)
+
+    def empty(i, c):
+        found[i] = -1
+        waiting[i] = 0
+        return c
+
+    def record(d, c):
+        x = home[pairs[2 * d]]
+        y = home[pairs[2 * d + 1]]
+        ahead = (y - x) & (NBLK - 1)
+        first = jnp.where(ahead <= NBLK // 2, x, y)
+        found[first * 8 + span(d)[0]] = d
+        return c
+
+    def serve(c, carry):
+        y = (c + BELOW) & (NBLK - 1)
+        for gap in range(span_limit + 1):
+            d = found[((y - gap) & (NBLK - 1)) * 8 + gap]
+            end = c + span_limit - gap
+
+            @pl.when(d >= 0)
+            def _(d=d, end=end):
+                queue[end * 8 + waiting[end]] = d
+                waiting[end] = waiting[end] + 1
+
+        def more(state):
+            end, room = state
+            return (room > 0) & (end <= c + span_limit)
+
+        def pop(state):
+            end, room = state
+            some = waiting[end] > 0
+
+            @pl.when(some)
+            def _():
+                last = waiting[end] - 1
+                spots[queue[end * 8 + last]] = c & (NBLK - 1)
+                waiting[end] = last
+
+            return jnp.where(some, end, end + 1), jnp.where(some, room - 1, room)
+
+        lax.while_loop(more, pop, (c, jnp.int32(CORES)))
+        return carry
+
+    @pl.when(even)
+    def _():
+        lax.fori_loop(0, NBLK * 8, empty, 0)
+        lax.fori_loop(0, n_pairs, record, 0)
+        lax.fori_loop(0, 3 * NBLK, serve, 0)
 
     for j in range(8 * JOBS):
         table[MINE + j] = 0
     table[17] = 0
 
-    def missed(d, c):
-        table[24 + d] = 0
-        return c + jnp.where(span(d)[0] > BELOW + ABOVE, 1, 0)
-
-    unfit = lax.fori_loop(0, n_pairs, missed, 0)
-    unfit = lax.fori_loop(0, BELOW + ABOVE + 1, rank, unfit)
+    def rest(z, c):
+        load[z] = 0
+        return c
+
+    lax.fori_loop(0, NBLK, rest, 0)
+
+    def settle(d, unfit):
+        spot = spots[d] & (NBLK - 1)
+        turn = load[spot]
+        load[spot] = turn + 1
+        table[24 + d] = jnp.minimum((spot * CORES + turn % CORES) * JOBS + turn // CORES, n_pairs * JOBS - 1)
+
+        @pl.when(turn >= CORES)
+        def _():
+            table[17] = 1
+
+        dp = ((home[pairs[2 * d]] - spot + 8) & 15) - 8
+        dq = ((home[pairs[2 * d + 1]] - spot + 8) & 15) - 8
+
+        @pl.when((spot == me[0] // CORES) & (turn < CORES * JOBS))
+        def _():
+            whose = jnp.where(turn % CORES == me[0] % CORES, MINE, OTHERS)
+            slot = whose + 3 * (turn // CORES)
+            table[slot] = 1
+            table[slot + 1] = dp
+            table[slot + 2] = dq
+
+        within = (dp >= -ABOVE) & (dp <= BELOW) & (dq >= -ABOVE) & (dq <= BELOW) & (turn < CORES * JOBS)
+        return unfit + jnp.where(within, 0, 1)
+
+    unfit = lax.fori_loop(0, n_pairs, settle, 0)
     table[0] = jnp.where(unfit == 0, 1, 0)
+
+    @pl.when(unfit > 0)
+    def _():
+        table[17] = 0
+        for j in range(8 * JOBS):
+            table[MINE + j] = 0
+
     for z in range(NBLK):
         table[1 + z] = home[z]
 
@@ -197,6 +284,10 @@
             pltpu.SMEM((NBLK,), jnp.int32),
             pltpu.SMEM((NBLK,), jnp.int32),
             pltpu.SMEM((NBLK,), jnp.int32),
+            pltpu.SMEM((pair_blocks.shape[0],), jnp.int32),
+            pltpu.SMEM((NBLK * 8,), jnp.int32),
+            pltpu.SMEM((NBLK * 8,), jnp.int32),
+            pltpu.SMEM((NBLK * 8 * 8,), jnp.int32),
         ],
         name="plan",
     )(me, pair_blocks.reshape(-1), jnp.asarray(swaps), jnp.asarray(coolness))
@@ -267,18 +358,31 @@
 OTHERS = 72
 
 
-def unflatten(refs, sources):
+def unflatten(refs, keys):
     refs = list(refs)
-    return [{d: refs.pop(0) for d in OFFSETS} for _ in sources]
-
-
-def flatten(pieces, sources):
-    return [pieces[s][d] for s in sources for d in OFFSETS]
-
-
-def select_kernel(table, *rest, sources, job):
-    count = len(sources) * len(OFFSETS)
-    pieces = unflatten(rest[:count], sources)
+    return [{d: refs.pop(0) for d in offsets} for offsets in keys]
+
+
+def flatten(pieces, keys, sources):
+    return [pieces[s][d] for s, offsets in zip(sources, keys) for d in offsets]
+
+
+def keys_of(pieces, sources):
+    return [sorted(pieces[s]) for s in sources]
+
+
+def held_here(wanted, offsets):
+    if len(offsets) == len(OFFSETS):
+        return None
+    here = wanted == min(offsets)
+    for d in sorted(offsets)[1:]:
+        here = here | (wanted == d)
+    return here
+
+
+def select_kernel(table, *rest, keys, sources, job):
+    count = sum(map(len, keys))
+    pieces = unflatten(rest[:count], keys)
     out, held, sems, out_sem = rest[count:]
 
     @pl.when(table[OTHERS + 3 * job] == 1)
@@ -293,19 +397,33 @@
                         pltpu.make_async_copy(piece, held.at[side, n], sems.at[side, n]).start()
 
         for side in range(2):
+            wanted = table[OTHERS + 3 * job + 1 + side]
             for n in range(len(sources)):
-                pltpu.make_async_copy(next(iter(pieces[n].values())), held.at[side, n], sems.at[side, n]).wait()
-                pltpu.make_async_copy(held.at[side, n], out.at[side, n], out_sem.at[side, n]).start()
+                here = held_here(wanted, pieces[n])
+                piece = next(iter(pieces[n].values()))
+
+                def pass_on(piece=piece, side=side, n=n):
+                    pltpu.make_async_copy(piece, held.at[side, n], sems.at[side, n]).wait()
+                    pltpu.make_async_copy(held.at[side, n], out.at[side, n], out_sem.at[side, n]).start()
+
+                pass_on() if here is None else pl.when(here)(pass_on)
         for side in range(2):
+            wanted = table[OTHERS + 3 * job + 1 + side]
             for n in range(len(sources)):
-                pltpu.make_async_copy(held.at[side, n], out.at[side, n], out_sem.at[side, n]).wait()
+                here = held_here(wanted, pieces[n])
+
+                def close(side=side, n=n):
+                    pltpu.make_async_copy(held.at[side, n], out.at[side, n], out_sem.at[side, n]).wait()
+
+                close() if here is None else pl.when(here)(close)
 
 
 def select(table, pieces, sources, job):
-    flat = flatten(pieces, sources)
+    keys = keys_of(pieces, sources)
+    flat = flatten(pieces, keys, sources)
     n = len(sources)
     return pl.pallas_call(
-        lambda *refs: select_kernel(*refs, sources=sources, job=job),
+        lambda *refs: select_kernel(*refs, keys=keys, sources=sources, job=job),
         in_specs=[pl.BlockSpec(memory_space=pltpu.SMEM)] + [pl.BlockSpec(memory_space=HBM)] * len(flat),
         out_specs=pl.BlockSpec(memory_space=HBM),
         out_shape=jax.ShapeDtypeStruct((2, n, WIDTH, LANES), jnp.bfloat16),
@@ -318,25 +436,33 @@
     )(table, *flat)
 
 
-def multiply(table, job, pieces, other, bufs, sems, acc, fresh):
+def multiply(table, job, pieces, other, late, bufs, sems, acc, fresh, ready=None):
     def lanes(n, who):
         return pl.ds((n * CORES + who) * LANES, LANES)
 
     for side, buf in enumerate(bufs):
         wanted = table[MINE + 3 * job + 1 + side]
         for n in range(len(pieces)):
-            pltpu.make_async_copy(other.at[side, n], buf.at[:, lanes(n, 1)], sems.at[side, n, 1]).start()
-            for d, piece in pieces[n].items():
-
-                @pl.when(wanted == d)
-                def _(piece=piece, n=n, side=side, buf=buf):
-                    pltpu.make_async_copy(piece, buf.at[:, lanes(n, 0)], sems.at[side, n, 0]).start()
+            sources = [(None, other.at[side, n], 1)] if not late[n] else []
+            if late[n]:
+                waits = held_here(wanted, late[n])
+                sources.append((jnp.logical_not(waits), other.at[side, n], 1))
+                sources += [(wanted == d, piece, 1) for d, piece in late[n].items()]
+            sources += [(wanted == d, piece, 0) for d, piece in pieces[n].items()]
+            for when, piece, who in sources:
+
+                def begin(piece=piece, n=n, side=side, buf=buf, who=who):
+                    pltpu.make_async_copy(piece, buf.at[:, lanes(n, who)], sems.at[side, n, who]).start()
+
+                begin() if when is None else pl.when(when)(begin)
 
     for side, buf in enumerate(bufs):
         for n in range(len(pieces)):
             for who in range(CORES):
                 pltpu.make_async_copy(other.at[side, n], buf.at[:, lanes(n, who)], sems.at[side, n, who]).wait()
     col_buf, row_buf = bufs
+    if ready is not None:
+        ready.wait()
 
     def rows(m, c):
         here = pl.ds(pl.multiple_of(m * ROW_TILE, ROW_TILE), ROW_TILE)
@@ -357,21 +483,22 @@
     lax.fori_loop(0, WIDTH // ROW_TILE, rows, 0)
 
 
-def early_kernel(table, other, *rest, sources, job, fresh):
+def early_kernel(table, other, *rest, keys, job, fresh):
     before = None
     if not fresh:
         before, *rest = rest
-    count = len(sources) * len(OFFSETS)
-    pieces = unflatten(rest[:count], sources)
+    count = sum(map(len, keys))
+    pieces = unflatten(rest[:count], keys)
     out, col_buf, row_buf, acc, sems, sem = rest[count:]
 
     @pl.when(table[MINE + 3 * job] == 1)
     def _():
+        ready = None
         if not fresh:
-            copy = pltpu.make_async_copy(before, acc, sem)
-            copy.start()
-            copy.wait()
-        multiply(table, job, pieces, other, (col_buf, row_buf), sems, acc, fresh)
+            ready = pltpu.make_async_copy(before, acc, sem)
+            ready.start()
+        late = [{} for _ in keys]
+        multiply(table, job, pieces, other, late, (col_buf, row_buf), sems, acc, fresh, ready)
         copy = pltpu.make_async_copy(acc, out, sem)
         copy.start()
         copy.wait()
@@ -397,9 +524,12 @@
     )(rdm)
 
 
-def finish_kernel(table, other, before, density, *rest, sources, job):
-    count = len(sources) * len(OFFSETS)
-    pieces = unflatten(rest[:count], sources)
+def finish_kernel(table, other, before, density, *rest, keys, late_keys, job):
+    count = sum(map(len, keys))
+    pieces = unflatten(rest[:count], keys)
+    rest = rest[count:]
+    count = sum(map(len, late_keys))
+    late = unflatten(rest[:count], late_keys)
     out, col_buf, row_buf, acc, spread, sems, sem = rest[count:]
 
     @pl.when(table[MINE + 3 * job] == 0)
@@ -411,8 +541,7 @@
         copy = pltpu.make_async_copy(before, acc.at[:, pl.ds(0, WIDTH), :], sem)
         copy.start()
         acc[:, WIDTH:, :] = jnp.zeros((TILES, acc.shape[1] - WIDTH, LANES), jnp.float32)
-        copy.wait()
-        multiply(table, job, pieces, other, (col_buf, row_buf), sems, acc, False)
+        multiply(table, job, pieces, other, late, (col_buf, row_buf), sems, acc, False, copy)
 
         def group(g, carry):
             for i in range(GROUP):
@@ -441,12 +570,13 @@
 
 
 def early(table, other, before, pieces, sources, job):
-    flat = flatten(pieces, sources)
+    keys = keys_of(pieces, sources)
+    flat = flatten(pieces, keys, sources)
     fresh = before is None
     held = [] if fresh else [before]
     in_hbm = pl.BlockSpec(memory_space=HBM)
     return pl.pallas_call(
-        lambda *refs: early_kernel(*refs, sources=sources, job=job, fresh=fresh),
+        lambda *refs: early_kernel(*refs, keys=keys, job=job, fresh=fresh),
         in_specs=[pl.BlockSpec(memory_space=pltpu.SMEM)] + [in_hbm] * (1 + len(held) + len(flat)),
         out_specs=in_hbm,
         out_shape=jax.ShapeDtypeStruct((TILES, WIDTH, LANES), jnp.float32),
@@ -457,11 +587,13 @@
     )(table, other, *held, *flat)
 
 
-def finish(table, other, before, density, pieces, sources, job):
-    flat = flatten(pieces, sources)
+def finish(table, other, before, density, pieces, late, sources, job):
+    keys = keys_of(pieces, sources)
+    late_keys = keys_of(late, sources)
+    flat = flatten(pieces, keys, sources) + flatten(late, late_keys, sources)
     in_hbm = pl.BlockSpec(memory_space=HBM)
     return pl.pallas_call(
-        lambda *refs: finish_kernel(*refs, sources=sources, job=job),
+        lambda *refs: finish_kernel(*refs, keys=keys, late_keys=late_keys, job=job),
         in_specs=[pl.BlockSpec(memory_space=pltpu.SMEM), in_hbm, in_hbm, pl.BlockSpec(memory_space=pltpu.VMEM)]
         + [in_hbm] * len(flat),
         out_specs=pl.BlockSpec(memory_space=pltpu.VMEM),
@@ -508,22 +640,41 @@
 FAR = sources_within(6, CHIPS)
 
 
+LAST_SELECTED = 8
+
+
+def both_cores(x):
+    core = lax.axis_index("aux") % CORES
+    other = to_other_core(x)
+    return jnp.where(core == 0, jnp.stack([x, other]), jnp.stack([other, x]))
+
+
+def of_everyone(x):
+    n = lax.axis_size("aux")
+    rings = [list(range(core, n, CORES)) for core in range(CORES)]
+    chips = lax.all_gather(both_cores(x), "aux", axis_index_groups=rings)
+    return chips.reshape(n, VBLK, VBLK)
+
+
 def planned(table, me, slabs, rdm, orbital_energy, pair_blocks):
     sent = pack(me, table, slabs)
     pieces = {s: {} for s in range(-CHIPS // 2, CHIPS // 2)}
-
-    def keep(source, offset, value):
+    late = {s: {} for s in range(-CHIPS // 2, CHIPS // 2)}
+
+    def keep(source, offset, value, hop):
+        source = (source + CHIPS // 2) % CHIPS - CHIPS // 2
         if -ABOVE <= offset <= BELOW:
-            pieces[(source + CHIPS // 2) % CHIPS - CHIPS // 2][offset] = value
+            pieces[source][offset] = value
+            if hop > LAST_SELECTED:
+                late[source][offset] = to_other_core(value)
 
     right = {reach: sent[reach - 1] for reach in range(1, LONGEST + 1)}
     left = {reach: sent[LONGEST + reach - 1] for reach in range(1, LONGEST + 1)}
     for offset in OFFSETS:
-        keep(0, offset, right[offset + ABOVE] if offset > -ABOVE else left[BELOW + ABOVE])
-    sums = None
-    density = None
-
-    def exchange(sources, job):
+        keep(0, offset, right[offset + ABOVE] if offset > -ABOVE else left[BELOW + ABOVE], 0)
+    none_late = {s: {} for s in pieces}
+
+    def exchange(pieces, sources, job):
         chosen = select(table, pieces, sources, job)
         return to_other_core(chosen)
 
@@ -531,29 +682,31 @@
         for reach in range(LONGEST, hop - 1, -1):
             right[reach] = lax.ppermute(right[reach], "aux", ring_shift(1))
             left[reach] = lax.ppermute(left[reach], "aux", ring_shift(-1))
-            keep(-hop, reach - ABOVE - hop, right[reach])
-            keep(hop, BELOW - reach + hop, left[reach])
+            keep(-hop, reach - ABOVE - hop, right[reach], hop)
+            keep(hop, BELOW - reach + hop, left[reach], hop)
         if hop == 1:
             density = spread_density(rdm)
         if hop == 3:
-            other = exchange(NEAREST, 0)
+            other = exchange(pieces, NEAREST, 0)
             sums = early(table, other, None, pieces, NEAREST, 0)
         if hop == 5:
-            other = exchange(NEAR, 0)
+            other = exchange(pieces, NEAR, 0)
             sums = early(table, other, sums, pieces, NEAR, 0)
-    other = exchange(FAR, 0)
-    paired = finish(table, other, sums, density, pieces, FAR, 0)
+        if hop == LAST_SELECTED:
+            other = exchange(pieces, FAR, 0)
+    paired = finish(table, other, sums, density, pieces, late, FAR, 0)
 
     def second_job(pieces):
-        other = exchange(NEAREST, 1)
+        other = exchange(pieces, NEAREST, 1)
         sums = early(table, other, None, pieces, NEAREST, 1)
-        other = exchange(NEAR, 1)
+        other = exchange(pieces, NEAR, 1)
         sums = early(table, other, sums, pieces, NEAR, 1)
-        other = exchange(FAR, 1)
-        return finish(table, other, sums, density, pieces, FAR, 1)
-
+        other = exchange(pieces, FAR, 1)
+        return of_everyone(finish(table, other, sums, density, pieces, none_late, FAR, 1))
+
+    paired = of_everyone(paired)
     extra = lax.cond(table[17] == 1, second_job, lambda pieces: jnp.zeros_like(paired), pieces)
-    everyone = lax.all_gather(jnp.stack([paired, extra]), "aux").reshape(-1, VBLK, VBLK)
+    everyone = jnp.stack([paired, extra], axis=1).reshape(-1, VBLK, VBLK)
     paired = everyone[lax.dynamic_slice_in_dim(table, 24, pair_blocks.shape[0])].transpose(0, 2, 1)
     return energies_of(paired, orbital_energy, pair_blocks)
 
@@ -581,7 +734,9 @@
 def per_device(slabs, rdm, orbital_energy, pair_blocks):
     me = lax.axis_index("aux").reshape(1).astype(jnp.int32)
     table = make_plan(me, pair_blocks)
-    return lax.cond(table[0] == 1, planned, unplanned, table, me, slabs, rdm, orbital_energy, pair_blocks)
+    given = (table, me, slabs, rdm, orbital_energy, pair_blocks)
+    results = planned(*given)
+    return lax.cond(table[0] == 1, lambda *_: results, unplanned, *given)
 
 
 def solution(mesh):

time: 678 us -> 619 us (0.913)
  the two profiles are of different devices: /device:TPU:69 before, /device:TPU:84 now
where the time goes in v2:
time: 619 us; the launch traced here: 610 us
  waiting for transfers between devices  298 us (48%)
  starting transfers between devices  158 us (26%)
  Pallas kernels  103 us (17%)
  blocking collectives  28.8 us (5%)
  local copies, waits for them, and re-layouts  7.92 us (1%)
  loops' own time  7.06 us (1%)
    ppermute x55, waiting for transfers between devices, planned(): right[reach] = lax.ppermute(right[reach], 'aux', ring_shift(1))  160 us
    ppermute x55, starting transfers between devices, planned(): left[reach] = lax.ppermute(left[reach], 'aux', ring_shift(-1))  148 us
    ppermute x55, waiting for transfers between devices, planned(): left[reach] = lax.ppermute(left[reach], 'aux', ring_shift(-1))  137 us
    pallas_call x2, Pallas kernels, early(): pl.pallas_call(lambda *refs: early_kernel(*refs, keys=keys, job=job, fres...  30.8 us
    all_gather x1, blocking collectives, of_everyone(): chips = lax.all_gather(both_cores(x), 'aux', axis_index_groups=rings)  28.8 us
    pallas_call x1, Pallas kernels, finish(): pl.pallas_call(lambda *refs: finish_kernel(*refs, keys=keys, late_keys=la...  22.6 us
    pallas_call x1, Pallas kernels, make_plan(): pl.pallas_call(plan_kernel, out_shape=jax.ShapeDtypeStruct((96,), jnp.int...  17.8 us
    pallas_call x3, Pallas kernels, select(): pl.pallas_call(lambda *refs: select_kernel(*refs, keys=keys, sources=sour...  12.8 us
  transfers between devices with their start and end apart: 120, of which 85 were waited for; matrix products, arithmetic and copies ran while one was open for 0% of the time, Pallas kernels for 8%

profile of v2, /device:TPU:84, one launch (start us, length us, event | category | flops | bytes accessed | tf_op | source)
XLA Modules:
  0.0 610.1 jit_solution(3132227551377552739)
XLA Ops:
  2.0 17.8 %plan.1.table.refs_0_ = s32[96]{0:T(128)S(1)} custom-call(s32[1]{0:T(128)} %bitcast.24.me, s32[64]{0:T(128)} %reshape.191.pairs, s32[304]{0:T(512)} %constant.102.clone.swaps, f32[152]{0:T(256)} %constant.103.clone.coolness), custom_call_target="tpu_custom_call" | custom-call | tf_op jit(solution)/shard_map/plan/pallas_call | solution.py:277
  19.8 11.4 %pack.1 = (bf16[1440,128]{1,0:T(8,128)(2,1)S(1)}, bf16[1440,128]{1,0:T(8,128)(2,1)S(1)}, bf16[1440,128]{1,0:T(8,128)(2,1)S(1)}, bf16[1440,128]{1,0:T(8,128)(2,1)...) custom-call(s32[1]{0:T(128)} %bitcast.24.me, ...), custom_call_target="tpu_custom_call" | custom-call | tf_op jit(solution)/shard_map/pack/pallas_call | solution.py:336
  35.6 8.5 %collective-permute-start.88 = (bf16[1440,128]{1,0:T(8,128)(2,1)S(1)}, bf16[1440,128]{1,0:T(8,128)(2,1)S(1)}, u32[]{:S(2)}, u32[]{:S(2)}) collective-permute-start(bf16[1440,128]{1,0:T(8,128)(2,1)S(1)} %get-tuple-element.416.refs_19_.refs_20_), channel_id=1, source_target_pairs={{0,30},{1,31},{2,0},{3,1},{4,2},{5,3},{6,4},{7,5},{8,6},{9,7},{10,... | collective-permute-start | bytes 1105928 | tf_op jit(solution)/shard_map/ppermute | solution.py:684
  44.2 9.2 %collective-permute-done.79.refs_17_.refs_18_ = bf16[1440,128]{1,0:T(8,128)(2,1)S(1)} collective-permute-done((bf16[1440,128]{1,0:T(8,128)(2,1)S(1)}, bf16[1440,128]{1,0:T(8,128)(2,1)S(1)}, u32[]{:S(2)}, u32[]{:S(2)}) %collective-permute-start.79) | collective-permute-done | bytes 368672 | tf_op jit(solution)/shard_map/ppermute | solution.py:683
  55.4 5.9 collective-permute-done.84.refs_16_.refs_17_
  64.1 5.1 collective-permute-done.98.refs_15_.refs_16_
  69.2 7.9 %collective-permute-done.59.refs_18_.refs_19_ = bf16[1440,128]{1,0:T(8,128)(2,1)S(1)} collective-permute-done((bf16[1440,128]{1,0:T(8,128)(2,1)S(1)}, bf16[1440,128]{1,0:T(8,128)(2,1)S(1)}, u32[]{:S(2)}, u32[]{:S(2)}) %collective-permute-start.59) | collective-permute-done | bytes 368672 | tf_op jit(solution)/shard_map/ppermute | solution.py:683
  87.0 5.9 collective-permute-done.52
  116.6 4.3 collective-permute-done.36
  120.9 3.7 collective-permute-start.89
  124.6 4.2 collective-permute-done.28
  134.4 5.9 collective-permute-done.85.refs_9_.refs_10_
  143.2 5.0 collective-permute-done.99.refs_8_.refs_9_
  148.2 7.9 %collective-permute-done.60.refs_11_.refs_12_ = bf16[1440,128]{1,0:T(8,128)(2,1)S(1)} collective-permute-done((bf16[1440,128]{1,0:T(8,128)(2,1)S(1)}, bf16[1440,128]{1,0:T(8,128)(2,1)S(1)}, u32[]{:S(2)}, u32[]{:S(2)}) %collective-permute-start.60) | collective-permute-done | bytes 368672 | tf_op jit(solution)/shard_map/ppermute | solution.py:683
  164.0 7.9 %collective-permute-done.53.refs_12_.refs_13_ = bf16[1440,128]{1,0:T(8,128)(2,1)S(1)} collective-permute-done((bf16[1440,128]{1,0:T(8,128)(2,1)S(1)}, bf16[1440,128]{1,0:T(8,128)(2,1)S(1)}, u32[]{:S(2)}, u32[]{:S(2)}) %collective-permute-start.53) | collective-permute-done | bytes 368672 | tf_op jit(solution)/shard_map/ppermute | solution.py:683
  176.3 7.9 %collective-permute-done.45 = bf16[1440,128]{1,0:T(8,128)(2,1)S(1)} collective-permute-done((bf16[1440,128]{1,0:T(8,128)(2,1)S(1)}, bf16[1440,128]{1,0:T(8,128)(2,1)S(1)}, u32[]{:S(2)}, u32[]{:S(2)}) %collective-permute-start.45) | collective-permute-done | bytes 368672 | tf_op jit(solution)/shard_map/ppermute | solution.py:684
  184.2 3.7 collective-permute-start.29
  188.1 4.1 collective-permute-done.37
  192.1 3.7 collective-permute-start.90
  195.8 4.2 collective-permute-done.29
  205.5 5.9 collective-permute-done.86.refs_2_.refs_3_
  214.3 5.0 collective-permute-done.100.refs_1_.refs_2_
  219.3 7.9 %collective-permute-done.61.refs_4_.refs_5_ = bf16[1440,128]{1,0:T(8,128)(2,1)S(1)} collective-permute-done((bf16[1440,128]{1,0:T(8,128)(2,1)S(1)}, bf16[1440,128]{1,0:T(8,128)(2,1)S(1)}, u32[]{:S(2)}, u32[]{:S(2)}) %collective-permute-start.61) | collective-permute-done | bytes 368672 | tf_op jit(solution)/shard_map/ppermute | solution.py:683
  238.7 7.9 %collective-permute-done.46.refs_37_.refs_38_ = bf16[1440,128]{1,0:T(8,128)(2,1)S(1)} collective-permute-done((bf16[1440,128]{1,0:T(8,128)(2,1)S(1)}, bf16[1440,128]{1,0:T(8,128)(2,1)S(1)}, u32[]{:S(2)}, u32[]{:S(2)}) %collective-permute-start.46) | collective-permute-done | bytes 368672 | tf_op jit(solution)/shard_map/ppermute | solution.py:684
  254.4 4.4 collective-permute-done.22
  262.3 4.4 collective-permute-done.82.refs_8_.refs_10_
  278.2 4.4 collective-permute-done.55.refs_10_.refs_12_
  286.1 7.9 %collective-permute-done.47.refs_14_.refs_16_ = bf16[1440,128]{1,0:T(8,128)(2,1)S(1)} collective-permute-done((bf16[1440,128]{1,0:T(8,128)(2,1)S(1)}, bf16[1440,128]{1,0:T(8,128)(2,1)S(1)}, u32[]{:S(2)}, u32[]{:S(2)}) %collective-permute-start.47) | collective-permute-done | bytes 368672 | tf_op jit(solution)/shard_map/ppermute | solution.py:684
  301.8 4.4 collective-permute-done.23
  317.8 4.3 collective-permute-done.56.refs_3_.refs_5_
  325.6 7.9 %collective-permute-done.48.refs_21_.refs_23_ = bf16[1440,128]{1,0:T(8,128)(2,1)S(1)} collective-permute-done((bf16[1440,128]{1,0:T(8,128)(2,1)S(1)}, bf16[1440,128]{1,0:T(8,128)(2,1)S(1)}, u32[]{:S(2)}, u32[]{:S(2)}) %collective-permute-start.48) | collective-permute-done | bytes 368672 | tf_op jit(solution)/shard_map/ppermute | solution.py:684
  341.5 4.4 collective-permute-done.24.refs_6_.refs_8_
  349.2 4.4 collective-permute-done.9.refs_13_.refs_18_
  357.1 4.4 collective-permute-done.57.refs_12_.refs_17_
  365.8 5.0 select.15
  448.3 4.6 select.13
  461.6 3.8 collective-permute-start.111
  465.4 8.7 %collective-permute-done.111.refs_14_ = bf16[1440,128]{1,0:T(8,128)(2,1)} collective-permute-done((bf16[1440,128]{1,0:T(8,128)(2,1)}, bf16[1440,128]{1,0:T(8,128)(2,1)}, u32[]{:S(2)}, u32[]{:S(2)}) %collective-permute-start.111) | collective-permute-done | bytes 368672 | tf_op jit(solution)/shard_map/ppermute | solution.py:684
  474.1 3.7 collective-permute-start.112
  477.8 7.8 %collective-permute-done.112.refs_15_ = bf16[1440,128]{1,0:T(8,128)(2,1)S(1)} collective-permute-done((bf16[1440,128]{1,0:T(8,128)(2,1)}, bf16[1440,128]{1,0:T(8,128)(2,1)S(1)}, u32[]{:S(2)}, u32[]{:S(2)}) %collective-permute-start.112) | collective-permute-done | bytes 368672 | tf_op jit(solution)/shard_map/ppermute | solution.py:684
  489.3 7.0 %collective-permute-done.113.refs_21_ = bf16[1440,128]{1,0:T(8,128)(2,1)} collective-permute-done((bf16[1440,128]{1,0:T(8,128)(2,1)}, bf16[1440,128]{1,0:T(8,128)(2,1)}, u32[]{:S(2)}, u32[]{:S(2)}) %collective-permute-start.113) | collective-permute-done | bytes 368672 | tf_op jit(solution)/shard_map/ppermute | solution.py:684
  502.8 7.9 %density.1.refs_3_ = bf16[960,960]{1,0:T(8,128)(2,1)} custom-call(bf16[900,900]{1,0:T(8,128)(2,1)} %rdm.1), custom_call_target="tpu_custom_call" | custom-call | tf_op jit(solution)/shard_map/density/pallas_call | solution.py:519
  511.5 17.4 %early.6.refs_2_ = f32[12,1440,128]{2,1,0:T(8,128)} custom-call(s32[96]{0:T(128)S(1)} %plan.1.table.refs_0_, bf16[2,7,1440,128]{3,2,1,0:T(8,128)(2,1)} %collective-permute-done.110.refs_1_, bf16[1440,128]{1,0:T(8,128)(2,1)} %copy-done.46, bf16[1440,128]{1,0:T(8,128)(2,1)} %copy-done.44, bf16[1440,128]{1,0:T(8,128)(2,1)} %copy-done.43, ...), custom_call_target="tpu_custom_call" | custom-call | tf_op jit(solution)/shard_map/early/pallas_call | solution.py:578
  529.1 13.4 %early.7.refs_2_ = f32[12,1440,128]{2,1,0:T(8,128)} custom-call(s32[96]{0:T(128)S(1)} %plan.1.table.refs_0_, bf16[2,4,1440,128]{3,2,1,0:T(8,128)(2,1)S(1)} %collective-permute-done.97.refs_1_, f32[12,1440,128]{2,1,0:T(8,128)} %early.6.refs_2_, bf16[1440,128]{1,0:T(8,128)(2,1)} %collective-permute-done.83.refs_1_.refs_3_, ...), custom_call_target="tpu_custom_call" | custom-call | tf_op jit(solution)/shard_map/early/pallas_call | solution.py:578
  542.6 22.6 %finish.3 = f32[6,384]{1,0:T(8,128)S(1)} custom-call(s32[96]{0:T(128)S(1)} %plan.1.table.refs_0_, bf16[2,5,1440,128]{3,2,1,0:T(8,128)(2,1)} %collective-permute-done.78.refs_1_, f32[12,1440,128]{2,1,0:T(8,128)} %early.7.refs_2_, bf16[960,960]{1,0:T(8,128)(2,1)S(1)} %copy-done.2, bf16[1440,128]{1,0:T(8,128)(2,1)} %copy-done.143, ...), custom_call_target="tpu_custom_call" | custom-call | tf_op jit(solution)/shard_map/finish/pallas_call | solution.py:595
  567.0 4.9 conditional.2
  572.0 28.8 %all_gather.11 = f32[16,2,6,384]{3,1,2,0:T(2,128)S(1)} all-gather(f32[1,2,6,384]{3,1,2,0:T(2,128)S(1)} %copy.23), channel_id=1, replica_groups={{0,2,4,6,8,10,12,14,16,18,20,22,24,26,28,30},{1,3,5,7,9,11,13,15,17,19,..., dimensions={0}, use_global_device_ids=true | all-gather | bytes 313344 | tf_op jit(solution)/shard_map/all_gather | solution.py:655
  603.2 5.5 conditional.3
  (456 shorter events, 256.2 us)
Async XLA Ops:
  31.3 22.1 %collective-permute-start.79 = (bf16[1440,128]{1,0:T(8,128)(2,1)S(1)}, bf16[1440,128]{1,0:T(8,128)(2,1)S(1)}, u32[]{:S(2)}, u32[]{:S(2)}) collective-permute-start(bf16[1440,128]{1,0:T(8,128)(2,1)S(1)} %get-tuple-element.414.refs_24_.refs_25_), channel_id=1, source_target_pairs={{0,2},{1,3},{2,4},{3,5},{4,6},{5,7},{6,8},{7,9},{8,10},{9,11},{10,... | collective-permute-start | bytes 1105928 | tf_op jit(solution)/shard_map/ppermute | solution.py:683
  33.5 27.8 %collective-permute-start.84 = (bf16[1440,128]{1,0:T(8,128)(2,1)S(1)}, bf16[1440,128]{1,0:T(8,128)(2,1)S(1)}, u32[]{:S(2)}, u32[]{:S(2)}) collective-permute-start(bf16[1440,128]{1,0:T(8,128)(2,1)S(1)} %get-tuple-element.415.refs_23_.refs_24_), channel_id=1, source_target_pairs={{0,2},{1,3},{2,4},{3,5},{4,6},{5,7},{6,8},{7,9},{8,10},{9,11},{10,... | collective-permute-start | bytes 1105928 | tf_op jit(solution)/shard_map/ppermute | solution.py:683
  35.6 27.7 %collective-permute-start.88 = (bf16[1440,128]{1,0:T(8,128)(2,1)S(1)}, bf16[1440,128]{1,0:T(8,128)(2,1)S(1)}, u32[]{:S(2)}, u32[]{:S(2)}) collective-permute-start(bf16[1440,128]{1,0:T(8,128)(2,1)S(1)} %get-tuple-element.416.refs_19_.refs_20_), channel_id=1, source_target_pairs={{0,30},{1,31},{2,0},{3,1},{4,2},{5,3},{6,4},{7,5},{8,6},{9,7},{10,... | collective-permute-start | bytes 1105928 | tf_op jit(solution)/shard_map/ppermute | solution.py:684
  44.2 25.0 %collective-permute-start.98 = (bf16[1440,128]{1,0:T(8,128)(2,1)S(1)}, bf16[1440,128]{1,0:T(8,128)(2,1)S(1)}, u32[]{:S(2)}, u32[]{:S(2)}) collective-permute-start(bf16[1440,128]{1,0:T(8,128)(2,1)S(1)} %get-tuple-element.418.refs_22_.refs_23_), channel_id=1, source_target_pairs={{0,2},{1,3},{2,4},{3,5},{4,6},{5,7},{6,8},{7,9},{8,10},{9,11},{10,... | collective-permute-start | bytes 1105928 | tf_op jit(solution)/shard_map/ppermute | solution.py:683
  44.2 32.9 %collective-permute-start.59 = (bf16[1440,128]{1,0:T(8,128)(2,1)S(1)}, bf16[1440,128]{1,0:T(8,128)(2,1)S(1)}, u32[]{:S(2)}, u32[]{:S(2)}) collective-permute-start(bf16[1440,128]{1,0:T(8,128)(2,1)S(1)} %get-tuple-element.411), channel_id=1, source_target_pairs={{0,2},{1,3},{2,4},{3,5},{4,6},{5,7},{6,8},{7,9},{8,10},{9,11},{10,... | collective-permute-start | bytes 1105928 | tf_op jit(solution)/shard_map/ppermute | solution.py:683
  53.4 23.7 %collective-permute-start.71 = (bf16[1440,128]{1,0:T(8,128)(2,1)S(1)}, bf16[1440,128]{1,0:T(8,128)(2,1)S(1)}, u32[]{:S(2)}, u32[]{:S(2)}) collective-permute-start(bf16[1440,128]{1,0:T(8,128)(2,1)S(1)} %get-tuple-element.413), channel_id=1, source_target_pairs={{0,30},{1,31},{2,0},{3,1},{4,2},{5,3},{6,4},{7,5},{8,6},{9,7},{10,... | collective-permute-start | bytes 1105928 | tf_op jit(solution)/shard_map/ppermute | solution.py:684
  81.1 19.6 %collective-permute-start.103 = (bf16[1440,128]{1,0:T(8,128)(2,1)S(1)}, bf16[1440,128]{1,0:T(8,128)(2,1)S(1)}, u32[]{:S(2)}, u32[]{:S(2)}) collective-permute-start(bf16[1440,128]{1,0:T(8,128)(2,1)S(1)} %get-tuple-element.420.refs_20_.refs_21_), channel_id=1, source_target_pairs={{0,2},{1,3},{2,4},{3,5},{4,6},{5,7},{6,8},{7,9},{8,10},{9,11},{10,... | collective-permute-start | bytes 1105928 | tf_op jit(solution)/shard_map/ppermute | solution.py:683
  85.0 20.1 %collective-permute-start.44 = (bf16[1440,128]{1,0:T(8,128)(2,1)S(1)}, bf16[1440,128]{1,0:T(8,128)(2,1)S(1)}, u32[]{:S(2)}, u32[]{:S(2)}) collective-permute-start(bf16[1440,128]{1,0:T(8,128)(2,1)S(1)} %get-tuple-element.409), channel_id=1, source_target_pairs={{0,30},{1,31},{2,0},{3,1},{4,2},{5,3},{6,4},{7,5},{8,6},{9,7},{10,... | collective-permute-start | bytes 1105928 | tf_op jit(solution)/shard_map/ppermute | solution.py:684
  92.9 20.1 %collective-permute-start.106 = (bf16[1440,128]{1,0:T(8,128)(2,1)S(1)}, bf16[1440,128]{1,0:T(8,128)(2,1)S(1)}, u32[]{:S(2)}, u32[]{:S(2)}) collective-permute-start(bf16[1440,128]{1,0:T(8,128)(2,1)S(1)} %get-tuple-element.423), channel_id=1, source_target_pairs={{0,30},{1,31},{2,0},{3,1},{4,2},{5,3},{6,4},{7,5},{8,6},{9,7},{10,... | collective-permute-start | bytes 1105928 | tf_op jit(solution)/shard_map/ppermute | solution.py:684
  100.8 20.1 %collective-permute-start.36 = (bf16[1440,128]{1,0:T(8,128)(2,1)S(1)}, bf16[1440,128]{1,0:T(8,128)(2,1)S(1)}, u32[]{:S(2)}, u32[]{:S(2)}) collective-permute-start(bf16[1440,128]{1,0:T(8,128)(2,1)S(1)} %get-tuple-element.408), channel_id=1, source_target_pairs={{0,30},{1,31},{2,0},{3,1},{4,2},{5,3},{6,4},{7,5},{8,6},{9,7},{10,... | collective-permute-start | bytes 1105928 | tf_op jit(solution)/shard_map/ppermute | solution.py:684
  108.7 20.1 %collective-permute-start.28 = (bf16[1440,128]{1,0:T(8,128)(2,1)S(1)}, bf16[1440,128]{1,0:T(8,128)(2,1)S(1)}, u32[]{:S(2)}, u32[]{:S(2)}) collective-permute-start(bf16[1440,128]{1,0:T(8,128)(2,1)S(1)} %get-tuple-element.407), channel_id=1, source_target_pairs={{0,30},{1,31},{2,0},{3,1},{4,2},{5,3},{6,4},{7,5},{8,6},{9,7},{10,... | collective-permute-start | bytes 1105928 | tf_op jit(solution)/shard_map/ppermute | solution.py:684
  116.6 23.7 %collective-permute-start.85 = (bf16[1440,128]{1,0:T(8,128)(2,1)S(1)}, bf16[1440,128]{1,0:T(8,128)(2,1)S(1)}, u32[]{:S(2)}, u32[]{:S(2)}) collective-permute-start(bf16[1440,128]{1,0:T(8,128)(2,1)S(1)} %collective-permute-done.84.refs_16_.refs_17_), channel_id=1, source_target_pairs={{0,2},{1,3},{2,4},{3,5},{4,6},{5,7},{6,8},{7,9},{8,10},{9,11},{10,... | collective-permute-start | bytes 1105928 | tf_op jit(solution)/shard_map/ppermute | solution.py:683
  120.9 21.4 %collective-permute-start.89 = (bf16[1440,128]{1,0:T(8,128)(2,1)S(1)}, bf16[1440,128]{1,0:T(8,128)(2,1)S(1)}, u32[]{:S(2)}, u32[]{:S(2)}) collective-permute-start(bf16[1440,128]{1,0:T(8,128)(2,1)S(1)} %collective-permute-done.88.refs_26_.refs_27_), channel_id=1, source_target_pairs={{0,30},{1,31},{2,0},{3,1},{4,2},{5,3},{6,4},{7,5},{8,6},{9,7},{10,... | collective-permute-start | bytes 1105928 | tf_op jit(solution)/shard_map/ppermute | solution.py:684
  124.6 23.6 %collective-permute-start.99 = (bf16[1440,128]{1,0:T(8,128)(2,1)S(1)}, bf16[1440,128]{1,0:T(8,128)(2,1)S(1)}, u32[]{:S(2)}, u32[]{:S(2)}) collective-permute-start(bf16[1440,128]{1,0:T(8,128)(2,1)S(1)} %collective-permute-done.98.refs_15_.refs_16_), channel_id=1, source_target_pairs={{0,2},{1,3},{2,4},{3,5},{4,6},{5,7},{6,8},{7,9},{8,10},{9,11},{10,... | collective-permute-start | bytes 1105928 | tf_op jit(solution)/shard_map/ppermute | solution.py:683
  128.8 27.3 %collective-permute-start.60 = (bf16[1440,128]{1,0:T(8,128)(2,1)S(1)}, bf16[1440,128]{1,0:T(8,128)(2,1)S(1)}, u32[]{:S(2)}, u32[]{:S(2)}) collective-permute-start(bf16[1440,128]{1,0:T(8,128)(2,1)S(1)} %collective-permute-done.59.refs_18_.refs_19_), channel_id=1, source_target_pairs={{0,2},{1,3},{2,4},{3,5},{4,6},{5,7},{6,8},{7,9},{8,10},{9,11},{10,... | collective-permute-start | bytes 1105928 | tf_op jit(solution)/shard_map/ppermute | solution.py:683
  132.4 23.7 %collective-permute-start.72 = (bf16[1440,128]{1,0:T(8,128)(2,1)S(1)}, bf16[1440,128]{1,0:T(8,128)(2,1)S(1)}, u32[]{:S(2)}, u32[]{:S(2)}) collective-permute-start(bf16[1440,128]{1,0:T(8,128)(2,1)S(1)} %collective-permute-done.71.refs_25_.refs_26_), channel_id=1, source_target_pairs={{0,30},{1,31},{2,0},{3,1},{4,2},{5,3},{6,4},{7,5},{8,6},{9,7},{10,... | collective-permute-start | bytes 1105928 | tf_op jit(solution)/shard_map/ppermute | solution.py:684
  160.3 23.9 %collective-permute-start.45 = (bf16[1440,128]{1,0:T(8,128)(2,1)S(1)}, bf16[1440,128]{1,0:T(8,128)(2,1)S(1)}, u32[]{:S(2)}, u32[]{:S(2)}) collective-permute-start(bf16[1440,128]{1,0:T(8,128)(2,1)S(1)} %collective-permute-done.44), channel_id=1, source_target_pairs={{0,30},{1,31},{2,0},{3,1},{4,2},{5,3},{6,4},{7,5},{8,6},{9,7},{10,... | collective-permute-start | bytes 1105928 | tf_op jit(solution)/shard_map/ppermute | solution.py:684
  164.0 23.9 %collective-permute-start.5 = (bf16[1440,128]{1,0:T(8,128)(2,1)S(1)}, bf16[1440,128]{1,0:T(8,128)(2,1)S(1)}, u32[]{:S(2)}, u32[]{:S(2)}) collective-permute-start(bf16[1440,128]{1,0:T(8,128)(2,1)S(1)} %collective-permute-done.4), channel_id=1, source_target_pairs={{0,2},{1,3},{2,4},{3,5},{4,6},{5,7},{6,8},{7,9},{8,10},{9,11},{10,... | collective-permute-start | bytes 1105928 | tf_op jit(solution)/shard_map/ppermute | solution.py:683
  171.9 20.2 %collective-permute-start.37 = (bf16[1440,128]{1,0:T(8,128)(2,1)S(1)}, bf16[1440,128]{1,0:T(8,128)(2,1)S(1)}, u32[]{:S(2)}, u32[]{:S(2)}) collective-permute-start(bf16[1440,128]{1,0:T(8,128)(2,1)S(1)} %collective-permute-done.36), channel_id=1, source_target_pairs={{0,30},{1,31},{2,0},{3,1},{4,2},{5,3},{6,4},{7,5},{8,6},{9,7},{10,... | collective-permute-start | bytes 1105928 | tf_op jit(solution)/shard_map/ppermute | solution.py:684
  187.9 23.5 %collective-permute-start.86 = (bf16[1440,128]{1,0:T(8,128)(2,1)S(1)}, bf16[1440,128]{1,0:T(8,128)(2,1)S(1)}, u32[]{:S(2)}, u32[]{:S(2)}) collective-permute-start(bf16[1440,128]{1,0:T(8,128)(2,1)S(1)} %collective-permute-done.85.refs_9_.refs_10_), channel_id=1, source_target_pairs={{0,2},{1,3},{2,4},{3,5},{4,6},{5,7},{6,8},{7,9},{8,10},{9,11},{10,... | collective-permute-start | bytes 1105928 | tf_op jit(solution)/shard_map/ppermute | solution.py:683
  192.1 21.3 %collective-permute-start.90 = (bf16[1440,128]{1,0:T(8,128)(2,1)S(1)}, bf16[1440,128]{1,0:T(8,128)(2,1)S(1)}, u32[]{:S(2)}, u32[]{:S(2)}) collective-permute-start(bf16[1440,128]{1,0:T(8,128)(2,1)S(1)} %collective-permute-done.89.refs_33_.refs_34_), channel_id=1, source_target_pairs={{0,30},{1,31},{2,0},{3,1},{4,2},{5,3},{6,4},{7,5},{8,6},{9,7},{10,... | collective-permute-start | bytes 1105928 | tf_op jit(solution)/shard_map/ppermute | solution.py:684
  195.8 23.5 %collective-permute-start.100 = (bf16[1440,128]{1,0:T(8,128)(2,1)S(1)}, bf16[1440,128]{1,0:T(8,128)(2,1)S(1)}, u32[]{:S(2)}, u32[]{:S(2)}) collective-permute-start(bf16[1440,128]{1,0:T(8,128)(2,1)S(1)} %collective-permute-done.99.refs_8_.refs_9_), channel_id=1, source_target_pairs={{0,2},{1,3},{2,4},{3,5},{4,6},{5,7},{6,8},{7,9},{8,10},{9,11},{10,... | collective-permute-start | bytes 1105928 | tf_op jit(solution)/shard_map/ppermute | solution.py:683
  200.0 27.2 %collective-permute-start.61 = (bf16[1440,128]{1,0:T(8,128)(2,1)S(1)}, bf16[1440,128]{1,0:T(8,128)(2,1)S(1)}, u32[]{:S(2)}, u32[]{:S(2)}) collective-permute-start(bf16[1440,128]{1,0:T(8,128)(2,1)S(1)} %collective-permute-done.60.refs_11_.refs_12_), channel_id=1, source_target_pairs={{0,2},{1,3},{2,4},{3,5},{4,6},{5,7},{6,8},{7,9},{8,10},{9,11},{10,... | collective-permute-start | bytes 1105928 | tf_op jit(solution)/shard_map/ppermute | solution.py:683
  203.5 25.7 %collective-permute-start.73 = (bf16[1440,128]{1,0:T(8,128)(2,1)S(1)}, bf16[1440,128]{1,0:T(8,128)(2,1)S(1)}, u32[]{:S(2)}, u32[]{:S(2)}) collective-permute-start(bf16[1440,128]{1,0:T(8,128)(2,1)S(1)} %collective-permute-done.72.refs_32_.refs_33_), channel_id=1, source_target_pairs={{0,30},{1,31},{2,0},{3,1},{4,2},{5,3},{6,4},{7,5},{8,6},{9,7},{10,... | collective-permute-start | bytes 1105928 | tf_op jit(solution)/shard_map/ppermute | solution.py:684
  230.3 19.7 %collective-permute-start.6 = (bf16[1440,128]{1,0:T(8,128)(2,1)S(1)}, bf16[1440,128]{1,0:T(8,128)(2,1)S(1)}, u32[]{:S(2)}, u32[]{:S(2)}) collective-permute-start(bf16[1440,128]{1,0:T(8,128)(2,1)S(1)} %collective-permute-done.5), channel_id=1, source_target_pairs={{0,2},{1,3},{2,4},{3,5},{4,6},{5,7},{6,8},{7,9},{8,10},{9,11},{10,... | collective-permute-start | bytes 1105928 | tf_op jit(solution)/shard_map/ppermute | solution.py:683
  238.7 20.2 %collective-permute-start.22 = (bf16[1440,128]{1,0:T(8,128)(2,1)S(1)}, bf16[1440,128]{1,0:T(8,128)(2,1)S(1)}, u32[]{:S(2)}, u32[]{:S(2)}) collective-permute-start(bf16[1440,128]{1,0:T(8,128)(2,1)S(1)} %collective-permute-done.21), channel_id=1, source_target_pairs={{0,2},{1,3},{2,4},{3,5},{4,6},{5,7},{6,8},{7,9},{8,10},{9,11},{10,... | collective-permute-start | bytes 1105928 | tf_op jit(solution)/shard_map/ppermute | solution.py:683
  254.4 20.2 %collective-permute-start.62 = (bf16[1440,128]{1,0:T(8,128)(2,1)S(1)}, bf16[1440,128]{1,0:T(8,128)(2,1)S(1)}, u32[]{:S(2)}, u32[]{:S(2)}) collective-permute-start(bf16[1440,128]{1,0:T(8,128)(2,1)S(1)} %collective-permute-done.61.refs_4_.refs_5_), channel_id=1, source_target_pairs={{0,2},{1,3},{2,4},{3,5},{4,6},{5,7},{6,8},{7,9},{8,10},{9,11},{10,... | collective-permute-start | bytes 1105928 | tf_op jit(solution)/shard_map/ppermute | solution.py:683
  262.3 20.2 %collective-permute-start.55 = (bf16[1440,128]{1,0:T(8,128)(2,1)S(1)}, bf16[1440,128]{1,0:T(8,128)(2,1)S(1)}, u32[]{:S(2)}, u32[]{:S(2)}) collective-permute-start(bf16[1440,128]{1,0:T(8,128)(2,1)S(1)} %collective-permute-done.54.refs_5_.refs_6_), channel_id=1, source_target_pairs={{0,2},{1,3},{2,4},{3,5},{4,6},{5,7},{6,8},{7,9},{8,10},{9,11},{10,... | collective-permute-start | bytes 1105928 | tf_op jit(solution)/shard_map/ppermute | solution.py:683
  270.2 23.7 %collective-permute-start.47 = (bf16[1440,128]{1,0:T(8,128)(2,1)S(1)}, bf16[1440,128]{1,0:T(8,128)(2,1)S(1)}, u32[]{:S(2)}, u32[]{:S(2)}) collective-permute-start(bf16[1440,128]{1,0:T(8,128)(2,1)S(1)} %collective-permute-done.46.refs_37_.refs_38_), channel_id=1, source_target_pairs={{0,30},{1,31},{2,0},{3,1},{4,2},{5,3},{6,4},{7,5},{8,6},{9,7},{10,... | collective-permute-start | bytes 1105928 | tf_op jit(solution)/shard_map/ppermute | solution.py:684
  274.7 22.8 %collective-permute-start.7 = (bf16[1440,128]{1,0:T(8,128)(2,1)S(1)}, bf16[1440,128]{1,0:T(8,128)(2,1)S(1)}, u32[]{:S(2)}, u32[]{:S(2)}) collective-permute-start(bf16[1440,128]{1,0:T(8,128)(2,1)S(1)} %collective-permute-done.6.refs_6_.refs_7_), channel_id=1, source_target_pairs={{0,2},{1,3},{2,4},{3,5},{4,6},{5,7},{6,8},{7,9},{8,10},{9,11},{10,... | collective-permute-start | bytes 1105928 | tf_op jit(solution)/shard_map/ppermute | solution.py:683
  278.1 20.2 %collective-permute-start.15 = (bf16[1440,128]{1,0:T(8,128)(2,1)S(1)}, bf16[1440,128]{1,0:T(8,128)(2,1)S(1)}, u32[]{:S(2)}, u32[]{:S(2)}) collective-permute-start(bf16[1440,128]{1,0:T(8,128)(2,1)S(1)} %collective-permute-done.14), channel_id=1, source_target_pairs={{0,2},{1,3},{2,4},{3,5},{4,6},{5,7},{6,8},{7,9},{8,10},{9,11},{10,... | collective-permute-start | bytes 1105928 | tf_op jit(solution)/shard_map/ppermute | solution.py:683
  286.0 20.2 %collective-permute-start.23 = (bf16[1440,128]{1,0:T(8,128)(2,1)S(1)}, bf16[1440,128]{1,0:T(8,128)(2,1)S(1)}, u32[]{:S(2)}, u32[]{:S(2)}) collective-permute-start(bf16[1440,128]{1,0:T(8,128)(2,1)S(1)} %collective-permute-done.22), channel_id=1, source_target_pairs={{0,2},{1,3},{2,4},{3,5},{4,6},{5,7},{6,8},{7,9},{8,10},{9,11},{10,... | collective-permute-start | bytes 1105928 | tf_op jit(solution)/shard_map/ppermute | solution.py:683
  301.8 20.2 %collective-permute-start.56 = (bf16[1440,128]{1,0:T(8,128)(2,1)S(1)}, bf16[1440,128]{1,0:T(8,128)(2,1)S(1)}, u32[]{:S(2)}, u32[]{:S(2)}) collective-permute-start(bf16[1440,128]{1,0:T(8,128)(2,1)S(1)} %collective-permute-done.55.refs_10_.refs_12_), channel_id=1, source_target_pairs={{0,2},{1,3},{2,4},{3,5},{4,6},{5,7},{6,8},{7,9},{8,10},{9,11},{10,... | collective-permute-start | bytes 1105928 | tf_op jit(solution)/shard_map/ppermute | solution.py:683
  309.7 23.7 %collective-permute-start.48 = (bf16[1440,128]{1,0:T(8,128)(2,1)S(1)}, bf16[1440,128]{1,0:T(8,128)(2,1)S(1)}, u32[]{:S(2)}, u32[]{:S(2)}) collective-permute-start(bf16[1440,128]{1,0:T(8,128)(2,1)S(1)} %collective-permute-done.47.refs_14_.refs_16_), channel_id=1, source_target_pairs={{0,30},{1,31},{2,0},{3,1},{4,2},{5,3},{6,4},{7,5},{8,6},{9,7},{10,... | collective-permute-start | bytes 1105928 | tf_op jit(solution)/shard_map/ppermute | solution.py:684
  314.3 22.7 %collective-permute-start.8 = (bf16[1440,128]{1,0:T(8,128)(2,1)S(1)}, bf16[1440,128]{1,0:T(8,128)(2,1)S(1)}, u32[]{:S(2)}, u32[]{:S(2)}) collective-permute-start(bf16[1440,128]{1,0:T(8,128)(2,1)S(1)} %collective-permute-done.7.refs_11_.refs_13_), channel_id=1, source_target_pairs={{0,2},{1,3},{2,4},{3,5},{4,6},{5,7},{6,8},{7,9},{8,10},{9,11},{10,... | collective-permute-start | bytes 1105928 | tf_op jit(solution)/shard_map/ppermute | solution.py:683
  317.8 20.2 %collective-permute-start.16 = (bf16[1440,128]{1,0:T(8,128)(2,1)S(1)}, bf16[1440,128]{1,0:T(8,128)(2,1)}, u32[]{:S(2)}, u32[]{:S(2)}) collective-permute-start(bf16[1440,128]{1,0:T(8,128)(2,1)S(1)} %collective-permute-done.15.refs_12_.refs_14_), channel_id=1, source_target_pairs={{0,2},{1,3},{2,4},{3,5},{4,6},{5,7},{6,8},{7,9},{8,10},{9,11},{10,... | collective-permute-start | bytes 1105928 | tf_op jit(solution)/shard_map/ppermute | solution.py:683
  325.5 20.3 %collective-permute-start.24 = (bf16[1440,128]{1,0:T(8,128)(2,1)S(1)}, bf16[1440,128]{1,0:T(8,128)(2,1)}, u32[]{:S(2)}, u32[]{:S(2)}) collective-permute-start(bf16[1440,128]{1,0:T(8,128)(2,1)S(1)} %collective-permute-done.23), channel_id=1, source_target_pairs={{0,2},{1,3},{2,4},{3,5},{4,6},{5,7},{6,8},{7,9},{8,10},{9,11},{10,... | collective-permute-start | bytes 1105928 | tf_op jit(solution)/shard_map/ppermute | solution.py:683
  341.5 20.1 %collective-permute-start.57 = (bf16[1440,128]{1,0:T(8,128)(2,1)S(1)}, bf16[1440,128]{1,0:T(8,128)(2,1)S(1)}, u32[]{:S(2)}, u32[]{:S(2)}) collective-permute-start(bf16[1440,128]{1,0:T(8,128)(2,1)S(1)} %collective-permute-done.56.refs_3_.refs_5_), channel_id=1, source_target_pairs={{0,2},{1,3},{2,4},{3,5},{4,6},{5,7},{6,8},{7,9},{8,10},{9,11},{10,... | collective-permute-start | bytes 1105928 | tf_op jit(solution)/shard_map/ppermute | solution.py:683
  349.2 21.7 %collective-permute-start.64 = (bf16[1440,128]{1,0:T(8,128)(2,1)}, bf16[1440,128]{1,0:T(8,128)(2,1)}, u32[]{:S(2)}, u32[]{:S(2)}) collective-permute-start(bf16[1440,128]{1,0:T(8,128)(2,1)} %collective-permute-done.63.refs_2_.refs_4_), channel_id=1, source_target_pairs={{0,2},{1,3},{2,4},{3,5},{4,6},{5,7},{6,8},{7,9},{8,10},{9,11},{10,... | collective-permute-start | bytes 1105928 | tf_op jit(solution)/shard_map/ppermute | solution.py:683
  357.1 20.3 %collective-permute-start.17 = (bf16[1440,128]{1,0:T(8,128)(2,1)}, bf16[1440,128]{1,0:T(8,128)(2,1)}, u32[]{:S(2)}, u32[]{:S(2)}) collective-permute-start(bf16[1440,128]{1,0:T(8,128)(2,1)} %collective-permute-done.16.refs_5_.refs_7_), channel_id=1, source_target_pairs={{0,2},{1,3},{2,4},{3,5},{4,6},{5,7},{6,8},{7,9},{8,10},{9,11},{10,... | collective-permute-start | bytes 1105928 | tf_op jit(solution)/shard_map/ppermute | solution.py:683
  371.0 131.6 %collective-permute-start.110 = (bf16[2,7,1440,128]{3,2,1,0:T(8,128)(2,1)}, bf16[2,7,1440,128]{3,2,1,0:T(8,128)(2,1)}, u32[]{:S(2)}, u32[]{:S(2)}) collective-permute-start(bf16[2,7,1440,128]{3,2,1,0:T(8,128)(2,1)} %select.15), channel_id=1, source_target_pairs={{0,1},{1,0},{2,3},{3,2},{4,5},{5,4},{6,7},{7,6},{8,9},{9,8},{10,11... | collective-permute-start | bytes 15482888 | tf_op jit(solution)/shard_map/ppermute | solution.py:619
  432.7 20.2 %collective-permute-start.87 = (bf16[1440,128]{1,0:T(8,128)(2,1)}, bf16[1440,128]{1,0:T(8,128)(2,1)}, u32[]{:S(2)}, u32[]{:S(2)}) collective-permute-start(bf16[1440,128]{1,0:T(8,128)(2,1)} %copy-done.44), channel_id=1, source_target_pairs={{0,2},{1,3},{2,4},{3,5},{4,6},{5,7},{6,8},{7,9},{8,10},{9,11},{10,... | collective-permute-start | bytes 1105928 | tf_op jit(solution)/shard_map/ppermute | solution.py:683
  452.9 89.7 %collective-permute-start.78 = (bf16[2,5,1440,128]{3,2,1,0:T(8,128)(2,1)}, bf16[2,5,1440,128]{3,2,1,0:T(8,128)(2,1)}, u32[]{:S(2)}, u32[]{:S(2)}) collective-permute-start(bf16[2,5,1440,128]{3,2,1,0:T(8,128)(2,1)} %select.13), channel_id=1, source_target_pairs={{0,1},{1,0},{2,3},{3,2},{4,5},{5,4},{6,7},{7,6},{8,9},{9,8},{10,11... | collective-permute-start | bytes 11059208 | tf_op jit(solution)/shard_map/ppermute | solution.py:619
  461.5 40.8 %collective-permute-start.97 = (bf16[2,4,1440,128]{3,2,1,0:T(8,128)(2,1)}, bf16[2,4,1440,128]{3,2,1,0:T(8,128)(2,1)S(1)}, u32[]{:S(2)}, u32[]{:S(2)}) collective-permute-start(bf16[2,4,1440,128]{3,2,1,0:T(8,128)(2,1)} %select.14), channel_id=1, source_target_pairs={{0,1},{1,0},{2,3},{3,2},{4,5},{5,4},{6,7},{7,6},{8,9},{9,8},{10,11... | collective-permute-start | bytes 8847368 | tf_op jit(solution)/shard_map/ppermute | solution.py:619
  499.7 42.8 %collective-permute-start.117 = (bf16[1440,128]{1,0:T(8,128)(2,1)}, bf16[1440,128]{1,0:T(8,128)(2,1)}, u32[]{:S(2)}, u32[]{:S(2)}) collective-permute-start(bf16[1440,128]{1,0:T(8,128)(2,1)} %collective-permute-done.111.refs_14_), channel_id=1, source_target_pairs={{0,1},{1,0},{2,3},{3,2},{4,5},{5,4},{6,7},{7,6},{8,9},{9,8},{10,11... | collective-permute-start | bytes 1105928 | tf_op jit(solution)/shard_map/ppermute | solution.py:619
  502.1 40.4 %collective-permute-start.122 = (bf16[1440,128]{1,0:T(8,128)(2,1)}, bf16[1440,128]{1,0:T(8,128)(2,1)}, u32[]{:S(2)}, u32[]{:S(2)}) collective-permute-start(bf16[1440,128]{1,0:T(8,128)(2,1)} %collective-permute-done.114.refs_29_), channel_id=1, source_target_pairs={{0,1},{1,0},{2,3},{3,2},{4,5},{5,4},{6,7},{7,6},{8,9},{9,8},{10,11... | collective-permute-start | bytes 1105928 | tf_op jit(solution)/shard_map/ppermute | solution.py:619
  502.2 40.3 %collective-permute-start.119 = (bf16[1440,128]{1,0:T(8,128)(2,1)}, bf16[1440,128]{1,0:T(8,128)(2,1)}, u32[]{:S(2)}, u32[]{:S(2)}) collective-permute-start(bf16[1440,128]{1,0:T(8,128)(2,1)} %collective-permute-done.113.refs_21_), channel_id=1, source_target_pairs={{0,1},{1,0},{2,3},{3,2},{4,5},{5,4},{6,7},{7,6},{8,9},{9,8},{10,11... | collective-permute-start | bytes 1105928 | tf_op jit(solution)/shard_map/ppermute | solution.py:619
  502.6 39.9 %collective-permute-start.120 = (bf16[1440,128]{1,0:T(8,128)(2,1)}, bf16[1440,128]{1,0:T(8,128)(2,1)}, u32[]{:S(2)}, u32[]{:S(2)}) collective-permute-start(bf16[1440,128]{1,0:T(8,128)(2,1)} %collective-permute-done.115.refs_22_), channel_id=1, source_target_pairs={{0,1},{1,0},{2,3},{3,2},{4,5},{5,4},{6,7},{7,6},{8,9},{9,8},{10,11... | collective-permute-start | bytes 1105928 | tf_op jit(solution)/shard_map/ppermute | solution.py:619
  (187 other events, 8215.3 us)

commit v3 on v2

--- a/solution.py
+++ b/solution.py
@@ -20,7 +20,7 @@
 JOBS = 2
 TPAD = 32
 PACKED = NACT * TPAD
-STEPS = 152
+STEPS = 144
 OFFSETS = range(-ABOVE, BELOW + 1)
 
 
@@ -29,7 +29,7 @@
     first = draw.integers(0, NBLK, STEPS)
     second = (first + draw.integers(1, NBLK, STEPS)) % NBLK
     heat = 0.5 * (0.15 / 0.5) ** (np.arange(STEPS) / STEPS)
-    heat[:24] = 4.0
+    heat[:12] = 4.0
     return (
         np.stack([first, second], axis=1).astype(np.int32).reshape(-1),
         (1.0 / heat).astype(np.float32),
@@ -436,7 +436,7 @@
     )(table, *flat)
 
 
-def multiply(table, job, pieces, other, late, bufs, sems, acc, fresh, ready=None):
+def multiply(table, job, pieces, other, late, bufs, sems, acc, fresh, ready=None, meanwhile=None):
     def lanes(n, who):
         return pl.ds((n * CORES + who) * LANES, LANES)
 
@@ -456,6 +456,8 @@
 
                 begin() if when is None else pl.when(when)(begin)
 
+    if meanwhile is not None:
+        meanwhile()
     for side, buf in enumerate(bufs):
         for n in range(len(pieces)):
             for who in range(CORES):
@@ -530,7 +532,7 @@
     rest = rest[count:]
     count = sum(map(len, late_keys))
     late = unflatten(rest[:count], late_keys)
-    out, col_buf, row_buf, acc, spread, sems, sem = rest[count:]
+    out, col_buf, row_buf, acc, prior, spread, sems, sem = rest[count:]
 
     @pl.when(table[MINE + 3 * job] == 0)
     def _():
@@ -538,15 +540,21 @@
 
     @pl.when(table[MINE + 3 * job] == 1)
     def _():
-        copy = pltpu.make_async_copy(before, acc.at[:, pl.ds(0, WIDTH), :], sem)
-        copy.start()
-        acc[:, WIDTH:, :] = jnp.zeros((TILES, acc.shape[1] - WIDTH, LANES), jnp.float32)
-        multiply(table, job, pieces, other, late, (col_buf, row_buf), sems, acc, False, copy)
+        copy = pltpu.make_async_copy(before, prior.at[:, pl.ds(0, WIDTH), :], sem)
+
+        def while_fetching():
+            copy.start()
+            for sums in (acc, prior):
+                sums[:, WIDTH:, :] = jnp.zeros((TILES, sums.shape[1] - WIDTH, LANES), jnp.float32)
+
+        multiply(table, job, pieces, other, late, (col_buf, row_buf), sems, acc, True, None, while_fetching)
+        copy.wait()
 
         def group(g, carry):
             for i in range(GROUP):
                 here = pl.ds(g * GROUP + i, TPAD, stride=VBLK)
-                rows = jnp.concatenate([acc[c, here, :] for c in range(TILES)], axis=1).astype(jnp.bfloat16)
+                rows = [acc[c, here, :] + prior[c, here, :] for c in range(TILES)]
+                rows = jnp.concatenate(rows, axis=1).astype(jnp.bfloat16)
                 for t in range(NACT):
                     spread[t * TPAD : (t + 1) * TPAD, i * VBLK : (i + 1) * VBLK] = rows[:, t * VBLK : (t + 1) * VBLK]
             x = spread[...]
@@ -600,6 +608,7 @@
         out_shape=jax.ShapeDtypeStruct((VBLK // GROUP, GROUP * VBLK), jnp.float32),
         scratch_shapes=product_scratch(sources, VBLK * TPAD)
         + [
+            pltpu.VMEM((TILES, VBLK * TPAD, LANES), jnp.float32),
             pltpu.VMEM((PACKED, GROUP * VBLK), jnp.bfloat16),
             pltpu.SemaphoreType.DMA((2, len(sources), CORES)),
             pltpu.SemaphoreType.DMA,
@@ -696,22 +705,32 @@
             other = exchange(pieces, FAR, 0)
     paired = finish(table, other, sums, density, pieces, late, FAR, 0)
 
-    def second_job(pieces):
+    def from_everyone(everyone, places):
+        return energies_of(everyone[places].transpose(0, 2, 1), orbital_energy, pair_blocks)
+
+    places = lax.dynamic_slice_in_dim(table, 24, pair_blocks.shape[0])
+    everyone = of_everyone(paired)
+
+    def with_second_job():
         other = exchange(pieces, NEAREST, 1)
         sums = early(table, other, None, pieces, NEAREST, 1)
         other = exchange(pieces, NEAR, 1)
         sums = early(table, other, sums, pieces, NEAR, 1)
         other = exchange(pieces, FAR, 1)
-        return of_everyone(finish(table, other, sums, density, pieces, none_late, FAR, 1))
-
-    paired = of_everyone(paired)
-    extra = lax.cond(table[17] == 1, second_job, lambda pieces: jnp.zeros_like(paired), pieces)
-    everyone = jnp.stack([paired, extra], axis=1).reshape(-1, VBLK, VBLK)
-    paired = everyone[lax.dynamic_slice_in_dim(table, 24, pair_blocks.shape[0])].transpose(0, 2, 1)
-    return energies_of(paired, orbital_energy, pair_blocks)
-
-
-def unplanned(table, me, slabs, rdm, orbital_energy, pair_blocks):
+        extra = of_everyone(finish(table, other, sums, density, pieces, none_late, FAR, 1))
+        return from_everyone(jnp.stack([everyone, extra], axis=1).reshape(-1, VBLK, VBLK), places)
+
+    return lax.switch(
+        jnp.where(table[0] == 1, 1 + table[17], 0),
+        (
+            lambda: unplanned(rdm, slabs, orbital_energy, pair_blocks),
+            lambda: from_everyone(everyone, places // JOBS),
+            with_second_job,
+        ),
+    )
+
+
+def unplanned(rdm, slabs, orbital_energy, pair_blocks):
     local_rows = slabs.shape[0]
     blocked = slabs.reshape(local_rows, NBLK, WIDTH)
     sides = []
@@ -734,9 +753,7 @@
 def per_device(slabs, rdm, orbital_energy, pair_blocks):
     me = lax.axis_index("aux").reshape(1).astype(jnp.int32)
     table = make_plan(me, pair_blocks)
-    given = (table, me, slabs, rdm, orbital_energy, pair_blocks)
-    results = planned(*given)
-    return lax.cond(table[0] == 1, lambda *_: results, unplanned, *given)
+    return planned(table, me, slabs, rdm, orbital_energy, pair_blocks)
 
 
 def solution(mesh):

time: 619 us -> 623 us (level)
  the two profiles are of different devices: /device:TPU:84 before, /device:TPU:196 now
where the time goes in v3:
time: 623 us; the launch traced here: 614 us
  waiting for transfers between devices  239 us (38%)
  starting transfers between devices  216 us (35%)
  Pallas kernels  103 us (17%)
  blocking collectives  30.9 us (5%)
  loops' own time  11.3 us (2%)
  local copies, waits for them, and re-layouts  7.57 us (1%)
    ppermute x55, starting transfers between devices, planned(): left[reach] = lax.ppermute(left[reach], 'aux', ring_shift(-1))  199 us
    ppermute x55, waiting for transfers between devices, planned(): left[reach] = lax.ppermute(left[reach], 'aux', ring_shift(-1))  129 us
    ppermute x55, waiting for transfers between devices, planned(): right[reach] = lax.ppermute(right[reach], 'aux', ring_shift(1))  109 us
    pallas_call x2, Pallas kernels, early(): pl.pallas_call(lambda *refs: early_kernel(*refs, keys=keys, job=job, fres...  31.4 us
    all_gather x1, blocking collectives, of_everyone(): chips = lax.all_gather(both_cores(x), 'aux', axis_index_groups=rings)  30.9 us
    pallas_call x1, Pallas kernels, finish(): pl.pallas_call(lambda *refs: finish_kernel(*refs, keys=keys, late_keys=la...  24.8 us
    pallas_call x1, Pallas kernels, make_plan(): pl.pallas_call(plan_kernel, out_shape=jax.ShapeDtypeStruct((96,), jnp.int...  16.9 us
    ppermute x55, starting transfers between devices, planned(): right[reach] = lax.ppermute(right[reach], 'aux', ring_shift(1))  15.2 us
  transfers between devices with their start and end apart: 120, of which 82 were waited for; matrix products, arithmetic and copies ran while one was open for 0% of the time, Pallas kernels for 8%

profile of v3, /device:TPU:196, one launch (start us, length us, event | category | flops | bytes accessed | tf_op | source)
XLA Modules:
  0.0 613.8 jit_solution(11920660762838732565)
XLA Ops:
  2.0 16.9 %plan.1.table.refs_0_ = s32[96]{0:T(128)S(1)} custom-call(s32[1]{0:T(128)} %bitcast.32.me, s32[64]{0:T(128)} %reshape.207.pairs, s32[288]{0:T(512)} %constant.130.clone.swaps, f32[144]{0:T(256)} %constant.131.clone.coolness), custom_call_target="tpu_custom_call" | custom-call | tf_op jit(solution)/shard_map/plan/pallas_call | solution.py:277
  19.0 11.4 %pack.1 = (bf16[1440,128]{1,0:T(8,128)(2,1)S(1)}, bf16[1440,128]{1,0:T(8,128)(2,1)S(1)}, bf16[1440,128]{1,0:T(8,128)(2,1)S(1)}, bf16[1440,128]{1,0:T(8,128)(2,1)...) custom-call(s32[1]{0:T(128)} %bitcast.32.me, ...), custom_call_target="tpu_custom_call" | custom-call | tf_op jit(solution)/shard_map/pack/pallas_call | solution.py:336
  34.8 4.4 collective-permute-start.88
  40.3 5.8 collective-permute-done.79.refs_17_.refs_18_
  46.1 6.4 %collective-permute-start.71 = (bf16[1440,128]{1,0:T(8,128)(2,1)S(1)}, bf16[1440,128]{1,0:T(8,128)(2,1)S(1)}, u32[]{:S(2)}, u32[]{:S(2)}) collective-permute-start(bf16[1440,128]{1,0:T(8,128)(2,1)S(1)} %get-tuple-element.363), channel_id=1, source_target_pairs={{0,30},{1,31},{2,0},{3,1},{4,2},{5,3},{6,4},{7,5},{8,6},{9,7},{10,... | collective-permute-start | bytes 1105928 | tf_op jit(solution)/shard_map/ppermute | solution.py:693
  54.0 6.4 %collective-permute-start.92 = (bf16[1440,128]{1,0:T(8,128)(2,1)S(1)}, bf16[1440,128]{1,0:T(8,128)(2,1)S(1)}, u32[]{:S(2)}, u32[]{:S(2)}) collective-permute-start(bf16[1440,128]{1,0:T(8,128)(2,1)S(1)} %get-tuple-element.367), channel_id=1, source_target_pairs={{0,30},{1,31},{2,0},{3,1},{4,2},{5,3},{6,4},{7,5},{8,6},{9,7},{10,... | collective-permute-start | bytes 1105928 | tf_op jit(solution)/shard_map/ppermute | solution.py:693
  67.9 8.4 %collective-permute-start.65 = (bf16[1440,128]{1,0:T(8,128)(2,1)S(1)}, bf16[1440,128]{1,0:T(8,128)(2,1)S(1)}, u32[]{:S(2)}, u32[]{:S(2)}) collective-permute-start(bf16[1440,128]{1,0:T(8,128)(2,1)S(1)} %get-tuple-element.362), channel_id=1, source_target_pairs={{0,30},{1,31},{2,0},{3,1},{4,2},{5,3},{6,4},{7,5},{8,6},{9,7},{10,... | collective-permute-start | bytes 1105928 | tf_op jit(solution)/shard_map/ppermute | solution.py:693
  79.4 4.6 collective-permute-start.44
  85.6 6.4 %collective-permute-start.106 = (bf16[1440,128]{1,0:T(8,128)(2,1)S(1)}, bf16[1440,128]{1,0:T(8,128)(2,1)S(1)}, u32[]{:S(2)}, u32[]{:S(2)}) collective-permute-start(bf16[1440,128]{1,0:T(8,128)(2,1)S(1)} %get-tuple-element.373), channel_id=1, source_target_pairs={{0,30},{1,31},{2,0},{3,1},{4,2},{5,3},{6,4},{7,5},{8,6},{9,7},{10,... | collective-permute-start | bytes 1105928 | tf_op jit(solution)/shard_map/ppermute | solution.py:693
  93.2 6.7 %collective-permute-start.36 = (bf16[1440,128]{1,0:T(8,128)(2,1)S(1)}, bf16[1440,128]{1,0:T(8,128)(2,1)S(1)}, u32[]{:S(2)}, u32[]{:S(2)}) collective-permute-start(bf16[1440,128]{1,0:T(8,128)(2,1)S(1)} %get-tuple-element.358), channel_id=1, source_target_pairs={{0,30},{1,31},{2,0},{3,1},{4,2},{5,3},{6,4},{7,5},{8,6},{9,7},{10,... | collective-permute-start | bytes 1105928 | tf_op jit(solution)/shard_map/ppermute | solution.py:693
  101.4 6.5 %collective-permute-start.28 = (bf16[1440,128]{1,0:T(8,128)(2,1)S(1)}, bf16[1440,128]{1,0:T(8,128)(2,1)S(1)}, u32[]{:S(2)}, u32[]{:S(2)}) collective-permute-start(bf16[1440,128]{1,0:T(8,128)(2,1)S(1)} %get-tuple-element.357), channel_id=1, source_target_pairs={{0,30},{1,31},{2,0},{3,1},{4,2},{5,3},{6,4},{7,5},{8,6},{9,7},{10,... | collective-permute-start | bytes 1105928 | tf_op jit(solution)/shard_map/ppermute | solution.py:693
  110.9 6.0 collective-permute-done.36
  120.0 4.8 collective-permute-done.28
  125.1 6.4 %collective-permute-start.72 = (bf16[1440,128]{1,0:T(8,128)(2,1)S(1)}, bf16[1440,128]{1,0:T(8,128)(2,1)S(1)}, u32[]{:S(2)}, u32[]{:S(2)}) collective-permute-start(bf16[1440,128]{1,0:T(8,128)(2,1)S(1)} %collective-permute-done.71.refs_25_.refs_26_), channel_id=1, source_target_pairs={{0,30},{1,31},{2,0},{3,1},{4,2},{5,3},{6,4},{7,5},{8,6},{9,7},{10,... | collective-permute-start | bytes 1105928 | tf_op jit(solution)/shard_map/ppermute | solution.py:693
  133.0 6.4 %collective-permute-start.93 = (bf16[1440,128]{1,0:T(8,128)(2,1)S(1)}, bf16[1440,128]{1,0:T(8,128)(2,1)S(1)}, u32[]{:S(2)}, u32[]{:S(2)}) collective-permute-start(bf16[1440,128]{1,0:T(8,128)(2,1)S(1)} %collective-permute-done.92.refs_27_.refs_28_), channel_id=1, source_target_pairs={{0,30},{1,31},{2,0},{3,1},{4,2},{5,3},{6,4},{7,5},{8,6},{9,7},{10,... | collective-permute-start | bytes 1105928 | tf_op jit(solution)/shard_map/ppermute | solution.py:693
  141.6 5.0 collective-permute-done.60.refs_11_.refs_12_
  146.9 8.4 %collective-permute-start.66 = (bf16[1440,128]{1,0:T(8,128)(2,1)S(1)}, bf16[1440,128]{1,0:T(8,128)(2,1)S(1)}, u32[]{:S(2)}, u32[]{:S(2)}) collective-permute-start(bf16[1440,128]{1,0:T(8,128)(2,1)S(1)} %collective-permute-done.65), channel_id=1, source_target_pairs={{0,30},{1,31},{2,0},{3,1},{4,2},{5,3},{6,4},{7,5},{8,6},{9,7},{10,... | collective-permute-start | bytes 1105928 | tf_op jit(solution)/shard_map/ppermute | solution.py:693
  164.3 6.8 %collective-permute-start.37 = (bf16[1440,128]{1,0:T(8,128)(2,1)S(1)}, bf16[1440,128]{1,0:T(8,128)(2,1)S(1)}, u32[]{:S(2)}, u32[]{:S(2)}) collective-permute-start(bf16[1440,128]{1,0:T(8,128)(2,1)S(1)} %collective-permute-done.36), channel_id=1, source_target_pairs={{0,30},{1,31},{2,0},{3,1},{4,2},{5,3},{6,4},{7,5},{8,6},{9,7},{10,... | collective-permute-start | bytes 1105928 | tf_op jit(solution)/shard_map/ppermute | solution.py:693
  172.2 7.9 %collective-permute-done.45 = bf16[1440,128]{1,0:T(8,128)(2,1)S(1)} collective-permute-done((bf16[1440,128]{1,0:T(8,128)(2,1)S(1)}, bf16[1440,128]{1,0:T(8,128)(2,1)S(1)}, u32[]{:S(2)}, u32[]{:S(2)}) %collective-permute-start.45) | collective-permute-done | bytes 368672 | tf_op jit(solution)/shard_map/ppermute | solution.py:693
  183.4 4.5 collective-permute-done.37
  191.2 4.7 collective-permute-done.29
  196.4 6.1 collective-permute-start.73
  204.3 6.1 collective-permute-start.94
  212.7 5.0 collective-permute-done.61.refs_4_.refs_5_
  217.8 8.5 %collective-permute-start.67 = (bf16[1440,128]{1,0:T(8,128)(2,1)S(1)}, bf16[1440,128]{1,0:T(8,128)(2,1)S(1)}, u32[]{:S(2)}, u32[]{:S(2)}) collective-permute-start(bf16[1440,128]{1,0:T(8,128)(2,1)S(1)} %collective-permute-done.66.refs_31_.refs_32_), channel_id=1, source_target_pairs={{0,30},{1,31},{2,0},{3,1},{4,2},{5,3},{6,4},{7,5},{8,6},{9,7},{10,... | collective-permute-start | bytes 1105928 | tf_op jit(solution)/shard_map/ppermute | solution.py:693
  229.1 5.0 collective-permute-start.38
  235.2 7.9 %collective-permute-done.46.refs_37_.refs_38_ = bf16[1440,128]{1,0:T(8,128)(2,1)S(1)} collective-permute-done((bf16[1440,128]{1,0:T(8,128)(2,1)S(1)}, bf16[1440,128]{1,0:T(8,128)(2,1)S(1)}, u32[]{:S(2)}, u32[]{:S(2)}) %collective-permute-start.46) | collective-permute-done | bytes 368672 | tf_op jit(solution)/shard_map/ppermute | solution.py:693
  251.0 5.1 collective-permute-done.22
  258.9 5.1 collective-permute-done.82.refs_8_.refs_10_
  274.8 5.1 collective-permute-done.55.refs_10_.refs_12_
  282.6 7.9 %collective-permute-done.47.refs_14_.refs_16_ = bf16[1440,128]{1,0:T(8,128)(2,1)S(1)} collective-permute-done((bf16[1440,128]{1,0:T(8,128)(2,1)S(1)}, bf16[1440,128]{1,0:T(8,128)(2,1)S(1)}, u32[]{:S(2)}, u32[]{:S(2)}) %collective-permute-start.47) | collective-permute-done | bytes 368672 | tf_op jit(solution)/shard_map/ppermute | solution.py:693
  298.4 5.1 collective-permute-done.23
  314.2 5.0 collective-permute-done.56.refs_3_.refs_5_
  322.1 7.9 %collective-permute-done.48.refs_21_.refs_23_ = bf16[1440,128]{1,0:T(8,128)(2,1)S(1)} collective-permute-done((bf16[1440,128]{1,0:T(8,128)(2,1)S(1)}, bf16[1440,128]{1,0:T(8,128)(2,1)S(1)}, u32[]{:S(2)}, u32[]{:S(2)}) %collective-permute-start.48) | collective-permute-done | bytes 368672 | tf_op jit(solution)/shard_map/ppermute | solution.py:693
  337.9 5.1 collective-permute-done.24.refs_6_.refs_8_
  345.8 5.0 collective-permute-done.9.refs_13_.refs_18_
  353.7 5.0 collective-permute-done.57.refs_12_.refs_17_
  362.4 4.3 select.19
  450.2 4.1 collective-permute-done.96.refs_24_.refs_26_
  461.3 8.7 %collective-permute-done.111.refs_14_ = bf16[1440,128]{1,0:T(8,128)(2,1)} collective-permute-done((bf16[1440,128]{1,0:T(8,128)(2,1)}, bf16[1440,128]{1,0:T(8,128)(2,1)}, u32[]{:S(2)}, u32[]{:S(2)}) %collective-permute-start.111) | collective-permute-done | bytes 368672 | tf_op jit(solution)/shard_map/ppermute | solution.py:693
  473.6 7.4 %collective-permute-done.112.refs_15_ = bf16[1440,128]{1,0:T(8,128)(2,1)S(1)} collective-permute-done((bf16[1440,128]{1,0:T(8,128)(2,1)}, bf16[1440,128]{1,0:T(8,128)(2,1)S(1)}, u32[]{:S(2)}, u32[]{:S(2)}) %collective-permute-start.112) | collective-permute-done | bytes 368672 | tf_op jit(solution)/shard_map/ppermute | solution.py:693
  485.1 6.6 %collective-permute-done.113.refs_21_ = bf16[1440,128]{1,0:T(8,128)(2,1)} collective-permute-done((bf16[1440,128]{1,0:T(8,128)(2,1)}, bf16[1440,128]{1,0:T(8,128)(2,1)}, u32[]{:S(2)}, u32[]{:S(2)}) %collective-permute-start.113) | collective-permute-done | bytes 368672 | tf_op jit(solution)/shard_map/ppermute | solution.py:693
  498.9 7.9 %density.1.refs_3_ = bf16[960,960]{1,0:T(8,128)(2,1)} custom-call(bf16[900,900]{1,0:T(8,128)(2,1)} %rdm.1), custom_call_target="tpu_custom_call" | custom-call | tf_op jit(solution)/shard_map/density/pallas_call | solution.py:521
  506.9 17.7 %early.6.refs_2_ = f32[12,1440,128]{2,1,0:T(8,128)} custom-call(s32[96]{0:T(128)S(1)} %plan.1.table.refs_0_, bf16[2,7,1440,128]{3,2,1,0:T(8,128)(2,1)} %collective-permute-done.110.refs_1_, bf16[1440,128]{1,0:T(8,128)(2,1)} %copy-done.46, bf16[1440,128]{1,0:T(8,128)(2,1)} %copy-done.44, bf16[1440,128]{1,0:T(8,128)(2,1)} %copy-done.43, ...), custom_call_target="tpu_custom_call" | custom-call | tf_op jit(solution)/shard_map/early/pallas_call | solution.py:586
  524.8 13.8 %early.7.refs_2_ = f32[12,1440,128]{2,1,0:T(8,128)} custom-call(s32[96]{0:T(128)S(1)} %plan.1.table.refs_0_, bf16[2,4,1440,128]{3,2,1,0:T(8,128)(2,1)S(1)} %collective-permute-done.97.refs_1_, f32[12,1440,128]{2,1,0:T(8,128)} %early.6.refs_2_, bf16[1440,128]{1,0:T(8,128)(2,1)} %collective-permute-done.83.refs_1_.refs_3_, ...), custom_call_target="tpu_custom_call" | custom-call | tf_op jit(solution)/shard_map/early/pallas_call | solution.py:586
  538.8 24.8 %finish.3 = f32[6,384]{1,0:T(8,128)S(1)} custom-call(s32[96]{0:T(128)S(1)} %plan.1.table.refs_0_, bf16[2,5,1440,128]{3,2,1,0:T(8,128)(2,1)} %collective-permute-done.78.refs_1_, f32[12,1440,128]{2,1,0:T(8,128)} %early.7.refs_2_, bf16[960,960]{1,0:T(8,128)(2,1)S(1)} %copy-done.2, bf16[1440,128]{1,0:T(8,128)(2,1)} %copy-done.143, ...), custom_call_target="tpu_custom_call" | custom-call | tf_op jit(solution)/shard_map/finish/pallas_call | solution.py:603
  565.7 30.9 %all_gather.11 = f32[16,2,6,384]{3,1,2,0:T(2,128)S(1)} all-gather(f32[1,2,6,384]{3,1,2,0:T(2,128)S(1)} %copy.34), channel_id=1, replica_groups={{0,2,4,6,8,10,12,14,16,18,20,22,24,26,28,30},{1,3,5,7,9,11,13,15,17,19,..., dimensions={0}, use_global_device_ids=true | all-gather | bytes 313344 | tf_op jit(solution)/shard_map/all_gather | solution.py:664
  596.7 14.8 %conditional.1 = (f32[1]{0:T(128)}, f32[48,48]{1,0:T(8,128)S(1)}) conditional(s32[]{:T(128)} %bitcast.33, (bf16[125,23040]{1,0:T(8,128)(2,1)}, s32[32,2]{0,1:T(2,128)S(1)}, bf16[900,900]{1,0:T(8,128)(2,1)}, f32[768]{0:T(1024)S(1)}) %tuple.141, (f32[16,2,6,384]{3,1,2,0:T(2,128)S(1)}, s32[32]{0:T(128)S(1)}, f32[768]{0:T(1024)S(1)}, ...), branch_computations={%region_0.5_spmd, %region_4.8_spmd, %region_7.11_spmd} | conditional | flops 20341391360 | bytes 239225824 | solution.py:723
  (453 shorter events, 231.7 us)
Async XLA Ops:
  32.7 21.3 %collective-permute-start.84 = (bf16[1440,128]{1,0:T(8,128)(2,1)S(1)}, bf16[1440,128]{1,0:T(8,128)(2,1)S(1)}, u32[]{:S(2)}, u32[]{:S(2)}) collective-permute-start(bf16[1440,128]{1,0:T(8,128)(2,1)S(1)} %get-tuple-element.365.refs_23_.refs_24_), channel_id=1, source_target_pairs={{0,2},{1,3},{2,4},{3,5},{4,6},{5,7},{6,8},{7,9},{8,10},{9,11},{10,... | collective-permute-start | bytes 1105928 | tf_op jit(solution)/shard_map/ppermute | solution.py:692
  34.8 25.6 %collective-permute-start.88 = (bf16[1440,128]{1,0:T(8,128)(2,1)S(1)}, bf16[1440,128]{1,0:T(8,128)(2,1)S(1)}, u32[]{:S(2)}, u32[]{:S(2)}) collective-permute-start(bf16[1440,128]{1,0:T(8,128)(2,1)S(1)} %get-tuple-element.366.refs_19_.refs_20_), channel_id=1, source_target_pairs={{0,30},{1,31},{2,0},{3,1},{4,2},{5,3},{6,4},{7,5},{8,6},{9,7},{10,... | collective-permute-start | bytes 1105928 | tf_op jit(solution)/shard_map/ppermute | solution.py:693
  39.2 23.2 %collective-permute-start.98 = (bf16[1440,128]{1,0:T(8,128)(2,1)S(1)}, bf16[1440,128]{1,0:T(8,128)(2,1)S(1)}, u32[]{:S(2)}, u32[]{:S(2)}) collective-permute-start(bf16[1440,128]{1,0:T(8,128)(2,1)S(1)} %get-tuple-element.368.refs_22_.refs_23_), channel_id=1, source_target_pairs={{0,2},{1,3},{2,4},{3,5},{4,6},{5,7},{6,8},{7,9},{8,10},{9,11},{10,... | collective-permute-start | bytes 1105928 | tf_op jit(solution)/shard_map/ppermute | solution.py:692
  39.2 26.1 %collective-permute-start.59 = (bf16[1440,128]{1,0:T(8,128)(2,1)S(1)}, bf16[1440,128]{1,0:T(8,128)(2,1)S(1)}, u32[]{:S(2)}, u32[]{:S(2)}) collective-permute-start(bf16[1440,128]{1,0:T(8,128)(2,1)S(1)} %get-tuple-element.361), channel_id=1, source_target_pairs={{0,2},{1,3},{2,4},{3,5},{4,6},{5,7},{6,8},{7,9},{8,10},{9,11},{10,... | collective-permute-start | bytes 1105928 | tf_op jit(solution)/shard_map/ppermute | solution.py:692
  46.1 21.8 %collective-permute-start.71 = (bf16[1440,128]{1,0:T(8,128)(2,1)S(1)}, bf16[1440,128]{1,0:T(8,128)(2,1)S(1)}, u32[]{:S(2)}, u32[]{:S(2)}) collective-permute-start(bf16[1440,128]{1,0:T(8,128)(2,1)S(1)} %get-tuple-element.363), channel_id=1, source_target_pairs={{0,30},{1,31},{2,0},{3,1},{4,2},{5,3},{6,4},{7,5},{8,6},{9,7},{10,... | collective-permute-start | bytes 1105928 | tf_op jit(solution)/shard_map/ppermute | solution.py:693
  54.0 22.3 %collective-permute-start.92 = (bf16[1440,128]{1,0:T(8,128)(2,1)S(1)}, bf16[1440,128]{1,0:T(8,128)(2,1)S(1)}, u32[]{:S(2)}, u32[]{:S(2)}) collective-permute-start(bf16[1440,128]{1,0:T(8,128)(2,1)S(1)} %get-tuple-element.367), channel_id=1, source_target_pairs={{0,30},{1,31},{2,0},{3,1},{4,2},{5,3},{6,4},{7,5},{8,6},{9,7},{10,... | collective-permute-start | bytes 1105928 | tf_op jit(solution)/shard_map/ppermute | solution.py:693
  79.4 21.6 %collective-permute-start.44 = (bf16[1440,128]{1,0:T(8,128)(2,1)S(1)}, bf16[1440,128]{1,0:T(8,128)(2,1)S(1)}, u32[]{:S(2)}, u32[]{:S(2)}) collective-permute-start(bf16[1440,128]{1,0:T(8,128)(2,1)S(1)} %get-tuple-element.359), channel_id=1, source_target_pairs={{0,30},{1,31},{2,0},{3,1},{4,2},{5,3},{6,4},{7,5},{8,6},{9,7},{10,... | collective-permute-start | bytes 1105928 | tf_op jit(solution)/shard_map/ppermute | solution.py:693
  85.6 23.4 %collective-permute-start.106 = (bf16[1440,128]{1,0:T(8,128)(2,1)S(1)}, bf16[1440,128]{1,0:T(8,128)(2,1)S(1)}, u32[]{:S(2)}, u32[]{:S(2)}) collective-permute-start(bf16[1440,128]{1,0:T(8,128)(2,1)S(1)} %get-tuple-element.373), channel_id=1, source_target_pairs={{0,30},{1,31},{2,0},{3,1},{4,2},{5,3},{6,4},{7,5},{8,6},{9,7},{10,... | collective-permute-start | bytes 1105928 | tf_op jit(solution)/shard_map/ppermute | solution.py:693
  93.2 23.7 %collective-permute-start.36 = (bf16[1440,128]{1,0:T(8,128)(2,1)S(1)}, bf16[1440,128]{1,0:T(8,128)(2,1)S(1)}, u32[]{:S(2)}, u32[]{:S(2)}) collective-permute-start(bf16[1440,128]{1,0:T(8,128)(2,1)S(1)} %get-tuple-element.358), channel_id=1, source_target_pairs={{0,30},{1,31},{2,0},{3,1},{4,2},{5,3},{6,4},{7,5},{8,6},{9,7},{10,... | collective-permute-start | bytes 1105928 | tf_op jit(solution)/shard_map/ppermute | solution.py:693
  101.4 23.4 %collective-permute-start.28 = (bf16[1440,128]{1,0:T(8,128)(2,1)S(1)}, bf16[1440,128]{1,0:T(8,128)(2,1)S(1)}, u32[]{:S(2)}, u32[]{:S(2)}) collective-permute-start(bf16[1440,128]{1,0:T(8,128)(2,1)S(1)} %get-tuple-element.357), channel_id=1, source_target_pairs={{0,30},{1,31},{2,0},{3,1},{4,2},{5,3},{6,4},{7,5},{8,6},{9,7},{10,... | collective-permute-start | bytes 1105928 | tf_op jit(solution)/shard_map/ppermute | solution.py:693
  109.3 23.7 %collective-permute-start.85 = (bf16[1440,128]{1,0:T(8,128)(2,1)S(1)}, bf16[1440,128]{1,0:T(8,128)(2,1)S(1)}, u32[]{:S(2)}, u32[]{:S(2)}) collective-permute-start(bf16[1440,128]{1,0:T(8,128)(2,1)S(1)} %collective-permute-done.84.refs_16_.refs_17_), channel_id=1, source_target_pairs={{0,2},{1,3},{2,4},{3,5},{4,6},{5,7},{6,8},{7,9},{8,10},{9,11},{10,... | collective-permute-start | bytes 1105928 | tf_op jit(solution)/shard_map/ppermute | solution.py:692
  116.9 22.5 %collective-permute-start.89 = (bf16[1440,128]{1,0:T(8,128)(2,1)S(1)}, bf16[1440,128]{1,0:T(8,128)(2,1)S(1)}, u32[]{:S(2)}, u32[]{:S(2)}) collective-permute-start(bf16[1440,128]{1,0:T(8,128)(2,1)S(1)} %collective-permute-done.88.refs_26_.refs_27_), channel_id=1, source_target_pairs={{0,30},{1,31},{2,0},{3,1},{4,2},{5,3},{6,4},{7,5},{8,6},{9,7},{10,... | collective-permute-start | bytes 1105928 | tf_op jit(solution)/shard_map/ppermute | solution.py:693
  120.0 21.5 %collective-permute-start.99 = (bf16[1440,128]{1,0:T(8,128)(2,1)S(1)}, bf16[1440,128]{1,0:T(8,128)(2,1)S(1)}, u32[]{:S(2)}, u32[]{:S(2)}) collective-permute-start(bf16[1440,128]{1,0:T(8,128)(2,1)S(1)} %collective-permute-done.98.refs_15_.refs_16_), channel_id=1, source_target_pairs={{0,2},{1,3},{2,4},{3,5},{4,6},{5,7},{6,8},{7,9},{8,10},{9,11},{10,... | collective-permute-start | bytes 1105928 | tf_op jit(solution)/shard_map/ppermute | solution.py:692
  124.8 21.9 %collective-permute-start.60 = (bf16[1440,128]{1,0:T(8,128)(2,1)S(1)}, bf16[1440,128]{1,0:T(8,128)(2,1)S(1)}, u32[]{:S(2)}, u32[]{:S(2)}) collective-permute-start(bf16[1440,128]{1,0:T(8,128)(2,1)S(1)} %collective-permute-done.59.refs_18_.refs_19_), channel_id=1, source_target_pairs={{0,2},{1,3},{2,4},{3,5},{4,6},{5,7},{6,8},{7,9},{8,10},{9,11},{10,... | collective-permute-start | bytes 1105928 | tf_op jit(solution)/shard_map/ppermute | solution.py:692
  125.1 21.8 %collective-permute-start.72 = (bf16[1440,128]{1,0:T(8,128)(2,1)S(1)}, bf16[1440,128]{1,0:T(8,128)(2,1)S(1)}, u32[]{:S(2)}, u32[]{:S(2)}) collective-permute-start(bf16[1440,128]{1,0:T(8,128)(2,1)S(1)} %collective-permute-done.71.refs_25_.refs_26_), channel_id=1, source_target_pairs={{0,30},{1,31},{2,0},{3,1},{4,2},{5,3},{6,4},{7,5},{8,6},{9,7},{10,... | collective-permute-start | bytes 1105928 | tf_op jit(solution)/shard_map/ppermute | solution.py:693
  133.0 22.3 %collective-permute-start.93 = (bf16[1440,128]{1,0:T(8,128)(2,1)S(1)}, bf16[1440,128]{1,0:T(8,128)(2,1)S(1)}, u32[]{:S(2)}, u32[]{:S(2)}) collective-permute-start(bf16[1440,128]{1,0:T(8,128)(2,1)S(1)} %collective-permute-done.92.refs_27_.refs_28_), channel_id=1, source_target_pairs={{0,30},{1,31},{2,0},{3,1},{4,2},{5,3},{6,4},{7,5},{8,6},{9,7},{10,... | collective-permute-start | bytes 1105928 | tf_op jit(solution)/shard_map/ppermute | solution.py:693
  158.6 21.5 %collective-permute-start.45 = (bf16[1440,128]{1,0:T(8,128)(2,1)S(1)}, bf16[1440,128]{1,0:T(8,128)(2,1)S(1)}, u32[]{:S(2)}, u32[]{:S(2)}) collective-permute-start(bf16[1440,128]{1,0:T(8,128)(2,1)S(1)} %collective-permute-done.44), channel_id=1, source_target_pairs={{0,30},{1,31},{2,0},{3,1},{4,2},{5,3},{6,4},{7,5},{8,6},{9,7},{10,... | collective-permute-start | bytes 1105928 | tf_op jit(solution)/shard_map/ppermute | solution.py:693
  159.5 23.8 %collective-permute-start.5 = (bf16[1440,128]{1,0:T(8,128)(2,1)S(1)}, bf16[1440,128]{1,0:T(8,128)(2,1)S(1)}, u32[]{:S(2)}, u32[]{:S(2)}) collective-permute-start(bf16[1440,128]{1,0:T(8,128)(2,1)S(1)} %collective-permute-done.4), channel_id=1, source_target_pairs={{0,2},{1,3},{2,4},{3,5},{4,6},{5,7},{6,8},{7,9},{8,10},{9,11},{10,... | collective-permute-start | bytes 1105928 | tf_op jit(solution)/shard_map/ppermute | solution.py:692
  162.5 20.8 %collective-permute-start.13 = (bf16[1440,128]{1,0:T(8,128)(2,1)S(1)}, bf16[1440,128]{1,0:T(8,128)(2,1)S(1)}, u32[]{:S(2)}, u32[]{:S(2)}) collective-permute-start(bf16[1440,128]{1,0:T(8,128)(2,1)S(1)} %collective-permute-done.12), channel_id=1, source_target_pairs={{0,2},{1,3},{2,4},{3,5},{4,6},{5,7},{6,8},{7,9},{8,10},{9,11},{10,... | collective-permute-start | bytes 1105928 | tf_op jit(solution)/shard_map/ppermute | solution.py:692
  164.3 23.7 %collective-permute-start.37 = (bf16[1440,128]{1,0:T(8,128)(2,1)S(1)}, bf16[1440,128]{1,0:T(8,128)(2,1)S(1)}, u32[]{:S(2)}, u32[]{:S(2)}) collective-permute-start(bf16[1440,128]{1,0:T(8,128)(2,1)S(1)} %collective-permute-done.36), channel_id=1, source_target_pairs={{0,30},{1,31},{2,0},{3,1},{4,2},{5,3},{6,4},{7,5},{8,6},{9,7},{10,... | collective-permute-start | bytes 1105928 | tf_op jit(solution)/shard_map/ppermute | solution.py:693
  183.3 21.0 %collective-permute-start.86 = (bf16[1440,128]{1,0:T(8,128)(2,1)S(1)}, bf16[1440,128]{1,0:T(8,128)(2,1)S(1)}, u32[]{:S(2)}, u32[]{:S(2)}) collective-permute-start(bf16[1440,128]{1,0:T(8,128)(2,1)S(1)} %collective-permute-done.85.refs_9_.refs_10_), channel_id=1, source_target_pairs={{0,2},{1,3},{2,4},{3,5},{4,6},{5,7},{6,8},{7,9},{8,10},{9,11},{10,... | collective-permute-start | bytes 1105928 | tf_op jit(solution)/shard_map/ppermute | solution.py:692
  188.0 22.5 %collective-permute-start.90 = (bf16[1440,128]{1,0:T(8,128)(2,1)S(1)}, bf16[1440,128]{1,0:T(8,128)(2,1)S(1)}, u32[]{:S(2)}, u32[]{:S(2)}) collective-permute-start(bf16[1440,128]{1,0:T(8,128)(2,1)S(1)} %collective-permute-done.89.refs_33_.refs_34_), channel_id=1, source_target_pairs={{0,30},{1,31},{2,0},{3,1},{4,2},{5,3},{6,4},{7,5},{8,6},{9,7},{10,... | collective-permute-start | bytes 1105928 | tf_op jit(solution)/shard_map/ppermute | solution.py:693
  191.2 21.4 %collective-permute-start.100 = (bf16[1440,128]{1,0:T(8,128)(2,1)S(1)}, bf16[1440,128]{1,0:T(8,128)(2,1)S(1)}, u32[]{:S(2)}, u32[]{:S(2)}) collective-permute-start(bf16[1440,128]{1,0:T(8,128)(2,1)S(1)} %collective-permute-done.99.refs_8_.refs_9_), channel_id=1, source_target_pairs={{0,2},{1,3},{2,4},{3,5},{4,6},{5,7},{6,8},{7,9},{8,10},{9,11},{10,... | collective-permute-start | bytes 1105928 | tf_op jit(solution)/shard_map/ppermute | solution.py:692
  195.9 21.9 %collective-permute-start.61 = (bf16[1440,128]{1,0:T(8,128)(2,1)S(1)}, bf16[1440,128]{1,0:T(8,128)(2,1)S(1)}, u32[]{:S(2)}, u32[]{:S(2)}) collective-permute-start(bf16[1440,128]{1,0:T(8,128)(2,1)S(1)} %collective-permute-done.60.refs_11_.refs_12_), channel_id=1, source_target_pairs={{0,2},{1,3},{2,4},{3,5},{4,6},{5,7},{6,8},{7,9},{8,10},{9,11},{10,... | collective-permute-start | bytes 1105928 | tf_op jit(solution)/shard_map/ppermute | solution.py:692
  196.4 29.8 %collective-permute-start.73 = (bf16[1440,128]{1,0:T(8,128)(2,1)S(1)}, bf16[1440,128]{1,0:T(8,128)(2,1)S(1)}, u32[]{:S(2)}, u32[]{:S(2)}) collective-permute-start(bf16[1440,128]{1,0:T(8,128)(2,1)S(1)} %collective-permute-done.72.refs_32_.refs_33_), channel_id=1, source_target_pairs={{0,30},{1,31},{2,0},{3,1},{4,2},{5,3},{6,4},{7,5},{8,6},{9,7},{10,... | collective-permute-start | bytes 1105928 | tf_op jit(solution)/shard_map/ppermute | solution.py:693
  204.3 24.5 %collective-permute-start.94 = (bf16[1440,128]{1,0:T(8,128)(2,1)S(1)}, bf16[1440,128]{1,0:T(8,128)(2,1)S(1)}, u32[]{:S(2)}, u32[]{:S(2)}) collective-permute-start(bf16[1440,128]{1,0:T(8,128)(2,1)S(1)} %collective-permute-done.93.refs_34_.refs_35_), channel_id=1, source_target_pairs={{0,30},{1,31},{2,0},{3,1},{4,2},{5,3},{6,4},{7,5},{8,6},{9,7},{10,... | collective-permute-start | bytes 1105928 | tf_op jit(solution)/shard_map/ppermute | solution.py:693
  229.1 21.9 %collective-permute-start.38 = (bf16[1440,128]{1,0:T(8,128)(2,1)S(1)}, bf16[1440,128]{1,0:T(8,128)(2,1)S(1)}, u32[]{:S(2)}, u32[]{:S(2)}) collective-permute-start(bf16[1440,128]{1,0:T(8,128)(2,1)S(1)} %collective-permute-done.37), channel_id=1, source_target_pairs={{0,30},{1,31},{2,0},{3,1},{4,2},{5,3},{6,4},{7,5},{8,6},{9,7},{10,... | collective-permute-start | bytes 1105928 | tf_op jit(solution)/shard_map/ppermute | solution.py:693
  235.2 20.9 %collective-permute-start.22 = (bf16[1440,128]{1,0:T(8,128)(2,1)S(1)}, bf16[1440,128]{1,0:T(8,128)(2,1)S(1)}, u32[]{:S(2)}, u32[]{:S(2)}) collective-permute-start(bf16[1440,128]{1,0:T(8,128)(2,1)S(1)} %collective-permute-done.21), channel_id=1, source_target_pairs={{0,2},{1,3},{2,4},{3,5},{4,6},{5,7},{6,8},{7,9},{8,10},{9,11},{10,... | collective-permute-start | bytes 1105928 | tf_op jit(solution)/shard_map/ppermute | solution.py:692
  251.0 20.9 %collective-permute-start.62 = (bf16[1440,128]{1,0:T(8,128)(2,1)S(1)}, bf16[1440,128]{1,0:T(8,128)(2,1)S(1)}, u32[]{:S(2)}, u32[]{:S(2)}) collective-permute-start(bf16[1440,128]{1,0:T(8,128)(2,1)S(1)} %collective-permute-done.61.refs_4_.refs_5_), channel_id=1, source_target_pairs={{0,2},{1,3},{2,4},{3,5},{4,6},{5,7},{6,8},{7,9},{8,10},{9,11},{10,... | collective-permute-start | bytes 1105928 | tf_op jit(solution)/shard_map/ppermute | solution.py:692
  258.9 20.9 %collective-permute-start.55 = (bf16[1440,128]{1,0:T(8,128)(2,1)S(1)}, bf16[1440,128]{1,0:T(8,128)(2,1)S(1)}, u32[]{:S(2)}, u32[]{:S(2)}) collective-permute-start(bf16[1440,128]{1,0:T(8,128)(2,1)S(1)} %collective-permute-done.54.refs_5_.refs_6_), channel_id=1, source_target_pairs={{0,2},{1,3},{2,4},{3,5},{4,6},{5,7},{6,8},{7,9},{8,10},{9,11},{10,... | collective-permute-start | bytes 1105928 | tf_op jit(solution)/shard_map/ppermute | solution.py:692
  266.8 23.7 %collective-permute-start.47 = (bf16[1440,128]{1,0:T(8,128)(2,1)S(1)}, bf16[1440,128]{1,0:T(8,128)(2,1)S(1)}, u32[]{:S(2)}, u32[]{:S(2)}) collective-permute-start(bf16[1440,128]{1,0:T(8,128)(2,1)S(1)} %collective-permute-done.46.refs_37_.refs_38_), channel_id=1, source_target_pairs={{0,30},{1,31},{2,0},{3,1},{4,2},{5,3},{6,4},{7,5},{8,6},{9,7},{10,... | collective-permute-start | bytes 1105928 | tf_op jit(solution)/shard_map/ppermute | solution.py:693
  271.9 21.1 %collective-permute-start.7 = (bf16[1440,128]{1,0:T(8,128)(2,1)S(1)}, bf16[1440,128]{1,0:T(8,128)(2,1)S(1)}, u32[]{:S(2)}, u32[]{:S(2)}) collective-permute-start(bf16[1440,128]{1,0:T(8,128)(2,1)S(1)} %collective-permute-done.6.refs_6_.refs_7_), channel_id=1, source_target_pairs={{0,2},{1,3},{2,4},{3,5},{4,6},{5,7},{6,8},{7,9},{8,10},{9,11},{10,... | collective-permute-start | bytes 1105928 | tf_op jit(solution)/shard_map/ppermute | solution.py:692
  274.7 20.9 %collective-permute-start.15 = (bf16[1440,128]{1,0:T(8,128)(2,1)S(1)}, bf16[1440,128]{1,0:T(8,128)(2,1)S(1)}, u32[]{:S(2)}, u32[]{:S(2)}) collective-permute-start(bf16[1440,128]{1,0:T(8,128)(2,1)S(1)} %collective-permute-done.14), channel_id=1, source_target_pairs={{0,2},{1,3},{2,4},{3,5},{4,6},{5,7},{6,8},{7,9},{8,10},{9,11},{10,... | collective-permute-start | bytes 1105928 | tf_op jit(solution)/shard_map/ppermute | solution.py:692
  282.6 20.9 %collective-permute-start.23 = (bf16[1440,128]{1,0:T(8,128)(2,1)S(1)}, bf16[1440,128]{1,0:T(8,128)(2,1)S(1)}, u32[]{:S(2)}, u32[]{:S(2)}) collective-permute-start(bf16[1440,128]{1,0:T(8,128)(2,1)S(1)} %collective-permute-done.22), channel_id=1, source_target_pairs={{0,2},{1,3},{2,4},{3,5},{4,6},{5,7},{6,8},{7,9},{8,10},{9,11},{10,... | collective-permute-start | bytes 1105928 | tf_op jit(solution)/shard_map/ppermute | solution.py:692
  298.4 20.8 %collective-permute-start.56 = (bf16[1440,128]{1,0:T(8,128)(2,1)S(1)}, bf16[1440,128]{1,0:T(8,128)(2,1)S(1)}, u32[]{:S(2)}, u32[]{:S(2)}) collective-permute-start(bf16[1440,128]{1,0:T(8,128)(2,1)S(1)} %collective-permute-done.55.refs_10_.refs_12_), channel_id=1, source_target_pairs={{0,2},{1,3},{2,4},{3,5},{4,6},{5,7},{6,8},{7,9},{8,10},{9,11},{10,... | collective-permute-start | bytes 1105928 | tf_op jit(solution)/shard_map/ppermute | solution.py:692
  306.3 23.7 %collective-permute-start.48 = (bf16[1440,128]{1,0:T(8,128)(2,1)S(1)}, bf16[1440,128]{1,0:T(8,128)(2,1)S(1)}, u32[]{:S(2)}, u32[]{:S(2)}) collective-permute-start(bf16[1440,128]{1,0:T(8,128)(2,1)S(1)} %collective-permute-done.47.refs_14_.refs_16_), channel_id=1, source_target_pairs={{0,30},{1,31},{2,0},{3,1},{4,2},{5,3},{6,4},{7,5},{8,6},{9,7},{10,... | collective-permute-start | bytes 1105928 | tf_op jit(solution)/shard_map/ppermute | solution.py:693
  311.6 21.0 %collective-permute-start.8 = (bf16[1440,128]{1,0:T(8,128)(2,1)S(1)}, bf16[1440,128]{1,0:T(8,128)(2,1)S(1)}, u32[]{:S(2)}, u32[]{:S(2)}) collective-permute-start(bf16[1440,128]{1,0:T(8,128)(2,1)S(1)} %collective-permute-done.7.refs_11_.refs_13_), channel_id=1, source_target_pairs={{0,2},{1,3},{2,4},{3,5},{4,6},{5,7},{6,8},{7,9},{8,10},{9,11},{10,... | collective-permute-start | bytes 1105928 | tf_op jit(solution)/shard_map/ppermute | solution.py:692
  314.2 20.9 %collective-permute-start.16 = (bf16[1440,128]{1,0:T(8,128)(2,1)S(1)}, bf16[1440,128]{1,0:T(8,128)(2,1)}, u32[]{:S(2)}, u32[]{:S(2)}) collective-permute-start(bf16[1440,128]{1,0:T(8,128)(2,1)S(1)} %collective-permute-done.15.refs_12_.refs_14_), channel_id=1, source_target_pairs={{0,2},{1,3},{2,4},{3,5},{4,6},{5,7},{6,8},{7,9},{8,10},{9,11},{10,... | collective-permute-start | bytes 1105928 | tf_op jit(solution)/shard_map/ppermute | solution.py:692
  322.1 20.9 %collective-permute-start.24 = (bf16[1440,128]{1,0:T(8,128)(2,1)S(1)}, bf16[1440,128]{1,0:T(8,128)(2,1)}, u32[]{:S(2)}, u32[]{:S(2)}) collective-permute-start(bf16[1440,128]{1,0:T(8,128)(2,1)S(1)} %collective-permute-done.23), channel_id=1, source_target_pairs={{0,2},{1,3},{2,4},{3,5},{4,6},{5,7},{6,8},{7,9},{8,10},{9,11},{10,... | collective-permute-start | bytes 1105928 | tf_op jit(solution)/shard_map/ppermute | solution.py:692
  345.8 21.0 %collective-permute-start.64 = (bf16[1440,128]{1,0:T(8,128)(2,1)}, bf16[1440,128]{1,0:T(8,128)(2,1)}, u32[]{:S(2)}, u32[]{:S(2)}) collective-permute-start(bf16[1440,128]{1,0:T(8,128)(2,1)} %collective-permute-done.63.refs_2_.refs_4_), channel_id=1, source_target_pairs={{0,2},{1,3},{2,4},{3,5},{4,6},{5,7},{6,8},{7,9},{8,10},{9,11},{10,... | collective-permute-start | bytes 1105928 | tf_op jit(solution)/shard_map/ppermute | solution.py:692
  353.7 20.9 %collective-permute-start.17 = (bf16[1440,128]{1,0:T(8,128)(2,1)}, bf16[1440,128]{1,0:T(8,128)(2,1)}, u32[]{:S(2)}, u32[]{:S(2)}) collective-permute-start(bf16[1440,128]{1,0:T(8,128)(2,1)} %collective-permute-done.16.refs_5_.refs_7_), channel_id=1, source_target_pairs={{0,2},{1,3},{2,4},{3,5},{4,6},{5,7},{6,8},{7,9},{8,10},{9,11},{10,... | collective-permute-start | bytes 1105928 | tf_op jit(solution)/shard_map/ppermute | solution.py:692
  366.9 131.8 %collective-permute-start.110 = (bf16[2,7,1440,128]{3,2,1,0:T(8,128)(2,1)}, bf16[2,7,1440,128]{3,2,1,0:T(8,128)(2,1)}, u32[]{:S(2)}, u32[]{:S(2)}) collective-permute-start(bf16[2,7,1440,128]{3,2,1,0:T(8,128)(2,1)} %select.19), channel_id=1, source_target_pairs={{0,1},{1,0},{2,3},{3,2},{4,5},{5,4},{6,7},{7,6},{8,9},{9,8},{10,11... | collective-permute-start | bytes 15482888 | tf_op jit(solution)/shard_map/ppermute | solution.py:628
  447.1 91.6 %collective-permute-start.78 = (bf16[2,5,1440,128]{3,2,1,0:T(8,128)(2,1)}, bf16[2,5,1440,128]{3,2,1,0:T(8,128)(2,1)}, u32[]{:S(2)}, u32[]{:S(2)}) collective-permute-start(bf16[2,5,1440,128]{3,2,1,0:T(8,128)(2,1)} %select.17), channel_id=1, source_target_pairs={{0,1},{1,0},{2,3},{3,2},{4,5},{5,4},{6,7},{7,6},{8,9},{9,8},{10,11... | collective-permute-start | bytes 11059208 | tf_op jit(solution)/shard_map/ppermute | solution.py:628
  457.6 40.8 %collective-permute-start.97 = (bf16[2,4,1440,128]{3,2,1,0:T(8,128)(2,1)}, bf16[2,4,1440,128]{3,2,1,0:T(8,128)(2,1)S(1)}, u32[]{:S(2)}, u32[]{:S(2)}) collective-permute-start(bf16[2,4,1440,128]{3,2,1,0:T(8,128)(2,1)} %select.18), channel_id=1, source_target_pairs={{0,1},{1,0},{2,3},{3,2},{4,5},{5,4},{6,7},{7,6},{8,9},{9,8},{10,11... | collective-permute-start | bytes 8847368 | tf_op jit(solution)/shard_map/ppermute | solution.py:628
  495.8 42.9 %collective-permute-start.117 = (bf16[1440,128]{1,0:T(8,128)(2,1)}, bf16[1440,128]{1,0:T(8,128)(2,1)}, u32[]{:S(2)}, u32[]{:S(2)}) collective-permute-start(bf16[1440,128]{1,0:T(8,128)(2,1)} %collective-permute-done.111.refs_14_), channel_id=1, source_target_pairs={{0,1},{1,0},{2,3},{3,2},{4,5},{5,4},{6,7},{7,6},{8,9},{9,8},{10,11... | collective-permute-start | bytes 1105928 | tf_op jit(solution)/shard_map/ppermute | solution.py:628
  498.2 40.5 %collective-permute-start.122 = (bf16[1440,128]{1,0:T(8,128)(2,1)}, bf16[1440,128]{1,0:T(8,128)(2,1)}, u32[]{:S(2)}, u32[]{:S(2)}) collective-permute-start(bf16[1440,128]{1,0:T(8,128)(2,1)} %collective-permute-done.114.refs_29_), channel_id=1, source_target_pairs={{0,1},{1,0},{2,3},{3,2},{4,5},{5,4},{6,7},{7,6},{8,9},{9,8},{10,11... | collective-permute-start | bytes 1105928 | tf_op jit(solution)/shard_map/ppermute | solution.py:628
  498.4 40.3 %collective-permute-start.119 = (bf16[1440,128]{1,0:T(8,128)(2,1)}, bf16[1440,128]{1,0:T(8,128)(2,1)}, u32[]{:S(2)}, u32[]{:S(2)}) collective-permute-start(bf16[1440,128]{1,0:T(8,128)(2,1)} %collective-permute-done.113.refs_21_), channel_id=1, source_target_pairs={{0,1},{1,0},{2,3},{3,2},{4,5},{5,4},{6,7},{7,6},{8,9},{9,8},{10,11... | collective-permute-start | bytes 1105928 | tf_op jit(solution)/shard_map/ppermute | solution.py:628
  498.7 39.9 %collective-permute-start.120 = (bf16[1440,128]{1,0:T(8,128)(2,1)}, bf16[1440,128]{1,0:T(8,128)(2,1)}, u32[]{:S(2)}, u32[]{:S(2)}) collective-permute-start(bf16[1440,128]{1,0:T(8,128)(2,1)} %collective-permute-done.115.refs_22_), channel_id=1, source_target_pairs={{0,1},{1,0},{2,3},{3,2},{4,5},{5,4},{6,7},{7,6},{8,9},{9,8},{10,11... | collective-permute-start | bytes 1105928 | tf_op jit(solution)/shard_map/ppermute | solution.py:628
  (187 other events, 8367.5 us)
